TPU v7x, 128 devices: a whole 4x4x4 slice. The times are simulated.
128 devices in a mesh: grp: 8 (over x, core), shard: 16 (over z, y).
Axes of the slice: x: 4, y: 4, z: 4, core: 2. Of those that a mesh axis runs over, the one named last changes fastest.
Arguments:
- activations: bfloat16 [1, 24576, 5120], P(None, ('grp', 'shard')), may hold values from -6 to 6
- out_grads: bfloat16 [1, 24576, 5120], P(None, ('grp', 'shard')), may hold values from -0.107910156 to 0.107910156
- error: float32 [8, 5120, 1, 5120], P('grp', 'shard'), may hold values from -6 to 6
- q_start: float32 [1, 32, 5120], replicated, may hold values from -6 to 6
Outputs:
- update: float32 [5120, 1, 5120], P('shard')
- error_next: float32 [8, 5120, 1, 5120], P('grp', 'shard')
- factor: float32 [1, 32, 5120], replicated
All inputs are finite; a program needn't handle non-finite values.
Results may differ from a plain program's by a relative error of at most 0.0034.
Values may be sent and summed in bfloat16 or wider, within the bound.
No kernel may reach another device: no remote copies, remote signals or barrier semaphores. Data moves between devices by JAX's collectives and lax.ppermute only.
A program may use at most 256 MiB of HBM per device.

v0:
```python
import jax
import jax.numpy as jnp
from jax import lax
from jax.sharding import Mesh
from jax.sharding import PartitionSpec as P

ITERS = 2
GRP = ("grp_0", "grp_1")
SHARD = ("shard_0", "shard_1")
GRP_SHARD = ("grp_0", "grp_1", "shard_0", "shard_1")


def from_everyone(x, axis):
    size = lax.axis_size(axis)
    return lax.all_to_all(jnp.broadcast_to(x[None], (size, *x.shape)), axis, 0, 0, tiled=True)


def over_copies(x, axis):
    return from_everyone(x, axis).sum(axis=0)


def one_axis_at_a_time(x, axes):
    for axis in axes:
        x = lax.psum(x, axis)
    return x


def padded_to(lines, size):
    spare = -len(lines) % size
    return jnp.pad(lines, [(0, spare)] + [(0, 0)] * (lines.ndim - 1))


def in_order(tiles, dim):
    tiles = jnp.moveaxis(tiles, 0, dim)
    shape = tiles.shape
    return tiles.reshape(*shape[:dim], shape[dim] * shape[dim + 1], *shape[dim + 2 :])


def gathered_by_axis(x, axes, dim):
    far, near = axes
    initial = from_everyone(x, far)
    tiles = jnp.swapaxes(from_everyone(initial, near), 0, 1)
    return in_order(tiles.reshape(-1, *x.shape), dim)


def in_blocks(x, dim, size):
    shape = x.shape
    tiles = x.reshape(*shape[:dim], size, shape[dim] // size, *shape[dim + 1 :])
    return jnp.moveaxis(tiles, dim, 0)


def summed_on_arrival(x, axis, dim):
    size = lax.axis_size(axis)
    tiles = lax.all_to_all(in_blocks(x, dim, size), axis, 0, 0, tiled=True)
    return jnp.sum(tiles, axis=0)


def sum_by_axis(x, axes, dim):
    far, near = axes
    tiles = in_blocks(x, dim, lax.axis_size(far))
    nearer = summed_on_arrival(tiles, near, dim + 1)
    arrived = lax.all_to_all(nearer, far, split_axis=0, concat_axis=0, tiled=True)
    return arrived.sum(axis=0)


def nested_sum(x, axes):
    lines = x.reshape(-1)
    padded = padded_to(lines, lax.axis_size(axes[0]) * lax.axis_size(axes[1]))
    whole = gathered_by_axis(sum_by_axis(padded, axes, 0), axes, 0)
    return lax.slice_in_dim(whole, 0, len(lines)).reshape(x.shape)


def local(activations, out_grads, error, q_start):
    own_rows = error.shape[1]
    mats = activations.shape[0]
    tok_count = activations.shape[1]
    width = activations.shape[2]
    groups = lax.axis_size(GRP)
    high = lax.Precision.HIGHEST
    input_cols = lax.all_to_all(activations, SHARD, split_axis=2, concat_axis=1, tiled=True)
    piece = lax.all_gather(out_grads, SHARD, axis=1, tiled=True)
    blocks = piece.shape[1] // tok_count
    mine = input_cols.reshape(mats, blocks, tok_count, own_rows)
    grads = piece.reshape(mats, blocks, tok_count, width)
    partial_sum = jnp.einsum("mkta,mktc->kamc", mine, grads, preferred_element_type=jnp.float32)
    rounded = lax.optimization_barrier(partial_sum.astype(jnp.bfloat16)).astype(jnp.float32)
    gradient = jnp.sum(rounded, axis=0)
    momentum = gradient + error[0]
    right = q_start
    for step in range(ITERS):
        left = jnp.einsum("rmc,mkc->rmk", momentum, right, precision=high)
        left = over_copies(left, GRP) / groups
        gram = one_axis_at_a_time(jnp.einsum("rmk,rml->mkl", left, left, precision=high), SHARD)
        lower = jnp.linalg.cholesky(gram)
        basis = jax.vmap(lambda tri, rhs: jax.scipy.linalg.solve_triangular(tri, rhs, lower=True))(
            lower, left.transpose(1, 2, 0)
        )
        right = jnp.einsum("mkr,rmc->mkc", basis, momentum, precision=high)
        right = nested_sum(right, (("grp_0", "grp_1", "shard_0"), "shard_1")) / groups
    update = jnp.einsum("mkr,mkc->rmc", basis, right, precision=high)
    return (update, (momentum - update)[None], right)


def solution(mesh):
    split = Mesh(mesh.devices.reshape(4, 2, 4, 4), ("grp_0", "grp_1", "shard_0", "shard_1"))
    return jax.shard_map(
        local,
        mesh=split,
        in_specs=(
            P(None, GRP_SHARD, None),
            P(None, GRP_SHARD, None),
            P(GRP, SHARD, None, None),
            P(),
        ),
        out_specs=(P(SHARD, None, None), P(GRP, SHARD, None, None), P()),
        check_vma=False,
    )
```

profile of v0, /device:TPU:1, one launch (start us, length us, event | category | flops | bytes accessed | tf_op | source)
XLA Modules:
  0.0 545.0 jit_solution(8008052416800188501)
XLA Ops:
  7.9 11.3 %copy.57 = bf16[1,192,5120]{1,0,2:T(2,128)(2,1)} copy(bf16[1,192,5120]{2,1,0:T(8,128)(2,1)} %param.7) | data formatting | bytes 3932160 | tf_op args[0]
  19.7 29.1 %reduce.12 = bf16[5120,192]{1,0:T(8,128)(2,1)S(1)} reduce(bf16[5120,1,192]{2,1,0:T(2,128)(2,1)} %bitcast.136, bf16[]{:T(256)} %broadcast.127), dimensions={1}, to_apply=%bitcast.124.reduce_sub_computation | reduce | bytes 3932162
  48.9 3.8 reshape.241
  52.7 46.4 %all_to_all.75 = bf16[16,2,30720]{2,1,0:T(2,128)(2,1)S(1)} all-to-all(bf16[16,2,30720]{2,1,0:T(2,128)(2,1)} %reshape.241), channel_id=1, replica_groups=mesh['grp_0'=4,'grp_1'=2,'shard_0'=4,'shard_1'=4] {'shard_0','shard_1'}, dimensions={0} | all-to-all | bytes 3932160 | tf_op jit(solution)/shard_map/all_to_all | solution.py:80
  99.1 7.8 %reshape.242 = bf16[5120,1,192]{2,1,0:T(2,128)(2,1)} reshape(bf16[16,2,30720]{2,1,0:T(2,128)(2,1)S(1)} %all_to_all.75) | data formatting | bytes 3932160
  106.8 3.0 copy.76
  112.5 100.8 %all-gather.2.cloned.1.call-done = bf16[1,3072,5120]{2,1,0:T(8,128)(2,1)} async-done(((bf16[1,192,5120]{2,1,0:T(8,128)(2,1)}), bf16[1,3072,5120]{2,1,0:T(8,128)(2,1)}) %all-gather.2.cloned.1.call-update) | async-done | bytes 31457296 | tf_op jit(solution)/shard_map/all_gather | solution.py:81
  213.2 32.9 %convert_bitcast_fusion = bf16[16,320,1,5120]{3,1,0,2:T(8,128)(2,1)} fusion(bf16[16,192,5120]{2,1,0:T(8,128)(2,1)} %bitcast.135, bf16[1,192,16,320]{3,1,2,0:T(8,128)(2,1)} %copy.59), kind=kOutput, calls=%fused_computation.1 | convolution fusion | flops 10092544000 | bytes 85852160 | tf_op jit(solution)/shard_map/mkta,mktc->kamc/dot_general | solution.py:85
  246.2 20.1 %convert_reduce_fusion = f32[320,5120]{1,0:T(8,128)} fusion(bf16[16,320,1,5120]{3,1,0,2:T(8,128)(2,1)} %convert_bitcast_fusion), kind=kLoop, calls=%fused_computation | loop fusion | flops 50790400 | bytes 58982400 | tf_op jit(solution)/shard_map/reduce_sum | solution.py:87
  266.2 8.8 %fusion.8 = f32[320,32]{0,1:T(8,128)S(1)} fusion(f32[320,5120]{1,0:T(8,128)} %convert_reduce_fusion, f32[1,320,1,5120]{3,2,1,0:T(1,128)} %param.9, f32[1,32,5120]{2,1,0:T(8,128)S(1)} %copy-done), kind=kOutput, calls=%fused_computation.13 | convolution fusion | flops 630784000 | bytes 13803520 | tf_op jit(solution)/shard_map/rmc,mkc->rmk/dot_general | solution.py:91
  275.9 4.8 all-to-all-start.1
  280.7 9.5 %bitcast_add_fusion.1 = f32[320,5120]{1,0:T(8,128)} fusion(f32[320,5120]{1,0:T(8,128)} %convert_reduce_fusion, f32[1,320,1,5120]{3,2,1,0:T(1,128)} %param.9), kind=kLoop, calls=%fused_computation.10 | loop fusion | flops 1638400 | bytes 19660800 | tf_op jit(solution)/shard_map/add | solution.py:88
  290.4 13.2 %psum.28 = f32[1,32,32]{1,2,0:T(8,128)S(1)} all-reduce(f32[1,32,32]{1,2,0:T(8,128)S(1)} %convolution_bitcast_fusion.3), channel_id=1, replica_groups=mesh['grp_0'=4,'grp_1'=2,'shard_0'=4,'shard_1'=4] {'shard_0'}, use_global_device_ids=true, to_apply=%region_2.0 | all-reduce | flops 1024 | bytes 8192 | tf_op jit(solution)/shard_map/psum | solution.py:24
  303.6 11.1 %psum.29 = f32[1,32,32]{1,2,0:T(8,128)S(1)} all-reduce(f32[1,32,32]{1,2,0:T(8,128)S(1)} %psum.28), channel_id=1, replica_groups=mesh['grp_0'=4,'grp_1'=2,'shard_0'=4,'shard_1'=4] {'shard_1'}, use_global_device_ids=true, to_apply=%region_3.0 | all-reduce | flops 1024 | bytes 8192 | tf_op jit(solution)/shard_map/psum | solution.py:24
  321.7 5.9 %fusion.12 = f32[4,32,1280]{2,1,0:T(8,128)S(1)} fusion(f32[32,320,1]{1,0,2:T(8,128)S(1)} %convolution_bitcast_fusion.1, f32[40,4,8,1280]{3,2,1,0:T(8,128)} %bitcast.133), kind=kOutput, calls=%fused_computation.18 | convolution fusion | flops 629145600 | bytes 7249920 | tf_op jit(solution)/shard_map/mkr,rmc->mkc/dot_general | solution.py:98
  327.6 10.0 %all_to_all.76 = f32[4,32,1280]{2,1,0:T(8,128)S(1)} all-to-all(f32[4,32,1280]{2,1,0:T(8,128)S(1)} %fusion.12), channel_id=1, replica_groups=mesh['grp_0'=4,'grp_1'=2,'shard_0'=4,'shard_1'=4] {'shard_1'}, dimensions={0} | all-to-all | bytes 1310720 | tf_op jit(solution)/shard_map/all_to_all | solution.py:54
  337.8 21.6 %all_to_all.77 = f32[32,1,1280]{2,1,0:T(1,128)S(1)} all-to-all(f32[32,1,1280]{2,1,0:T(1,128)S(1)} %all_to_all.54), channel_id=1, replica_groups=mesh['grp_0'=4,'grp_1'=2,'shard_0'=4,'shard_1'=4] {'grp_0','grp_1','shar..., dimensions={0} | all-to-all | bytes 327680 | tf_op jit(solution)/shard_map/all_to_all | solution.py:62
  359.6 11.7 %all_to_all.78 = f32[32,1,1280]{2,1,0:T(1,128)S(1)} all-to-all(f32[32,1,1280]{2,1,0:T(1,128)S(1)} %broadcast_in_dim.23), channel_id=1, replica_groups=mesh['grp_0'=4,'grp_1'=2,'shard_0'=4,'shard_1'=4] {'grp_0','grp_1','shar..., dimensions={0} | all-to-all | bytes 327680 | tf_op jit(solution)/shard_map/all_to_all | solution.py:15
  371.4 12.9 %all_to_all.79 = f32[4,32,1280]{2,1,0:T(8,128)S(1)} all-to-all(f32[4,32,1280]{2,1,0:T(8,128)S(1)} %broadcast_in_dim.25), channel_id=1, replica_groups=mesh['grp_0'=4,'grp_1'=2,'shard_0'=4,'shard_1'=4] {'shard_1'}, dimensions={0} | all-to-all | bytes 1310720 | tf_op jit(solution)/shard_map/all_to_all | solution.py:15
  384.4 8.9 %fusion.19 = f32[320,32]{0,1:T(8,128)S(1)} fusion(f32[32,5120]{1,0:T(8,128)S(1)} %bitcast.140, f32[1,320,1,5120]{3,2,1,0:T(1,128)} %param.9, f32[320,5120]{1,0:T(8,128)} %convert_reduce_fusion), kind=kOutput, calls=%fused_computation.21 | convolution fusion | flops 630784000 | bytes 13803520 | tf_op jit(solution)/shard_map/rmc,mkc->rmk/dot_general | solution.py:91
  393.4 11.8 %all_to_all.80 = f32[8,320,1,32]{1,3,2,0:T(8,128)S(1)} all-to-all(f32[8,320,1,32]{1,3,2,0:T(8,128)S(1)} %broadcast_in_dim.27), channel_id=1, replica_groups=mesh['grp_0'=4,'grp_1'=2,'shard_0'=4,'shard_1'=4] {'grp_0','grp_1'}, dimensions={0} | all-to-all | bytes 655360 | tf_op jit(solution)/shard_map/all_to_all | solution.py:15
  405.4 11.4 %psum.30 = f32[1,32,32]{1,2,0:T(8,128)S(1)} all-reduce(f32[1,32,32]{1,2,0:T(8,128)S(1)} %convolution_bitcast_fusion.2), channel_id=1, replica_groups=mesh['grp_0'=4,'grp_1'=2,'shard_0'=4,'shard_1'=4] {'shard_0'}, use_global_device_ids=true, to_apply=%region_9.12 | all-reduce | flops 1024 | bytes 8192 | tf_op jit(solution)/shard_map/psum | solution.py:24
  416.8 11.6 %psum.31 = f32[1,32,32]{1,2,0:T(8,128)S(1)} all-reduce(f32[1,32,32]{1,2,0:T(8,128)S(1)} %psum.30), channel_id=1, replica_groups=mesh['grp_0'=4,'grp_1'=2,'shard_0'=4,'shard_1'=4] {'shard_1'}, use_global_device_ids=true, to_apply=%region_10.13 | all-reduce | flops 1024 | bytes 8192 | tf_op jit(solution)/shard_map/psum | solution.py:24
  435.4 5.9 %fusion.15 = f32[4,32,1280]{2,1,0:T(8,128)S(1)} fusion(f32[40,4,8,1280]{3,2,1,0:T(8,128)} %bitcast.134, f32[32,320]{1,0:T(8,128)S(1)} %fusion.23), kind=kOutput, calls=%fused_computation.19 | convolution fusion | flops 629145600 | bytes 7249920 | tf_op jit(solution)/shard_map/mkr,rmc->mkc/dot_general | solution.py:98
  441.3 10.0 %all_to_all.81 = f32[4,32,1280]{2,1,0:T(8,128)S(1)} all-to-all(f32[4,32,1280]{2,1,0:T(8,128)S(1)} %fusion.15), channel_id=1, replica_groups=mesh['grp_0'=4,'grp_1'=2,'shard_0'=4,'shard_1'=4] {'shard_1'}, dimensions={0} | all-to-all | bytes 1310720 | tf_op jit(solution)/shard_map/all_to_all | solution.py:54
  451.5 20.1 %all_to_all.82 = f32[32,1,1280]{2,1,0:T(1,128)S(1)} all-to-all(f32[32,1,1280]{2,1,0:T(1,128)S(1)} %all_to_all.60), channel_id=1, replica_groups=mesh['grp_0'=4,'grp_1'=2,'shard_0'=4,'shard_1'=4] {'grp_0','grp_1','shar..., dimensions={0} | all-to-all | bytes 327680 | tf_op jit(solution)/shard_map/all_to_all | solution.py:62
  471.9 11.7 %all_to_all.83 = f32[32,1,1280]{2,1,0:T(1,128)S(1)} all-to-all(f32[32,1,1280]{2,1,0:T(1,128)S(1)} %broadcast_in_dim.28), channel_id=1, replica_groups=mesh['grp_0'=4,'grp_1'=2,'shard_0'=4,'shard_1'=4] {'grp_0','grp_1','shar..., dimensions={0} | all-to-all | bytes 327680 | tf_op jit(solution)/shard_map/all_to_all | solution.py:15
  483.7 12.9 %all_to_all.84 = f32[4,32,1280]{2,1,0:T(8,128)S(1)} all-to-all(f32[4,32,1280]{2,1,0:T(8,128)S(1)} %broadcast_in_dim.55), channel_id=1, replica_groups=mesh['grp_0'=4,'grp_1'=2,'shard_0'=4,'shard_1'=4] {'shard_1'}, dimensions={0} | all-to-all | bytes 1310720 | tf_op jit(solution)/shard_map/all_to_all | solution.py:15
  496.7 7.2 %convolution_bitcast_fusion = f32[320,1,5120]{2,0,1:T(8,128)} fusion(f32[32,5120]{1,0:T(8,128)S(1)} %bitcast.139, f32[32,320]{1,0:T(8,128)S(1)} %fusion.23), kind=kOutput, calls=%fused_computation.2 | convolution fusion | flops 629145600 | bytes 7249920 | tf_op jit(solution)/shard_map/mkr,mkc->rmc/dot_general | solution.py:100
  503.9 12.1 %fusion.5 = f32[1,320,1,5120]{3,1,2,0:T(8,128)} fusion(f32[320,1,5120]{2,0,1:T(8,128)} %convolution_bitcast_fusion, f32[320,5120]{1,0:T(8,128)} %convert_reduce_fusion, f32[1,320,1,5120]{3,2,1,0:T(1,128)} %param.9), kind=kLoop, calls=%fused_computation.9 | loop fusion | flops 3276800 | bytes 26214400 | tf_op jit(solution)/shard_map/broadcast_in_dim | solution.py:101
  516.0 10.3 %copy.70 = f32[320,1,5120]{2,1,0:T(1,128)} copy(f32[320,1,5120]{2,0,1:T(8,128)} %convolution_bitcast_fusion) | data formatting | bytes 13107200
  527.9 10.3 %copy.71 = f32[1,320,1,5120]{3,2,1,0:T(1,128)} copy(f32[1,320,1,5120]{3,1,2,0:T(8,128)} %fusion.5) | data formatting | bytes 13107200
  (47 shorter events, 21.8 us)
Async XLA Ops:
  7.2 259.1 %copy-start = (f32[1,32,5120]{2,1,0:T(8,128)S(1)}, f32[1,32,5120]{2,1,0:T(8,128)}, u32[]{:S(2)}) copy-start(f32[1,32,5120]{2,1,0:T(8,128)} %param.10) | copy-start | bytes 1966084
  7.2 206.0 %all-gather.2.cloned.1.call-start = ((), (), s32[]{:S(2)}) async-start(), calls=%async_computation.11 | async-start | bytes 33423360 | tf_op jit(solution)/shard_map/all_gather | solution.py:81
  275.9 14.3 %all-to-all-start.1 = ((f32[8,320,1,32]{1,3,2,0:T(8,128)}), f32[8,320,1,32]{1,3,2,0:T(8,128)S(1)}, u32[]{:S(2)}, u32[]{:S(2)}) async-start(f32[8,320,1,32]{1,3,2,0:T(8,128)} %broadcast_in_dim.22), calls=%async_computation.1 | async-start | bytes 786432 | tf_op jit(solution)/shard_map/all_to_all | solution.py:15
Sparse Core Ops, SparseCore 0:
  10.1 203.0 all-gather.1
where the time goes:
time: 546 us; the launch traced here: 545 us
  blocking collectives  216 us (40%)
  waiting for transfers between devices  101 us (18%)
  other arithmetic  84.6 us (15%)
  matrix products  70.6 us (13%)
  local copies, waits for them, and re-layouts  52.8 us (10%)
  between operations  14.2 us (3%)
    all_gather x1, waiting for transfers between devices, local(): piece = lax.all_gather(out_grads, SHARD, axis=1, tiled=True)  101 us
    all_to_all x5, blocking collectives, from_everyone(): lax.all_to_all(jnp.broadcast_to(x[None], (size, *x.shape)), axis, 0, 0, t...  61 us
    psum x4, blocking collectives, one_axis_at_a_time(): x = lax.psum(x, axis)  47.2 us
    unnamed x11, local copies, waits for them, and re-layouts  47.1 us
    all_to_all x1, blocking collectives, local(): lax.all_to_all(activations, SHARD, split_axis=2, concat_axis=1, tiled=True)  46.4 us
    all_to_all x2, blocking collectives, sum_by_axis(): lax.all_to_all(nearer, far, split_axis=0, concat_axis=0, tiled=True)  41.7 us
    dot_general x1, matrix products, local(): jnp.einsum('mkta,mktc->kamc', mine, grads, preferred_element_type=jnp.flo...  32.9 us
    unnamed x2, other arithmetic  29.2 us
  transfers between devices with their start and end apart: 2, of which 1 were waited for; matrix products, arithmetic and copies ran while one was open for 12% of the time, Pallas kernels for 0%

commit v1 on v0

v1 whole, which is shorter than its diff:
```python
import functools

import jax
import jax.numpy as jnp
from jax import lax
from jax.experimental import pallas as pl
from jax.experimental.pallas import tpu as pltpu
from jax.sharding import Mesh
from jax.sharding import PartitionSpec as P

GRP = ("x", "c")
SHARD = ("z", "y")
ALL = ("x", "c", "z", "y")
BF = jnp.bfloat16
F32 = jnp.float32
HIGH = lax.Precision.HIGHEST
ITERS = 2
LANES = 128
HEIGHT = 256


def shift(v, axis, by):
    n = lax.axis_size(axis)
    return lax.ppermute(v, axis, [(i, (i + by) % n) for i in range(n)])


def swapped(v):
    n = lax.axis_size("x")
    pairs = [(i * n + j, j * n + i) for i in range(n) for j in range(n)]
    return lax.ppermute(v, ("x", "y"), pairs)


def times(a, b, dims):
    return lax.dot_general(a, b, (dims, ((), ())), precision=HIGH)


def spread(v, axis, dim, size):
    n = lax.axis_size(axis)
    me = lax.axis_index(axis)
    got = []
    for k in range(n):
        piece = lax.dynamic_slice_in_dim(v, lax.rem(me + k, n) * size, size, dim)
        if k > 0:
            piece = shift(piece, axis, k)
        got.append(piece)
    return got


def ring_gather(pieces, axis):
    below = [shift(v, axis, 1) for v in pieces]
    above = [shift(v, axis, -1) for v in pieces]
    far = []
    for k in range(4):
        far.append(shift((below if k < 2 else above)[k], axis, 1 if k < 2 else -1))
    return [pieces, below, far, above]


def split_kernel(core, err, mine, other):
    rows, chunks = mine.shape[1], err.shape[0] // mine.shape[1]
    per = mine.shape[2] // LANES
    for b in range(mine.shape[0]):
        for j in range(per):
            lanes = slice(j * LANES, (j + 1) * LANES)
            for out, half in ((mine, core[0]), (other, 1 - core[0])):
                out[b, :, lanes] = err[pl.ds(2 * per * b + per * half + j, rows, stride=chunks), :]


def split_error(err, core, chunks, side):
    rows = err.shape[0] // chunks
    step = 64
    shape = jax.ShapeDtypeStruct((4, rows, side // 2), F32)
    out = pl.BlockSpec((4, step, side // 2), lambda i, s: (0, i, 0))
    return pl.pallas_call(
        split_kernel,
        out_shape=(shape, shape),
        grid_spec=pltpu.PrefetchScalarGridSpec(
            num_scalar_prefetch=1,
            grid=(rows // step,),
            in_specs=[pl.BlockSpec((step * chunks, LANES), lambda i, s: (i, 0))],
            out_specs=(out, out),
        ),
        compiler_params=pltpu.CompilerParams(vmem_limit_bytes=24 * 2**20),
        cost_estimate=pl.CostEstimate(flops=10**6, bytes_accessed=8 * err.size, transcendentals=0),
    )(core, err)


def fold_kernel(x, mine, theirs, own, *sent):
    k = pl.program_id(0)
    total = mine[...] + theirs[...]

    @pl.when(k == 0)
    def _():
        own[...] = total

    for j, out in enumerate(sent):

        @pl.when(k == j + 1)
        def _(out=out):
            out[...] = total.astype(out.dtype)


def fold(x, mine, theirs, dtype):
    rows, width = mine.shape[0] // 4, mine.shape[1]
    taken = pl.BlockSpec((rows, width), lambda k, s: (lax.rem(s[0] + k, 4), 0))
    fixed = pl.BlockSpec((rows, width), lambda k, s: (0, 0))
    sent = jax.ShapeDtypeStruct((rows, width), dtype)
    parts = pl.pallas_call(
        fold_kernel,
        out_shape=(jax.ShapeDtypeStruct((rows, width), F32), sent, sent, sent),
        grid_spec=pltpu.PrefetchScalarGridSpec(
            num_scalar_prefetch=1, grid=(4,), in_specs=[taken, taken], out_specs=(fixed,) * 4
        ),
        compiler_params=pltpu.CompilerParams(vmem_limit_bytes=16 * 2**20),
        cost_estimate=pl.CostEstimate(flops=10**6, bytes_accessed=40 * rows * width, transcendentals=0),
    )(x.astype(jnp.int32).reshape(1), mine, theirs)
    return [parts[0]] + [shift(parts[k], "x", k) for k in (1, 2, 3)]


def pair_copies(n, refs, sa, sg, sems):
    toks = sa.shape[0] // n
    copies = []
    for i in range(n):
        rows = pl.ds(i * toks, toks)
        left = pltpu.make_async_copy(refs[i], sa.at[rows], sems.at[i])
        right = pltpu.make_async_copy(refs[n + i], sg.at[rows], sems.at[n + i])
        copies.append((left, right))
    return copies


def product(sa, sg, rows, lanes):
    dims = (((0,), (0,)), ((), ()))
    return lax.dot_general(sa[rows, lanes], sg[rows, :], dims, preferred_element_type=F32)


def block_rows(n, refs, sa, sg, sems, height, store):
    step = pl.program_id(0)
    toks = sa.shape[0] // n

    @pl.when(step == 0)
    def _():
        copies = pair_copies(n, refs, sa, sg, sems)
        for left, right in copies:
            left.start()
            right.start()
        total = None
        for low in range(0, n, 3):
            high = min(low + 3, n)
            for left, right in copies[low:high]:
                left.wait()
                right.wait()
            part = product(sa, sg, slice(low * toks, high * toks), slice(0, height))
            total = part if total is None else total + part
        store(total)

    @pl.when(step > 0)
    def _():
        lanes = pl.ds(pl.multiple_of(step * height, height), height)
        store(product(sa, sg, slice(0, n * toks), lanes))


def near_kernel(n, *refs):
    out, sa, sg, sems = refs[-4:]

    def store(total):
        out[...] = total

    block_rows(n, refs, sa, sg, sems, out.shape[0], store)


def rest_kernel(n, *refs):
    core, start, rounded, mine, other, sa, sg, sems = refs[-8:]
    half = mine.shape[1]

    def store(total):
        total = start[...] + total
        rounded[...] = total.astype(BF)
        first = core[0] == 0
        low, high = total[:, :half], total[:, half:]
        mine[...] = jnp.where(first, low, high)
        other[...] = jnp.where(first, high, low)

    block_rows(n, refs, sa, sg, sems, start.shape[0], store)


def block_call(kernel, pairs, a_all, g_all, extra, extra_specs, shapes):
    a = [a_all[m][k] for m, k in pairs]
    g = [g_all[k][m] for m, k in pairs]
    n, (toks, side) = len(pairs), a[0].shape
    moved = 4 * n * toks * side + 4 * side * side
    return pl.pallas_call(
        functools.partial(kernel, n),
        grid=(side // HEIGHT,),
        out_shape=shapes,
        in_specs=[pl.BlockSpec(memory_space=pl.ANY)] * (2 * n) + extra_specs,
        out_specs=jax.tree.map(lambda v: pl.BlockSpec((HEIGHT, v.shape[1]), lambda i: (i, 0)), shapes),
        scratch_shapes=[
            pltpu.VMEM((n * toks, side), BF),
            pltpu.VMEM((n * toks, side), BF),
            pltpu.SemaphoreType.DMA((2 * n,)),
        ],
        compiler_params=pltpu.CompilerParams(vmem_limit_bytes=32 * 2**20),
        cost_estimate=pl.CostEstimate(flops=2 * n * toks * side * side, bytes_accessed=moved, transcendentals=0),
    )(*a, *g, *extra)


def small_call(kernel, shapes, args, scalars=()):
    spec = pl.BlockSpec(memory_space=pltpu.VMEM)
    return pl.pallas_call(
        kernel,
        out_shape=shapes,
        in_specs=[pl.BlockSpec(memory_space=pltpu.SMEM)] * len(scalars) + [spec] * len(args),
        out_specs=jax.tree.map(lambda _: spec, shapes),
        compiler_params=pltpu.CompilerParams(vmem_limit_bytes=16 * 2**20),
        cost_estimate=pl.CostEstimate(flops=2 * 10**8, bytes_accessed=10**6, transcendentals=0),
    )(*scalars, *args)


def dot(a, b, dims):
    return lax.dot_general(a, b, (dims, ((), ())), precision=HIGH, preferred_element_type=F32)


def left_kernel(right, mean, out):
    out[...] = dot(right[...], mean[...], ((1,), (1,)))


def left_sum_kernel(own, far, below, above, mean, out, gram):
    half = mean.shape[1]
    right = (own[...] + far[...]) + (below[...] + above[...])
    out[...] = dot(right[:, :half], mean[...], ((1,), (1,)))
    gram[...] = right[:, half : half + LANES]


def right_kernel(scaled, *refs):
    if scaled:
        inv, own, far, below, above, mean, left_out, out = refs
    else:
        own, far, below, above, mean, left_out, out = refs
    left = (own[...] + far[...]) + (below[...] + above[...])
    if scaled:
        left = dot(inv[...], left, ((1,), (0,)))
    half = mean.shape[1]
    left_out[...] = left
    out[:, :half] = dot(left, mean[...], ((1,), (0,)))
    out[:, half:] = jnp.zeros((left.shape[0], LANES), F32)
    out[:, half : half + left.shape[0]] = dot(left, left, ((1,), (1,)))


def factor_kernel(place, inv, mine, theirs, factor, stacked):
    rank = inv.shape[0]
    half = mine.shape[1]
    y, core = place[0], place[1]
    for b in range(4):
        k = lax.rem(y - b + 4, 4)
        rows = pl.ds(pl.multiple_of(k * rank, rank), rank)
        ours, others = mine[rows, :], theirs[rows, :]
        for h in range(2):
            lanes = slice((2 * b + h) * half, (2 * b + h + 1) * half)
            value = dot(inv[...], jnp.where(core == h, ours, others), ((1,), (0,)))
            factor[:, lanes] = value
            hi = value.astype(BF)
            lo = (value - hi.astype(F32)).astype(BF)
            stacked[0:rank, lanes] = hi
            stacked[rank : 2 * rank, lanes] = lo
            stacked[2 * rank : 3 * rank, lanes] = hi


def ring(v, axis):
    return v, shift(v, axis, 2), shift(v, axis, 1), shift(v, axis, -1)


def after(v, token):
    return lax.optimization_barrier((v, token))[0]


def final_kernel(me, basis, factor, err, g0, g1, g2, g3, update, error_next):
    rows, chunks = basis.shape[0], factor.shape[1] // LANES
    per = g0.shape[1] // LANES
    for j in range(chunks):
        at, lanes = pl.ds(j, rows, stride=chunks), slice(j * LANES, (j + 1) * LANES)
        b, own = j // per, slice((j % per) * LANES, (j % per + 1) * LANES)
        k = lax.rem(me[0] - b + 4, 4)
        new = jnp.dot(basis[...], factor[:, lanes], preferred_element_type=F32)
        grad = jnp.where(
            k < 2,
            jnp.where(k == 0, g0[:, own].astype(F32), g1[:, own].astype(F32)),
            jnp.where(k == 2, g2[:, own].astype(F32), g3[:, own].astype(F32)),
        )
        update[at, :] = new
        error_next[at, :] = grad + err[at, :] - new


def basis_terms(basis):
    b = basis.T
    hi = lax.reduce_precision(b, 8, 7)
    return jnp.concatenate([hi, hi, b - hi], axis=1).astype(BF)


def finish(basis, right3, err, pieces):
    left3 = basis_terms(basis)
    own_rows, width = basis.shape[1], right3.shape[1]
    side = pieces[0].shape[1]
    step = 64
    chunks = width // LANES
    me = lax.axis_index("y").astype(jnp.int32).reshape(1)
    tall = pl.BlockSpec((step * chunks, LANES), lambda i, s: (i, 0))
    grads = pl.BlockSpec((step, side), lambda i, s: (i, 0))
    shape = jax.ShapeDtypeStruct((own_rows * chunks, LANES), F32)
    return pl.pallas_call(
        final_kernel,
        out_shape=(shape, shape),
        grid_spec=pltpu.PrefetchScalarGridSpec(
            num_scalar_prefetch=1,
            grid=(own_rows // step,),
            in_specs=[
                pl.BlockSpec((step, left3.shape[1]), lambda i, s: (i, 0)),
                pl.BlockSpec(right3.shape, lambda i, s: (0, 0)),
                tall,
                *[grads] * 4,
            ],
            out_specs=(tall, tall),
        ),
        compiler_params=pltpu.CompilerParams(vmem_limit_bytes=40 * 2**20),
        cost_estimate=pl.CostEstimate(flops=2 * 96 * own_rows * width, bytes_accessed=14 * own_rows * width, transcendentals=0),
    )(me, left3, right3, err, *pieces)


def inverse_kernel(gram, out):
    rank = gram.shape[0]
    row = lax.broadcasted_iota(jnp.int32, (rank, LANES), 0)
    lane = lax.broadcasted_iota(jnp.int32, (rank, LANES), 1)
    work = jnp.where(lane < rank, gram[...], jnp.where(lane == row + rank, 1.0, 0.0))
    for j in range(rank - 1):
        pivot = work[j : j + 1, :]
        ratio = jnp.where(row > j, work[:, j : j + 1] / work[j : j + 1, j : j + 1], 0.0)
        work = work - ratio * pivot
    scale = jnp.sum(jnp.where(lane == row, work, 0.0), axis=1, keepdims=True)
    out[...] = work[:, rank : 2 * rank] / jnp.sqrt(scale)


def inverse_factor(gram):
    rank = gram.shape[0]
    return small_call(inverse_kernel, jax.ShapeDtypeStruct((rank, rank), F32), (gram,))


def local(activations, out_grads, error, q_start):
    acts, grads = activations[0], out_grads[0]
    _, width = acts.shape
    own_rows = error.shape[1]
    rank = q_start.shape[1]
    groups = lax.axis_size(GRP)
    side, half = width // 4, width // 8
    chunks = width // LANES
    x, core, y = lax.axis_index("x"), lax.axis_index("c"), lax.axis_index("y")
    core_ref = core.astype(jnp.int32).reshape(1)

    a_own = spread(acts, "z", 1, side)
    g_own = spread(grads, "y", 1, side)
    a_all = ring_gather(a_own, "y")
    g_all = ring_gather(g_own, "z")

    err = error.reshape(own_rows * chunks, LANES)
    mine, other = split_error(err, core_ref, chunks, side)
    other = shift(other, "c", 1).reshape(4 * own_rows, half)
    parts = fold(x, mine.reshape(4 * own_rows, half), other, F32)
    mean = swapped((parts[0] + parts[1]) + (parts[2] + parts[3]))

    seen = [(m, k) for m in (0, 1, 3) for k in (0, 1, 3)]
    rest = [(2, k) for k in range(4)] + [(m, 2) for m in (0, 1, 3)]
    whole = jax.ShapeDtypeStruct((side, side), F32)
    part = jax.ShapeDtypeStruct((side, half), F32)
    smem = pl.BlockSpec(memory_space=pltpu.SMEM)
    block = pl.BlockSpec((HEIGHT, side), lambda i: (i, 0))
    near = block_call(near_kernel, seen, a_all, g_all, [], [], whole)
    rounded, mine, other = block_call(
        rest_kernel, rest, a_all, g_all, [core_ref, near], [smem, block],
        (jax.ShapeDtypeStruct((side, side), BF), part, part),
    )
    parts = fold(x, mine, shift(other, "c", 1), BF)
    pieces = [lax.dynamic_slice_in_dim(rounded, lax.rem(y + k, 4) * own_rows, own_rows, 0) for k in range(4)]
    pieces[1], pieces[3] = shift(pieces[1], "y", 1), shift(pieces[3], "y", 3)
    mean = ((mean + parts[0]) + (parts[1].astype(F32) + parts[2].astype(F32)) + parts[3].astype(F32)) / groups

    right = lax.dynamic_slice_in_dim(q_start[0], y * side + core * half, half, 1)
    left_shape = jax.ShapeDtypeStruct((rank, own_rows), F32)
    right_shape = jax.ShapeDtypeStruct((rank, half + LANES), F32)
    gram_shape = jax.ShapeDtypeStruct((rank, LANES), F32)
    partial = small_call(left_kernel, left_shape, (right, mean))
    for step in range(ITERS):
        partial = partial + shift(partial, "c", 1)
        if step == 0:
            partial, pieces[1], pieces[3] = lax.optimization_barrier((partial, pieces[1], pieces[3]))
            terms = (*ring(partial, "y"), mean)
        else:
            partial, pieces[2] = lax.optimization_barrier((partial, pieces[2]))
            terms = (inverse_factor(gram), *ring(partial, "y"), mean)
        left, both = small_call(functools.partial(right_kernel, step > 0), (left_shape, right_shape), terms)
        if step == 0:
            pieces[2] = shift(after(pieces[2], both), "y", 2)
        own, far, below, above = ring(both, "z")
        both = (own + far) + (below + above)
        if step + 1 < ITERS:
            partial, gram = small_call(left_sum_kernel, (left_shape, gram_shape), (*ring(both, "x"), mean))
    own, far, below, above = ring(both, "x")
    both = (own + far) + (below + above)
    right, gram = both[:, :half], both[:, half:]
    inv = inverse_factor(gram)
    got = jnp.concatenate([right] + [shift(right, "y", k) for k in (1, 2, 3)], axis=0)
    place = jnp.stack([y, core]).astype(jnp.int32)
    right, stacked = small_call(
        factor_kernel,
        (jax.ShapeDtypeStruct((rank, width), F32), jax.ShapeDtypeStruct((3 * rank, width), BF)),
        (inv, got, shift(got, "c", 1)),
        (place,),
    )
    basis = times(inv, swapped(left), ((1,), (0,)))
    update, error_next = finish(basis, stacked, err, pieces)
    return (
        update.reshape(own_rows, 1, width),
        error_next.reshape(1, own_rows, 1, width),
        right[None],
    )


def solution(mesh):
    split = Mesh(mesh.devices.reshape(4, 2, 4, 4), ALL)

    return jax.shard_map(
        local,
        mesh=split,
        in_specs=(
            P(None, ALL, None),
            P(None, ALL, None),
            P(GRP, SHARD, None, None),
            P(),
        ),
        out_specs=(P(SHARD, None, None), P(GRP, SHARD, None, None), P()),
        check_vma=False,
    )
```

time: 546 us -> 350 us (0.64)
  blocking collectives: 216 us -> 0 us
  starting transfers between devices: 4.84 us -> 131 us
  other arithmetic: 84.6 us -> 4.08 us
  matrix products: 70.6 us -> 0.83 us
  Pallas kernels: 0 us -> 54.6 us
  waiting for transfers between devices: 101 us -> 131 us
  local copies, waits for them, and re-layouts: 52.8 us -> 26.9 us
  between operations: 14.2 us -> 1.07 us
    all_to_all x10 -> x0, blocking collectives: 169 us -> none  [the longest x5 61 us: from_everyone(): lax.all_to_all(jnp.broadcast_to(x[None], (size, *x.shape)), axis, 0, 0, t...]
    ppermute x0 -> x67, starting transfers between devices: none -> 131 us  [the longest x65 122 us: shift(): return lax.ppermute(v, axis, [(i, (i + by) % n) for i in range(n)])]
    ppermute x0 -> x67, waiting for transfers between devices: none -> 131 us  [the longest x65 131 us: shift(): return lax.ppermute(v, axis, [(i, (i + by) % n) for i in range(n)])]
    all_gather x1 -> x0, waiting for transfers between devices: 101 us -> none  [local(): piece = lax.all_gather(out_grads, SHARD, axis=1, tiled=True)]
    dot_general x8 -> x1, matrix products: 70.1 us -> 0.83 us  [times(): return lax.dot_general(a, b, (dims, ((), ())), precision=HIGH)]
    pallas_call x0 -> x13, Pallas kernels: none -> 54.6 us  [the longest x2 26.1 us: block_call(): pl.pallas_call(functools.partial(kernel, n), grid=(side // HEIGHT,), out_...]
    psum x4 -> x0, blocking collectives: 47.2 us -> none  [one_axis_at_a_time(): x = lax.psum(x, axis)]
    unnamed x2 -> x0, other arithmetic: 29.2 us -> none
  transfers between devices with their start and end apart: 2 -> 67, of which waited for: 1 -> 34; matrix products, arithmetic and copies ran while one was open for 12% -> 3% of each run, Pallas kernels for 0% -> 12%
where the time goes in v1:
time: 350 us; the launch traced here: 349 us
  starting transfers between devices  131 us (37%)
  waiting for transfers between devices  131 us (37%)
  Pallas kernels  54.6 us (16%)
  local copies, waits for them, and re-layouts  26.9 us (8%)
  other arithmetic  4.08 us (1%)
    ppermute x65, waiting for transfers between devices, shift(): return lax.ppermute(v, axis, [(i, (i + by) % n) for i in range(n)])  131 us
    ppermute x65, starting transfers between devices, shift(): return lax.ppermute(v, axis, [(i, (i + by) % n) for i in range(n)])  122 us
    pallas_call x2, Pallas kernels, block_call(): pl.pallas_call(functools.partial(kernel, n), grid=(side // HEIGHT,), out_...  26.1 us
    unnamed x58, local copies, waits for them, and re-layouts  18 us
    pallas_call x7, Pallas kernels, small_call(): pl.pallas_call(kernel, out_shape=shapes, in_specs=[pl.BlockSpec(memory_sp...  10.7 us
    ppermute x2, starting transfers between devices, swapped(): return lax.ppermute(v, ('x', 'y'), pairs)  8.54 us
    pallas_call x1, Pallas kernels, finish(): pl.pallas_call(final_kernel, out_shape=(shape, shape), grid_spec=pltpu.Pr...  7.62 us
  transfers between devices with their start and end apart: 67, of which 34 were waited for; matrix products, arithmetic and copies ran while one was open for 3% of the time, Pallas kernels for 12%

profile of v1, /device:TPU:1, one launch (start us, length us, event | category | flops | bytes accessed | tf_op | source)
XLA Modules:
  0.0 349.0 jit_solution(3787415444185129806)
XLA Ops:
  0.7 2.7 dynamic-slice_bitcast_fusion
  8.6 3.8 %collective-permute-start.13 = (bf16[192,1280]{1,0:T(8,128)(2,1)S(1)}, bf16[192,1280]{1,0:T(8,128)(2,1)S(1)}, u32[]{:S(2)}, u32[]{:S(2)}) collective-permute-start(bf16[192,1280]{1,0:T(8,128)(2,1)S(1)} %get-tuple-element.73), channel_id=1, source_target_pairs={{0,12},{4,0},{8,4},{12,8},{1,13},{5,1},{9,5},{13,9},{2,14},{6,2},{... | collective-permute-start | bytes 1474568 | tf_op jit(solution)/shard_map/ppermute | solution.py:24
  12.4 5.5 %collective-permute-done.23.refs_12_ = bf16[192,1280]{1,0:T(8,128)(2,1)S(1)} collective-permute-done((bf16[192,1280]{1,0:T(8,128)(2,1)}, bf16[192,1280]{1,0:T(8,128)(2,1)S(1)}, u32[]{:S(2)}, u32[]{:S(2)}) %collective-permute-start.23) | collective-permute-done | bytes 491552 | tf_op jit(solution)/shard_map/ppermute | solution.py:24
  17.9 3.6 %collective-permute-start.32 = (bf16[192,1280]{1,0:T(8,128)(2,1)S(1)}, bf16[192,1280]{1,0:T(8,128)(2,1)S(1)}, u32[]{:S(2)}, u32[]{:S(2)}) collective-permute-start(bf16[192,1280]{1,0:T(8,128)(2,1)S(1)} %get-tuple-element.70.refs_9_), channel_id=1, source_target_pairs={{0,12},{4,0},{8,4},{12,8},{1,13},{5,1},{9,5},{13,9},{2,14},{6,2},{... | collective-permute-start | bytes 1474568 | tf_op jit(solution)/shard_map/ppermute | solution.py:24
  26.6 8.8 %collective-permute-done.21.refs_10_ = bf16[192,1280]{1,0:T(8,128)(2,1)S(1)} collective-permute-done((bf16[192,1280]{1,0:T(8,128)(2,1)S(1)}, bf16[192,1280]{1,0:T(8,128)(2,1)S(1)}, u32[]{:S(2)}, u32[]{:S(2)}) %collective-permute-start.21) | collective-permute-done | bytes 491552 | tf_op jit(solution)/shard_map/ppermute | solution.py:24
  40.3 3.3 collective-permute-done.17.refs_7_
  43.7 3.8 %collective-permute-done.10.refs_4_ = bf16[192,1280]{1,0:T(8,128)(2,1)S(1)} collective-permute-done((bf16[192,1280]{1,0:T(8,128)(2,1)S(1)}, bf16[192,1280]{1,0:T(8,128)(2,1)S(1)}, u32[]{:S(2)}, u32[]{:S(2)}) %collective-permute-start.10) | collective-permute-done | bytes 491552 | tf_op jit(solution)/shard_map/ppermute | solution.py:24
  48.9 11.8 %collective-permute-done.24.refs_13_ = bf16[192,1280]{1,0:T(8,128)(2,1)S(1)} collective-permute-done((bf16[192,1280]{1,0:T(8,128)(2,1)S(1)}, bf16[192,1280]{1,0:T(8,128)(2,1)S(1)}, u32[]{:S(2)}, u32[]{:S(2)}) %collective-permute-start.24) | collective-permute-done | bytes 491552 | tf_op jit(solution)/shard_map/ppermute | solution.py:24
  67.8 2.9 copy-done.1
  70.8 3.4 shard_map.67
  80.1 2.7 collective-permute-start.11
  84.7 6.7 %collective-permute-done.19.refs_10_ = bf16[192,1280]{1,0:T(8,128)(2,1)S(1)} collective-permute-done((bf16[192,1280]{1,0:T(8,128)(2,1)S(1)}, bf16[192,1280]{1,0:T(8,128)(2,1)S(1)}, u32[]{:S(2)}, u32[]{:S(2)}) %collective-permute-start.19) | collective-permute-done | bytes 491552 | tf_op jit(solution)/shard_map/ppermute | solution.py:24
  96.3 10.4 %collective-permute-done.22.refs_11_ = bf16[192,1280]{1,0:T(8,128)(2,1)S(1)} collective-permute-done((bf16[192,1280]{1,0:T(8,128)(2,1)S(1)}, bf16[192,1280]{1,0:T(8,128)(2,1)S(1)}, u32[]{:S(2)}, u32[]{:S(2)}) %collective-permute-start.22) | collective-permute-done | bytes 491552 | tf_op jit(solution)/shard_map/ppermute | solution.py:24
  109.4 6.0 %collective-permute-done.6.refs_0_ = bf16[192,1280]{1,0:T(8,128)(2,1)S(1)} collective-permute-done((bf16[192,1280]{1,0:T(8,128)(2,1)S(1)}, bf16[192,1280]{1,0:T(8,128)(2,1)S(1)}, u32[]{:S(2)}, u32[]{:S(2)}) %collective-permute-start.6) | collective-permute-done | bytes 491552 | tf_op jit(solution)/shard_map/ppermute | solution.py:24
  119.2 11.9 %shard_map.69.refs_15_ = f32[1280,1280]{1,0:T(8,128)S(1)} custom-call(bf16[192,1280]{1,0:T(8,128)(2,1)S(1)} %get-tuple-element.75.refs_0_, bf16[192,1280]{1,0:T(8,128)(2,1)} %collective-permute-done.7.refs_1_, bf16[192,1280]{1,0:T(8,128)(2,1)S(1)} %collective-permute-done.13.refs_2_, bf16[192,1280]{1,0:T(8,128)(2,1)S(1)} %copy-done.19, ...), custom_call_target="tpu_custom_call" | custom-call | flops 5662310400 | bytes 15400960 | tf_op jit(solution)/shard_map/pallas_call | solution.py:190
  131.1 2.8 copy-done.26
  133.9 3.3 collective-permute-done.15.refs_3_
  137.2 14.3 %shard_map.70 = (bf16[1280,1280]{1,0:T(8,128)(2,1)S(1)}, f32[1280,640]{1,0:T(8,128)S(1)}, f32[1280,640]{1,0:T(8,128)}) custom-call(bf16[192,1280]{1,0:T(8,128)(2,1)S(1)} %collective-permute-done.6.refs_0_, bf16[192,1280]{1,0:T(8,128)(2,1)S(1)} %collective-permute-done.9.refs_1_, bf16[192,1280]{1,0:T(8,128)(2,1)S(1)} %collective-permute-done.12.refs_2_, ...), custom_call_target="tpu_custom_call" | custom-call | flops 4404019200 | bytes 13434880 | tf_op jit(solution)/shard_map/pallas_call | solution.py:190
  159.1 3.0 shard_map.68
  166.9 16.2 %collective-permute-done.1 = f32[320,640]{1,0:T(8,128)S(1)} collective-permute-done((f32[320,640]{1,0:T(8,128)S(1)}, f32[320,640]{1,0:T(8,128)S(1)}, u32[]{:S(2)}, u32[]{:S(2)}) %collective-permute-start.1) | collective-permute-done | bytes 819232 | tf_op jit(solution)/shard_map/ppermute | solution.py:24
  183.1 18.5 %collective-permute-done.2 = f32[320,640]{1,0:T(8,128)S(1)} collective-permute-done((f32[320,640]{1,0:T(8,128)S(1)}, f32[320,640]{1,0:T(8,128)S(1)}, u32[]{:S(2)}, u32[]{:S(2)}) %collective-permute-start.2) | collective-permute-done | bytes 819232 | tf_op jit(solution)/shard_map/ppermute | solution.py:24
  202.7 7.9 %collective-permute-start.4 = (f32[320,640]{1,0:T(8,128)}, f32[320,640]{1,0:T(8,128)}, u32[]{:S(2)}, u32[]{:S(2)}) collective-permute-start(f32[320,640]{1,0:T(8,128)} %add_add_fusion), channel_id=1, source_target_pairs={{0,0},{1,32},{2,64},{3,96},{32,1},{33,33},{34,65},{35,97},{64,2},{... | collective-permute-start | bytes 2457608 | tf_op jit(solution)/shard_map/ppermute | solution.py:30
  210.6 3.5 %constant_dynamic-slice_fusion = (bf16[320,1280]{1,0:T(8,128)(2,1)S(1)}, bf16[320,1280]{1,0:T(8,128)(2,1)}, bf16[320,1280]{1,0:T(8,128)(2,1)}, bf16[320,1280]{1,0:T(8,128)(2,1)}) fusion(bf16[1280,1280]{1,0:T(8,128)(2,1)} %copy-done.3, s32[]{:T(128)S(6)} %select_n.51, s32[]{:T(128)S(6)} %select_n.50, s32[]{:T(128)S(6)} %select_n.49, s32[]{:T(128)S(6)} %select_n.48), kind=kLoop, calls=%fused_computation.17 | loop fusion | bytes 6553616 | tf_op jit(solution)/shard_map/dynamic_slice | solution.py:379
  216.8 3.8 %shard_map.71 = (f32[320,640]{1,0:T(8,128)S(1)}, bf16[320,640]{1,0:T(8,128)(2,1)}, bf16[320,640]{1,0:T(8,128)(2,1)}, bf16[320,640]{1,0:T(8,128)(2,1)S(1)}) custom-call(s32[1]{0:T(128)} %bitcast.2.x, f32[1280,640]{1,0:T(8,128)S(1)} %copy-done.7, f32[1280,640]{1,0:T(8,128)} %collective-permute-done.35.theirs), custom_call_target="tpu_custom_call" | custom-call | flops 1000000 | bytes 8192000 | tf_op jit(solution)/shard_map/pallas_call | solution.py:107
  220.6 3.5 collective-permute-start.37
  224.1 33.0 %collective-permute-start.38 = (bf16[320,640]{1,0:T(8,128)(2,1)S(1)}, bf16[320,640]{1,0:T(8,128)(2,1)}, u32[]{:S(2)}, u32[]{:S(2)}) collective-permute-start(bf16[320,640]{1,0:T(8,128)(2,1)S(1)} %get-tuple-element.42), channel_id=1, source_target_pairs={{0,96},{32,0},{64,32},{96,64},{1,97},{33,1},{65,33},{97,65},{2,98}... | collective-permute-start | bytes 1228808 | tf_op jit(solution)/shard_map/ppermute | solution.py:24
  257.1 5.6 %collective-permute-done.36 = bf16[320,640]{1,0:T(8,128)(2,1)} collective-permute-done((bf16[320,640]{1,0:T(8,128)(2,1)}, bf16[320,640]{1,0:T(8,128)(2,1)}, u32[]{:S(2)}, u32[]{:S(2)}) %collective-permute-start.36) | collective-permute-done | bytes 409632 | tf_op jit(solution)/shard_map/ppermute | solution.py:24
  292.7 4.9 %collective-permute-start.51 = (f32[32,320]{1,0:T(8,128)S(1)}, f32[32,320]{1,0:T(8,128)S(1)}, u32[]{:S(2)}, u32[]{:S(2)}) collective-permute-start(f32[32,320]{1,0:T(8,128)S(1)} %get-tuple-element.47), channel_id=1, source_target_pairs={{0,16},{16,0},{1,17},{17,1},{2,18},{18,2},{3,19},{19,3},{4,20},{20... | collective-permute-start | bytes 122888 | tf_op jit(solution)/shard_map/ppermute | solution.py:24
  311.5 2.9 collective-permute-done.58
  331.3 3.7 %collective-permute-start.66 = (f32[128,640]{1,0:T(8,128)S(1)}, f32[128,640]{1,0:T(8,128)S(1)}, u32[]{:S(2)}, u32[]{:S(2)}) collective-permute-start(f32[128,640]{1,0:T(8,128)S(1)} %pad_maximum_fusion.mine), channel_id=1, source_target_pairs={{0,16},{16,0},{1,17},{17,1},{2,18},{18,2},{3,19},{19,3},{4,20},{20... | collective-permute-start | bytes 983048 | tf_op jit(solution)/shard_map/ppermute | solution.py:24
  338.5 2.9 copy-done.2
  341.3 7.6 %shard_map.79 = (f32[12800,128]{1,0:T(8,128)}, f32[12800,128]{1,0:T(8,128)}) custom-call(s32[1]{0:T(128)} %bitcast.me, bf16[320,96]{1,0:T(8,128)(2,1)S(1)} %pad_maximum_fusion.1.basis, bf16[96,5120]{1,0:T(8,128)(2,1)S(1)} %get-tuple-element.52.factor, f32[12800,128]{1,0:T(8,128)S(1)} %bitcast.30, bf16[320,1280]{1,0:T(8,128)(2,1)S(1)} %get-tuple-element.65.g0, ...), custom_call_target="tpu_custom_call" | custom-call | flops 314572800 | bytes 22937600 | tf_op jit(solution)/shard_map/pallas_call | solution.py:308
  (193 shorter events, 123.4 us)
Async XLA Ops:
  5.5 16.1 %collective-permute-start.26 = (bf16[192,1280]{1,0:T(8,128)(2,1)}, bf16[192,1280]{1,0:T(8,128)(2,1)S(1)}, u32[]{:S(2)}, u32[]{:S(2)}) collective-permute-start(bf16[192,1280]{1,0:T(8,128)(2,1)} %get-tuple-element.69), channel_id=1, source_target_pairs={{0,3},{1,0},{2,1},{3,2},{4,7},{5,4},{6,5},{7,6},{8,11},{9,8},{10,9... | collective-permute-start | bytes 1474568 | tf_op jit(solution)/shard_map/ppermute | solution.py:24
  12.4 23.1 %collective-permute-start.21 = (bf16[192,1280]{1,0:T(8,128)(2,1)S(1)}, bf16[192,1280]{1,0:T(8,128)(2,1)S(1)}, u32[]{:S(2)}, u32[]{:S(2)}) collective-permute-start(bf16[192,1280]{1,0:T(8,128)(2,1)S(1)} %get-tuple-element.70.refs_9_), channel_id=1, source_target_pairs={{0,4},{4,8},{8,12},{12,0},{1,5},{5,9},{9,13},{13,1},{2,6},{6,10},{... | collective-permute-start | bytes 1474568 | tf_op jit(solution)/shard_map/ppermute | solution.py:24
  17.9 17.5 %collective-permute-start.32 = (bf16[192,1280]{1,0:T(8,128)(2,1)S(1)}, bf16[192,1280]{1,0:T(8,128)(2,1)S(1)}, u32[]{:S(2)}, u32[]{:S(2)}) collective-permute-start(bf16[192,1280]{1,0:T(8,128)(2,1)S(1)} %get-tuple-element.70.refs_9_), channel_id=1, source_target_pairs={{0,12},{4,0},{8,4},{12,8},{1,13},{5,1},{9,5},{13,9},{2,14},{6,2},{... | collective-permute-start | bytes 1474568 | tf_op jit(solution)/shard_map/ppermute | solution.py:24
  23.1 16.7 %collective-permute-start.5 = (bf16[192,1280]{1,0:T(8,128)(2,1)S(1)}, bf16[192,1280]{1,0:T(8,128)(2,1)S(1)}, u32[]{:S(2)}, u32[]{:S(2)}) collective-permute-start(bf16[192,1280]{1,0:T(8,128)(2,1)S(1)} %get-tuple-element.75.refs_0_), channel_id=1, source_target_pairs={{0,1},{1,2},{2,3},{3,0},{4,5},{5,6},{6,7},{7,4},{8,9},{9,10},{10,1... | collective-permute-start | bytes 1474568 | tf_op jit(solution)/shard_map/ppermute | solution.py:24
  25.0 18.5 %collective-permute-start.17 = (bf16[192,1280]{1,0:T(8,128)(2,1)S(1)}, bf16[192,1280]{1,0:T(8,128)(2,1)S(1)}, u32[]{:S(2)}, u32[]{:S(2)}) collective-permute-start(bf16[192,1280]{1,0:T(8,128)(2,1)S(1)} %copy-done.28), channel_id=1, source_target_pairs={{0,2},{1,3},{2,0},{3,1},{4,6},{5,7},{6,4},{7,5},{8,10},{9,11},{10,... | collective-permute-start | bytes 1474568 | tf_op jit(solution)/shard_map/ppermute | solution.py:24
  36.3 24.3 %collective-permute-start.24 = (bf16[192,1280]{1,0:T(8,128)(2,1)S(1)}, bf16[192,1280]{1,0:T(8,128)(2,1)S(1)}, u32[]{:S(2)}, u32[]{:S(2)}) collective-permute-start(bf16[192,1280]{1,0:T(8,128)(2,1)S(1)} %collective-permute-done.23.refs_12_), channel_id=1, source_target_pairs={{0,4},{4,8},{8,12},{12,0},{1,5},{5,9},{9,13},{13,1},{2,6},{6,10},{... | collective-permute-start | bytes 1474568 | tf_op jit(solution)/shard_map/ppermute | solution.py:24
  37.1 23.6 %collective-permute-start.27 = (bf16[192,1280]{1,0:T(8,128)(2,1)S(1)}, bf16[192,1280]{1,0:T(8,128)(2,1)S(1)}, u32[]{:S(2)}, u32[]{:S(2)}) collective-permute-start(bf16[192,1280]{1,0:T(8,128)(2,1)S(1)} %collective-permute-done.26.refs_15_), channel_id=1, source_target_pairs={{0,12},{4,0},{8,4},{12,8},{1,13},{5,1},{9,5},{13,9},{2,14},{6,2},{... | collective-permute-start | bytes 1474568 | tf_op jit(solution)/shard_map/ppermute | solution.py:24
  39.8 25.7 %collective-permute-start.33 = (bf16[192,1280]{1,0:T(8,128)(2,1)S(1)}, bf16[192,1280]{1,0:T(8,128)(2,1)S(1)}, u32[]{:S(2)}, u32[]{:S(2)}) collective-permute-start(bf16[192,1280]{1,0:T(8,128)(2,1)S(1)} %collective-permute-done.23.refs_12_), channel_id=1, source_target_pairs={{0,12},{4,0},{8,4},{12,8},{1,13},{5,1},{9,5},{13,9},{2,14},{6,2},{... | collective-permute-start | bytes 1474568 | tf_op jit(solution)/shard_map/ppermute | solution.py:24
  43.6 32.3 %collective-permute-start.34 = (bf16[192,1280]{1,0:T(8,128)(2,1)S(1)}, bf16[192,1280]{1,0:T(8,128)(2,1)}, u32[]{:S(2)}, u32[]{:S(2)}) collective-permute-start(bf16[192,1280]{1,0:T(8,128)(2,1)S(1)} %collective-permute-done.26.refs_15_), channel_id=1, source_target_pairs={{0,4},{4,8},{8,12},{12,0},{1,5},{5,9},{9,13},{13,1},{2,6},{6,10},{... | collective-permute-start | bytes 1474568 | tf_op jit(solution)/shard_map/ppermute | solution.py:24
  47.5 30.2 %collective-permute-start.14 = (bf16[192,1280]{1,0:T(8,128)(2,1)S(1)}, bf16[192,1280]{1,0:T(8,128)(2,1)}, u32[]{:S(2)}, u32[]{:S(2)}) collective-permute-start(bf16[192,1280]{1,0:T(8,128)(2,1)S(1)} %collective-permute-done.13.refs_2_), channel_id=1, source_target_pairs={{0,3},{1,0},{2,1},{3,2},{4,7},{5,4},{6,5},{7,6},{8,11},{9,8},{10,9... | collective-permute-start | bytes 1474568 | tf_op jit(solution)/shard_map/ppermute | solution.py:24
  60.7 19.4 %collective-permute-start.29 = (bf16[192,1280]{1,0:T(8,128)(2,1)S(1)}, bf16[192,1280]{1,0:T(8,128)(2,1)}, u32[]{:S(2)}, u32[]{:S(2)}) collective-permute-start(bf16[192,1280]{1,0:T(8,128)(2,1)S(1)} %collective-permute-done.13.refs_2_), channel_id=1, source_target_pairs={{0,1},{1,2},{2,3},{3,0},{4,5},{5,6},{6,7},{7,4},{8,9},{9,10},{10,1... | collective-permute-start | bytes 1474568 | tf_op jit(solution)/shard_map/ppermute | solution.py:24
  60.7 22.1 %collective-permute-start.31 = (bf16[192,1280]{1,0:T(8,128)(2,1)}, bf16[192,1280]{1,0:T(8,128)(2,1)}, u32[]{:S(2)}, u32[]{:S(2)}) collective-permute-start(bf16[192,1280]{1,0:T(8,128)(2,1)} %collective-permute-done.7.refs_1_), channel_id=1, source_target_pairs={{0,3},{1,0},{2,1},{3,2},{4,7},{5,4},{6,5},{7,6},{8,11},{9,8},{10,9... | collective-permute-start | bytes 1474568 | tf_op jit(solution)/shard_map/ppermute | solution.py:24
  66.4 18.3 %collective-permute-start.8 = (bf16[192,1280]{1,0:T(8,128)(2,1)}, bf16[192,1280]{1,0:T(8,128)(2,1)}, u32[]{:S(2)}, u32[]{:S(2)}) collective-permute-start(bf16[192,1280]{1,0:T(8,128)(2,1)} %collective-permute-done.7.refs_1_), channel_id=1, source_target_pairs={{0,1},{1,2},{2,3},{3,0},{4,5},{5,6},{6,7},{7,4},{8,9},{9,10},{10,1... | collective-permute-start | bytes 1474568 | tf_op jit(solution)/shard_map/ppermute | solution.py:24
  75.9 81.3 %collective-permute-start = (f32[4,320,640]{2,1,0:T(8,128)}, f32[4,320,640]{2,1,0:T(8,128)}, u32[]{:S(2)}, u32[]{:S(2)}) collective-permute-start(f32[4,320,640]{2,1,0:T(8,128)} %get-tuple-element.32), channel_id=1, source_target_pairs={{0,16},{16,0},{1,17},{17,1},{2,18},{18,2},{3,19},{19,3},{4,20},{20... | collective-permute-start | bytes 9830408 | tf_op jit(solution)/shard_map/ppermute | solution.py:24
  84.7 22.0 %collective-permute-start.22 = (bf16[192,1280]{1,0:T(8,128)(2,1)S(1)}, bf16[192,1280]{1,0:T(8,128)(2,1)S(1)}, u32[]{:S(2)}, u32[]{:S(2)}) collective-permute-start(bf16[192,1280]{1,0:T(8,128)(2,1)S(1)} %copy-done.9), channel_id=1, source_target_pairs={{0,4},{4,8},{8,12},{12,0},{1,5},{5,9},{9,13},{13,1},{2,6},{6,10},{... | collective-permute-start | bytes 1474568 | tf_op jit(solution)/shard_map/ppermute | solution.py:24
  93.0 22.3 %collective-permute-start.6 = (bf16[192,1280]{1,0:T(8,128)(2,1)S(1)}, bf16[192,1280]{1,0:T(8,128)(2,1)S(1)}, u32[]{:S(2)}, u32[]{:S(2)}) collective-permute-start(bf16[192,1280]{1,0:T(8,128)(2,1)S(1)} %copy-done.19), channel_id=1, source_target_pairs={{0,1},{1,2},{2,3},{3,0},{4,5},{5,6},{6,7},{7,4},{8,9},{9,10},{10,1... | collective-permute-start | bytes 1474568 | tf_op jit(solution)/shard_map/ppermute | solution.py:24
  96.1 20.6 %collective-permute-start.20 = (bf16[192,1280]{1,0:T(8,128)(2,1)S(1)}, bf16[192,1280]{1,0:T(8,128)(2,1)S(1)}, u32[]{:S(2)}, u32[]{:S(2)}) collective-permute-start(bf16[192,1280]{1,0:T(8,128)(2,1)S(1)} %collective-permute-done.19.refs_10_), channel_id=1, source_target_pairs={{0,12},{4,0},{8,4},{12,8},{1,13},{5,1},{9,5},{13,9},{2,14},{6,2},{... | collective-permute-start | bytes 1474568 | tf_op jit(solution)/shard_map/ppermute | solution.py:24
  106.7 27.2 %collective-permute-start.28 = (bf16[192,1280]{1,0:T(8,128)(2,1)S(1)}, bf16[192,1280]{1,0:T(8,128)(2,1)S(1)}, u32[]{:S(2)}, u32[]{:S(2)}) collective-permute-start(bf16[192,1280]{1,0:T(8,128)(2,1)S(1)} %copy-done.23), channel_id=1, source_target_pairs={{0,12},{4,0},{8,4},{12,8},{1,13},{5,1},{9,5},{13,9},{2,14},{6,2},{... | collective-permute-start | bytes 1474568 | tf_op jit(solution)/shard_map/ppermute | solution.py:24
  115.3 18.5 %collective-permute-start.12 = (bf16[192,1280]{1,0:T(8,128)(2,1)S(1)}, bf16[192,1280]{1,0:T(8,128)(2,1)S(1)}, u32[]{:S(2)}, u32[]{:S(2)}) collective-permute-start(bf16[192,1280]{1,0:T(8,128)(2,1)S(1)} %collective-permute-done.11.refs_6_), channel_id=1, source_target_pairs={{0,3},{1,0},{2,1},{3,2},{4,7},{5,4},{6,5},{7,6},{8,11},{9,8},{10,9... | collective-permute-start | bytes 1474568 | tf_op jit(solution)/shard_map/ppermute | solution.py:24
  116.8 20.4 %collective-permute-start.15 = (bf16[192,1280]{1,0:T(8,128)(2,1)}, bf16[192,1280]{1,0:T(8,128)(2,1)S(1)}, u32[]{:S(2)}, u32[]{:S(2)}) collective-permute-start(bf16[192,1280]{1,0:T(8,128)(2,1)} %collective-permute-done.14.refs_8_), channel_id=1, source_target_pairs={{0,3},{1,0},{2,1},{3,2},{4,7},{5,4},{6,5},{7,6},{8,11},{9,8},{10,9... | collective-permute-start | bytes 1474568 | tf_op jit(solution)/shard_map/ppermute | solution.py:24
  119.2 18.0 %collective-permute-start.9 = (bf16[192,1280]{1,0:T(8,128)(2,1)}, bf16[192,1280]{1,0:T(8,128)(2,1)S(1)}, u32[]{:S(2)}, u32[]{:S(2)}) collective-permute-start(bf16[192,1280]{1,0:T(8,128)(2,1)} %collective-permute-done.8.refs_4_), channel_id=1, source_target_pairs={{0,1},{1,2},{2,3},{3,0},{4,5},{5,6},{6,7},{7,4},{8,9},{9,10},{10,1... | collective-permute-start | bytes 1474568 | tf_op jit(solution)/shard_map/ppermute | solution.py:24
  154.8 62.0 %collective-permute-start.35 = (f32[1280,640]{1,0:T(8,128)}, f32[1280,640]{1,0:T(8,128)}, u32[]{:S(2)}, u32[]{:S(2)}) collective-permute-start(f32[1280,640]{1,0:T(8,128)} %get-tuple-element.38), channel_id=1, source_target_pairs={{0,16},{16,0},{1,17},{17,1},{2,18},{18,2},{3,19},{19,3},{4,20},{20... | collective-permute-start | bytes 9830408 | tf_op jit(solution)/shard_map/ppermute | solution.py:24
  162.1 21.1 %collective-permute-start.1 = (f32[320,640]{1,0:T(8,128)S(1)}, f32[320,640]{1,0:T(8,128)S(1)}, u32[]{:S(2)}, u32[]{:S(2)}) collective-permute-start(f32[320,640]{1,0:T(8,128)S(1)} %get-tuple-element.34), channel_id=1, source_target_pairs={{0,32},{32,64},{64,96},{96,0},{1,33},{33,65},{65,97},{97,1},{2,34}... | collective-permute-start | bytes 2457608 | tf_op jit(solution)/shard_map/ppermute | solution.py:24
  163.3 38.3 %collective-permute-start.2 = (f32[320,640]{1,0:T(8,128)S(1)}, f32[320,640]{1,0:T(8,128)S(1)}, u32[]{:S(2)}, u32[]{:S(2)}) collective-permute-start(f32[320,640]{1,0:T(8,128)S(1)} %get-tuple-element.35), channel_id=1, source_target_pairs={{0,64},{32,96},{64,0},{96,32},{1,65},{33,97},{65,1},{97,33},{2,66}... | collective-permute-start | bytes 2457608 | tf_op jit(solution)/shard_map/ppermute | solution.py:24
  165.8 35.9 %collective-permute-start.3 = (f32[320,640]{1,0:T(8,128)S(1)}, f32[320,640]{1,0:T(8,128)S(1)}, u32[]{:S(2)}, u32[]{:S(2)}) collective-permute-start(f32[320,640]{1,0:T(8,128)S(1)} %get-tuple-element.36), channel_id=1, source_target_pairs={{0,96},{32,0},{64,32},{96,64},{1,97},{33,1},{65,33},{97,65},{2,98}... | collective-permute-start | bytes 2457608 | tf_op jit(solution)/shard_map/ppermute | solution.py:24
  202.7 21.4 %collective-permute-start.4 = (f32[320,640]{1,0:T(8,128)}, f32[320,640]{1,0:T(8,128)}, u32[]{:S(2)}, u32[]{:S(2)}) collective-permute-start(f32[320,640]{1,0:T(8,128)} %add_add_fusion), channel_id=1, source_target_pairs={{0,0},{1,32},{2,64},{3,96},{32,1},{33,33},{34,65},{35,97},{64,2},{... | collective-permute-start | bytes 2457608 | tf_op jit(solution)/shard_map/ppermute | solution.py:30
  214.2 56.2 %collective-permute-start.40 = (bf16[320,1280]{1,0:T(8,128)(2,1)}, bf16[320,1280]{1,0:T(8,128)(2,1)S(1)}, u32[]{:S(2)}, u32[]{:S(2)}) collective-permute-start(bf16[320,1280]{1,0:T(8,128)(2,1)} %get-tuple-element.68), channel_id=1, source_target_pairs={{0,1},{1,2},{2,3},{3,0},{4,5},{5,6},{6,7},{7,4},{8,9},{9,10},{10,1... | collective-permute-start | bytes 2457608 | tf_op jit(solution)/shard_map/ppermute | solution.py:24
  214.2 56.2 %collective-permute-start.41 = (bf16[320,1280]{1,0:T(8,128)(2,1)}, bf16[320,1280]{1,0:T(8,128)(2,1)}, u32[]{:S(2)}, u32[]{:S(2)}) collective-permute-start(bf16[320,1280]{1,0:T(8,128)(2,1)} %get-tuple-element.67), channel_id=1, source_target_pairs={{0,3},{1,0},{2,1},{3,2},{4,7},{5,4},{6,5},{7,6},{8,11},{9,8},{10,9... | collective-permute-start | bytes 2457608 | tf_op jit(solution)/shard_map/ppermute | solution.py:24
  220.6 42.1 %collective-permute-start.36 = (bf16[320,640]{1,0:T(8,128)(2,1)}, bf16[320,640]{1,0:T(8,128)(2,1)}, u32[]{:S(2)}, u32[]{:S(2)}) collective-permute-start(bf16[320,640]{1,0:T(8,128)(2,1)} %get-tuple-element.40), channel_id=1, source_target_pairs={{0,32},{32,64},{64,96},{96,0},{1,33},{33,65},{65,97},{97,1},{2,34}... | collective-permute-start | bytes 1228808 | tf_op jit(solution)/shard_map/ppermute | solution.py:24
  220.6 42.1 %collective-permute-start.37 = (bf16[320,640]{1,0:T(8,128)(2,1)}, bf16[320,640]{1,0:T(8,128)(2,1)}, u32[]{:S(2)}, u32[]{:S(2)}) collective-permute-start(bf16[320,640]{1,0:T(8,128)(2,1)} %get-tuple-element.41), channel_id=1, source_target_pairs={{0,64},{32,96},{64,0},{96,32},{1,65},{33,97},{65,1},{97,33},{2,66}... | collective-permute-start | bytes 1228808 | tf_op jit(solution)/shard_map/ppermute | solution.py:24
  224.1 41.3 %collective-permute-start.38 = (bf16[320,640]{1,0:T(8,128)(2,1)S(1)}, bf16[320,640]{1,0:T(8,128)(2,1)}, u32[]{:S(2)}, u32[]{:S(2)}) collective-permute-start(bf16[320,640]{1,0:T(8,128)(2,1)S(1)} %get-tuple-element.42), channel_id=1, source_target_pairs={{0,96},{32,0},{64,32},{96,64},{1,97},{33,1},{65,33},{97,65},{2,98}... | collective-permute-start | bytes 1228808 | tf_op jit(solution)/shard_map/ppermute | solution.py:24
  276.8 21.7 %collective-permute-start.52 = (bf16[320,1280]{1,0:T(8,128)(2,1)S(1)}, bf16[320,1280]{1,0:T(8,128)(2,1)S(1)}, u32[]{:S(2)}, u32[]{:S(2)}) collective-permute-start(bf16[320,1280]{1,0:T(8,128)(2,1)S(1)} %copy-done.27), channel_id=1, source_target_pairs={{0,2},{1,3},{2,0},{3,1},{4,6},{5,7},{6,4},{7,5},{8,10},{9,11},{10,... | collective-permute-start | bytes 2457608 | tf_op jit(solution)/shard_map/ppermute | solution.py:24
  (64 other events, 968.1 us)

commit v2 on v1

--- a/solution.py
+++ b/solution.py
@@ -17,6 +17,7 @@
 ITERS = 2
 LANES = 128
 HEIGHT = 256
+FULL = 60 * 2**20
 
 
 def shift(v, axis, by):
@@ -79,7 +80,7 @@
             in_specs=[pl.BlockSpec((step * chunks, LANES), lambda i, s: (i, 0))],
             out_specs=(out, out),
         ),
-        compiler_params=pltpu.CompilerParams(vmem_limit_bytes=24 * 2**20),
+        compiler_params=pltpu.CompilerParams(vmem_limit_bytes=FULL),
         cost_estimate=pl.CostEstimate(flops=10**6, bytes_accessed=8 * err.size, transcendentals=0),
     )(core, err)
 
@@ -110,7 +111,7 @@
         grid_spec=pltpu.PrefetchScalarGridSpec(
             num_scalar_prefetch=1, grid=(4,), in_specs=[taken, taken], out_specs=(fixed,) * 4
         ),
-        compiler_params=pltpu.CompilerParams(vmem_limit_bytes=16 * 2**20),
+        compiler_params=pltpu.CompilerParams(vmem_limit_bytes=FULL),
         cost_estimate=pl.CostEstimate(flops=10**6, bytes_accessed=40 * rows * width, transcendentals=0),
     )(x.astype(jnp.int32).reshape(1), mine, theirs)
     return [parts[0]] + [shift(parts[k], "x", k) for k in (1, 2, 3)]
@@ -163,6 +164,15 @@
 
     def store(total):
         out[...] = total
+
+    block_rows(n, refs, sa, sg, sems, out.shape[0], store)
+
+
+def middle_kernel(n, *refs):
+    start, out, sa, sg, sems = refs[-5:]
+
+    def store(total):
+        out[...] = start[...] + total
 
     block_rows(n, refs, sa, sg, sems, out.shape[0], store)
 
@@ -198,7 +208,7 @@
             pltpu.VMEM((n * toks, side), BF),
             pltpu.SemaphoreType.DMA((2 * n,)),
         ],
-        compiler_params=pltpu.CompilerParams(vmem_limit_bytes=32 * 2**20),
+        compiler_params=pltpu.CompilerParams(vmem_limit_bytes=FULL),
         cost_estimate=pl.CostEstimate(flops=2 * n * toks * side * side, bytes_accessed=moved, transcendentals=0),
     )(*a, *g, *extra)
 
@@ -319,7 +329,7 @@
             ],
             out_specs=(tall, tall),
         ),
-        compiler_params=pltpu.CompilerParams(vmem_limit_bytes=40 * 2**20),
+        compiler_params=pltpu.CompilerParams(vmem_limit_bytes=FULL),
         cost_estimate=pl.CostEstimate(flops=2 * 96 * own_rows * width, bytes_accessed=14 * own_rows * width, transcendentals=0),
     )(me, left3, right3, err, *pieces)
 
@@ -365,12 +375,14 @@
     mean = swapped((parts[0] + parts[1]) + (parts[2] + parts[3]))
 
     seen = [(m, k) for m in (0, 1, 3) for k in (0, 1, 3)]
-    rest = [(2, k) for k in range(4)] + [(m, 2) for m in (0, 1, 3)]
+    middle = [(2, 0), (0, 2), (2, 2)]
+    rest = [(2, 1), (1, 2), (2, 3), (3, 2)]
     whole = jax.ShapeDtypeStruct((side, side), F32)
     part = jax.ShapeDtypeStruct((side, half), F32)
     smem = pl.BlockSpec(memory_space=pltpu.SMEM)
     block = pl.BlockSpec((HEIGHT, side), lambda i: (i, 0))
     near = block_call(near_kernel, seen, a_all, g_all, [], [], whole)
+    near = block_call(middle_kernel, middle, a_all, g_all, [near], [block], whole)
     rounded, mine, other = block_call(
         rest_kernel, rest, a_all, g_all, [core_ref, near], [smem, block],
         (jax.ShapeDtypeStruct((side, side), BF), part, part),

time: 350 us -> 343 us (0.980)
  Pallas kernels: 54.6 us -> 75.3 us
  local copies, waits for them, and re-layouts: 26.9 us -> 10.1 us
  waiting for transfers between devices: 131 us -> 124 us
  starting transfers between devices: 131 us -> 126 us
    unnamed x58 -> x56, local copies, waits for them, and re-layouts: 18 us -> 3.65 us
    pallas_call x2 -> x3, Pallas kernels: 26.1 us -> 34.1 us  [block_call(): pl.pallas_call(functools.partial(kernel, n), grid=(side // HEIGHT,), out_...]
    ppermute x65, waiting for transfers between devices: 131 us -> 124 us  [shift(): return lax.ppermute(v, axis, [(i, (i + by) % n) for i in range(n)])]
    ppermute x2, starting transfers between devices: 8.54 us -> 2.44 us  [swapped(): return lax.ppermute(v, ('x', 'y'), pairs)]
    pallas_call x1, Pallas kernels: 7.62 us -> 12.3 us  [finish(): pl.pallas_call(final_kernel, out_shape=(shape, shape), grid_spec=pltpu.Pr...]
    pallas_call x1, Pallas kernels: 3.4 us -> 7.78 us  [split_error(): pl.pallas_call(split_kernel, out_shape=(shape, shape), grid_spec=pltpu.Pr...]
    pallas_call x2, Pallas kernels: 6.72 us -> 10.4 us  [fold(): pl.pallas_call(fold_kernel, out_shape=(jax.ShapeDtypeStruct((rows, width)...]
  transfers between devices with their start and end apart: 67 -> 67, of which waited for: 34 -> 32; matrix products, arithmetic and copies ran while one was open for 3% -> 3% of each run, Pallas kernels for 12% -> 17%
where the time goes in v2:
time: 343 us; the launch traced here: 342 us
  starting transfers between devices  126 us (37%)
  waiting for transfers between devices  124 us (36%)
  Pallas kernels  75.3 us (22%)
  local copies, waits for them, and re-layouts  10.1 us (3%)
  other arithmetic  4.77 us (1%)
    ppermute x65, waiting for transfers between devices, shift(): return lax.ppermute(v, axis, [(i, (i + by) % n) for i in range(n)])  124 us
    ppermute x65, starting transfers between devices, shift(): return lax.ppermute(v, axis, [(i, (i + by) % n) for i in range(n)])  124 us
    pallas_call x3, Pallas kernels, block_call(): pl.pallas_call(functools.partial(kernel, n), grid=(side // HEIGHT,), out_...  34.1 us
    pallas_call x1, Pallas kernels, finish(): pl.pallas_call(final_kernel, out_shape=(shape, shape), grid_spec=pltpu.Pr...  12.3 us
    pallas_call x7, Pallas kernels, small_call(): pl.pallas_call(kernel, out_shape=shapes, in_specs=[pl.BlockSpec(memory_sp...  10.7 us
    pallas_call x2, Pallas kernels, fold(): pl.pallas_call(fold_kernel, out_shape=(jax.ShapeDtypeStruct((rows, width)...  10.4 us
    pallas_call x1, Pallas kernels, split_error(): pl.pallas_call(split_kernel, out_shape=(shape, shape), grid_spec=pltpu.Pr...  7.78 us
  transfers between devices with their start and end apart: 67, of which 32 were waited for; matrix products, arithmetic and copies ran while one was open for 3% of the time, Pallas kernels for 17%

profile of v2, /device:TPU:1, one launch (start us, length us, event | category | flops | bytes accessed | tf_op | source)
XLA Modules:
  0.0 341.8 jit_solution(4298646234018170529)
XLA Ops:
  0.7 2.8 dynamic-slice_bitcast_fusion
  7.2 3.8 %collective-permute-start.10 = (bf16[192,1280]{1,0:T(8,128)(2,1)S(1)}, bf16[192,1280]{1,0:T(8,128)(2,1)S(1)}, u32[]{:S(2)}, u32[]{:S(2)}) collective-permute-start(bf16[192,1280]{1,0:T(8,128)(2,1)S(1)} %get-tuple-element.76), channel_id=1, source_target_pairs={{0,12},{4,0},{8,4},{12,8},{1,13},{5,1},{9,5},{13,9},{2,14},{6,2},{... | collective-permute-start | bytes 1474568 | tf_op jit(solution)/shard_map/ppermute | solution.py:25
  11.1 7.1 %collective-permute-done.16.refs_12_ = bf16[192,1280]{1,0:T(8,128)(2,1)} collective-permute-done((bf16[192,1280]{1,0:T(8,128)(2,1)}, bf16[192,1280]{1,0:T(8,128)(2,1)}, u32[]{:S(2)}, u32[]{:S(2)}) %collective-permute-start.16) | collective-permute-done | bytes 491552 | tf_op jit(solution)/shard_map/ppermute | solution.py:25
  18.1 3.6 %collective-permute-start.32 = (bf16[192,1280]{1,0:T(8,128)(2,1)S(1)}, bf16[192,1280]{1,0:T(8,128)(2,1)S(1)}, u32[]{:S(2)}, u32[]{:S(2)}) collective-permute-start(bf16[192,1280]{1,0:T(8,128)(2,1)S(1)} %get-tuple-element.69.refs_9_), channel_id=1, source_target_pairs={{0,12},{4,0},{8,4},{12,8},{1,13},{5,1},{9,5},{13,9},{2,14},{6,2},{... | collective-permute-start | bytes 1474568 | tf_op jit(solution)/shard_map/ppermute | solution.py:25
  21.8 2.7 collective-permute-start.30
  25.2 9.0 %collective-permute-done.26.refs_10_ = bf16[192,1280]{1,0:T(8,128)(2,1)S(1)} collective-permute-done((bf16[192,1280]{1,0:T(8,128)(2,1)S(1)}, bf16[192,1280]{1,0:T(8,128)(2,1)S(1)}, u32[]{:S(2)}, u32[]{:S(2)}) %collective-permute-start.26) | collective-permute-done | bytes 491552 | tf_op jit(solution)/shard_map/ppermute | solution.py:25
  38.4 6.0 %collective-permute-done.14.refs_3_ = bf16[192,1280]{1,0:T(8,128)(2,1)S(1)} collective-permute-done((bf16[192,1280]{1,0:T(8,128)(2,1)S(1)}, bf16[192,1280]{1,0:T(8,128)(2,1)S(1)}, u32[]{:S(2)}, u32[]{:S(2)}) %collective-permute-start.14) | collective-permute-done | bytes 491552 | tf_op jit(solution)/shard_map/ppermute | solution.py:25
  48.3 11.8 %collective-permute-done.17.refs_13_ = bf16[192,1280]{1,0:T(8,128)(2,1)S(1)} collective-permute-done((bf16[192,1280]{1,0:T(8,128)(2,1)}, bf16[192,1280]{1,0:T(8,128)(2,1)S(1)}, u32[]{:S(2)}, u32[]{:S(2)}) %collective-permute-start.17) | collective-permute-done | bytes 491552 | tf_op jit(solution)/shard_map/ppermute | solution.py:25
  62.8 3.8 %collective-permute-done.33.refs_14_ = bf16[192,1280]{1,0:T(8,128)(2,1)S(1)} collective-permute-done((bf16[192,1280]{1,0:T(8,128)(2,1)}, bf16[192,1280]{1,0:T(8,128)(2,1)S(1)}, u32[]{:S(2)}, u32[]{:S(2)}) %collective-permute-start.33) | collective-permute-done | bytes 491552 | tf_op jit(solution)/shard_map/ppermute | solution.py:25
  67.5 7.8 %shard_map.67 = (f32[4,320,640]{2,1,0:T(8,128)}, f32[4,320,640]{2,1,0:T(8,128)}) custom-call(s32[1]{0:T(128)} %bitcast.3.core.refs_8_, f32[12800,128]{1,0:T(8,128)} %bitcast.29), custom_call_target="tpu_custom_call" | custom-call | flops 1000000 | bytes 13107200 | tf_op jit(solution)/shard_map/pallas_call | solution.py:74
  79.4 2.8 collective-permute-start.13
  84.2 6.5 %collective-permute-done.19.refs_6_ = bf16[192,1280]{1,0:T(8,128)(2,1)S(1)} collective-permute-done((bf16[192,1280]{1,0:T(8,128)(2,1)S(1)}, bf16[192,1280]{1,0:T(8,128)(2,1)S(1)}, u32[]{:S(2)}, u32[]{:S(2)}) %collective-permute-start.19) | collective-permute-done | bytes 491552 | tf_op jit(solution)/shard_map/ppermute | solution.py:25
  97.0 9.2 %collective-permute-done.15.refs_4_ = bf16[192,1280]{1,0:T(8,128)(2,1)S(1)} collective-permute-done((bf16[192,1280]{1,0:T(8,128)(2,1)S(1)}, bf16[192,1280]{1,0:T(8,128)(2,1)S(1)}, u32[]{:S(2)}, u32[]{:S(2)}) %collective-permute-start.15) | collective-permute-done | bytes 491552 | tf_op jit(solution)/shard_map/ppermute | solution.py:25
  110.5 11.5 %shard_map.69.refs_6_ = f32[1280,1280]{1,0:T(8,128)} custom-call(bf16[192,1280]{1,0:T(8,128)(2,1)} %copy-done.5, bf16[192,1280]{1,0:T(8,128)(2,1)} %copy-done.20, bf16[192,1280]{1,0:T(8,128)(2,1)} %copy-done.19, bf16[192,1280]{1,0:T(8,128)(2,1)} %copy-done.23, bf16[192,1280]{1,0:T(8,128)(2,1)} %collective-permute-done.6.refs_4_, ...), custom_call_target="tpu_custom_call" | custom-call | flops 5662310400 | bytes 15400960 | tf_op jit(solution)/shard_map/pallas_call | solution.py:200
  122.1 10.7 %shard_map.70.refs_9_ = f32[1280,1280]{1,0:T(8,128)} custom-call(bf16[192,1280]{1,0:T(8,128)(2,1)} %copy-done.10, bf16[192,1280]{1,0:T(8,128)(2,1)} %copy-done.8, bf16[192,1280]{1,0:T(8,128)(2,1)} %copy-done.12, bf16[192,1280]{1,0:T(8,128)(2,1)} %copy-done.7, bf16[192,1280]{1,0:T(8,128)(2,1)} %copy-done.9, bf16[192,1280]{1,0:T(8,128)(2,1)} %copy-done.11, ...), custom_call_target="tpu_custom_call" | custom-call | flops 1887436800 | bytes 9502720 | tf_op jit(solution)/shard_map/pallas_call | solution.py:200
  133.8 11.9 %shard_map.71 = (bf16[1280,1280]{1,0:T(8,128)(2,1)}, f32[1280,640]{1,0:T(8,128)}, f32[1280,640]{1,0:T(8,128)}) custom-call(bf16[192,1280]{1,0:T(8,128)(2,1)} %collective-permute-done.7.refs_0_, bf16[192,1280]{1,0:T(8,128)(2,1)} %copy-done.16, bf16[192,1280]{1,0:T(8,128)(2,1)} %collective-permute-done.12.refs_2_, bf16[192,1280]{1,0:T(8,128)(2,1)} %copy-done.14, ...), custom_call_target="tpu_custom_call" | custom-call | flops 2516582400 | bytes 10485760 | tf_op jit(solution)/shard_map/pallas_call | solution.py:200
  145.7 2.7 collective-permute-start.35
  148.4 5.4 %shard_map.68 = (f32[320,640]{1,0:T(8,128)}, f32[320,640]{1,0:T(8,128)}, f32[320,640]{1,0:T(8,128)}, f32[320,640]{1,0:T(8,128)}) custom-call(s32[1]{0:T(128)} %bitcast.2.x, f32[1280,640]{1,0:T(8,128)} %bitcast.31, f32[1280,640]{1,0:T(8,128)} %bitcast.6.theirs), custom_call_target="tpu_custom_call" | custom-call | flops 1000000 | bytes 8192000 | tf_op jit(solution)/shard_map/pallas_call | solution.py:108
  158.7 16.4 %collective-permute-done.1 = f32[320,640]{1,0:T(8,128)S(1)} collective-permute-done((f32[320,640]{1,0:T(8,128)}, f32[320,640]{1,0:T(8,128)S(1)}, u32[]{:S(2)}, u32[]{:S(2)}) %collective-permute-start.1) | collective-permute-done | bytes 819232 | tf_op jit(solution)/shard_map/ppermute | solution.py:25
  175.0 18.5 %collective-permute-done.2 = f32[320,640]{1,0:T(8,128)S(1)} collective-permute-done((f32[320,640]{1,0:T(8,128)}, f32[320,640]{1,0:T(8,128)S(1)}, u32[]{:S(2)}, u32[]{:S(2)}) %collective-permute-start.2) | collective-permute-done | bytes 819232 | tf_op jit(solution)/shard_map/ppermute | solution.py:25
  197.5 3.3 constant_dynamic-slice_fusion
  202.9 2.8 collective-permute-start.41
  205.8 5.0 %shard_map.72 = (f32[320,640]{1,0:T(8,128)}, bf16[320,640]{1,0:T(8,128)(2,1)}, bf16[320,640]{1,0:T(8,128)(2,1)}, bf16[320,640]{1,0:T(8,128)(2,1)}) custom-call(s32[1]{0:T(128)} %bitcast.2.x, f32[1280,640]{1,0:T(8,128)} %get-tuple-element.37.mine, f32[1280,640]{1,0:T(8,128)} %collective-permute-done.35.theirs), custom_call_target="tpu_custom_call" | custom-call | flops 1000000 | bytes 8192000 | tf_op jit(solution)/shard_map/pallas_call | solution.py:108
  210.9 3.1 collective-permute-start.37
  214.0 35.9 %collective-permute-start.38 = (bf16[320,640]{1,0:T(8,128)(2,1)}, bf16[320,640]{1,0:T(8,128)(2,1)}, u32[]{:S(2)}, u32[]{:S(2)}) collective-permute-start(bf16[320,640]{1,0:T(8,128)(2,1)} %get-tuple-element.42), channel_id=1, source_target_pairs={{0,96},{32,0},{64,32},{96,64},{1,97},{33,1},{65,33},{97,65},{2,98}... | collective-permute-start | bytes 1228808 | tf_op jit(solution)/shard_map/ppermute | solution.py:25
  249.9 4.8 %collective-permute-done.36 = bf16[320,640]{1,0:T(8,128)(2,1)S(1)} collective-permute-done((bf16[320,640]{1,0:T(8,128)(2,1)}, bf16[320,640]{1,0:T(8,128)(2,1)S(1)}, u32[]{:S(2)}, u32[]{:S(2)}) %collective-permute-start.36) | collective-permute-done | bytes 409632 | tf_op jit(solution)/shard_map/ppermute | solution.py:25
  254.8 3.8 %collective-permute-done.38 = bf16[320,640]{1,0:T(8,128)(2,1)} collective-permute-done((bf16[320,640]{1,0:T(8,128)(2,1)}, bf16[320,640]{1,0:T(8,128)(2,1)}, u32[]{:S(2)}, u32[]{:S(2)}) %collective-permute-start.38) | collective-permute-done | bytes 409632 | tf_op jit(solution)/shard_map/ppermute | solution.py:25
  271.3 2.7 collective-permute-start.47
  285.3 4.4 %collective-permute-start.51 = (f32[32,320]{1,0:T(8,128)S(1)}, f32[32,320]{1,0:T(8,128)S(1)}, u32[]{:S(2)}, u32[]{:S(2)}) collective-permute-start(f32[32,320]{1,0:T(8,128)S(1)} %get-tuple-element.47), channel_id=1, source_target_pairs={{0,16},{16,0},{1,17},{17,1},{2,18},{18,2},{3,19},{19,3},{4,20},{20... | collective-permute-start | bytes 122888 | tf_op jit(solution)/shard_map/ppermute | solution.py:25
  304.1 2.7 collective-permute-done.58
  321.4 3.8 %collective-permute-start.66 = (f32[128,640]{1,0:T(8,128)S(1)}, f32[128,640]{1,0:T(8,128)S(1)}, u32[]{:S(2)}, u32[]{:S(2)}) collective-permute-start(f32[128,640]{1,0:T(8,128)S(1)} %pad_maximum_fusion.mine), channel_id=1, source_target_pairs={{0,16},{16,0},{1,17},{17,1},{2,18},{18,2},{3,19},{19,3},{4,20},{20... | collective-permute-start | bytes 983048 | tf_op jit(solution)/shard_map/ppermute | solution.py:25
  329.5 12.3 %shard_map.80 = (f32[12800,128]{1,0:T(8,128)}, f32[12800,128]{1,0:T(8,128)}) custom-call(s32[1]{0:T(128)} %bitcast.me, bf16[320,96]{1,0:T(8,128)(2,1)} %pad_maximum_fusion.1.basis, bf16[96,5120]{1,0:T(8,128)(2,1)} %copy-done.1, f32[12800,128]{1,0:T(8,128)} %bitcast.30, bf16[320,1280]{1,0:T(8,128)(2,1)} %get-tuple-element.65.g0, ...), custom_call_target="tpu_custom_call" | custom-call | flops 314572800 | bytes 22937600 | tf_op jit(solution)/shard_map/pallas_call | solution.py:318
  (192 shorter events, 102.0 us)
Async XLA Ops:
  3.5 14.7 %collective-permute-start.16 = (bf16[192,1280]{1,0:T(8,128)(2,1)}, bf16[192,1280]{1,0:T(8,128)(2,1)}, u32[]{:S(2)}, u32[]{:S(2)}) collective-permute-start(bf16[192,1280]{1,0:T(8,128)(2,1)} %get-tuple-element.70), channel_id=1, source_target_pairs={{0,1},{1,2},{2,3},{3,0},{4,5},{5,6},{6,7},{7,4},{8,9},{9,10},{10,1... | collective-permute-start | bytes 1474568 | tf_op jit(solution)/shard_map/ppermute | solution.py:25
  5.6 16.2 %collective-permute-start.20 = (bf16[192,1280]{1,0:T(8,128)(2,1)}, bf16[192,1280]{1,0:T(8,128)(2,1)}, u32[]{:S(2)}, u32[]{:S(2)}) collective-permute-start(bf16[192,1280]{1,0:T(8,128)(2,1)} %get-tuple-element.72), channel_id=1, source_target_pairs={{0,3},{1,0},{2,1},{3,2},{4,7},{5,4},{6,5},{7,6},{8,11},{9,8},{10,9... | collective-permute-start | bytes 1474568 | tf_op jit(solution)/shard_map/ppermute | solution.py:25
  11.1 23.1 %collective-permute-start.26 = (bf16[192,1280]{1,0:T(8,128)(2,1)S(1)}, bf16[192,1280]{1,0:T(8,128)(2,1)S(1)}, u32[]{:S(2)}, u32[]{:S(2)}) collective-permute-start(bf16[192,1280]{1,0:T(8,128)(2,1)S(1)} %get-tuple-element.69.refs_9_), channel_id=1, source_target_pairs={{0,4},{4,8},{8,12},{12,0},{1,5},{5,9},{9,13},{13,1},{2,6},{6,10},{... | collective-permute-start | bytes 1474568 | tf_op jit(solution)/shard_map/ppermute | solution.py:25
  18.1 16.8 %collective-permute-start.32 = (bf16[192,1280]{1,0:T(8,128)(2,1)S(1)}, bf16[192,1280]{1,0:T(8,128)(2,1)S(1)}, u32[]{:S(2)}, u32[]{:S(2)}) collective-permute-start(bf16[192,1280]{1,0:T(8,128)(2,1)S(1)} %get-tuple-element.69.refs_9_), channel_id=1, source_target_pairs={{0,12},{4,0},{8,4},{12,8},{1,13},{5,1},{9,5},{13,9},{2,14},{6,2},{... | collective-permute-start | bytes 1474568 | tf_op jit(solution)/shard_map/ppermute | solution.py:25
  21.8 15.9 %collective-permute-start.30 = (bf16[192,1280]{1,0:T(8,128)(2,1)S(1)}, bf16[192,1280]{1,0:T(8,128)(2,1)S(1)}, u32[]{:S(2)}, u32[]{:S(2)}) collective-permute-start(bf16[192,1280]{1,0:T(8,128)(2,1)S(1)} %get-tuple-element.73.refs_0_), channel_id=1, source_target_pairs={{0,3},{1,0},{2,1},{3,2},{4,7},{5,4},{6,5},{7,6},{8,11},{9,8},{10,9... | collective-permute-start | bytes 1474568 | tf_op jit(solution)/shard_map/ppermute | solution.py:25
  24.5 20.0 %collective-permute-start.14 = (bf16[192,1280]{1,0:T(8,128)(2,1)S(1)}, bf16[192,1280]{1,0:T(8,128)(2,1)S(1)}, u32[]{:S(2)}, u32[]{:S(2)}) collective-permute-start(bf16[192,1280]{1,0:T(8,128)(2,1)S(1)} %copy-done.6), channel_id=1, source_target_pairs={{0,2},{1,3},{2,0},{3,1},{4,6},{5,7},{6,4},{7,5},{8,10},{9,11},{10,... | collective-permute-start | bytes 1474568 | tf_op jit(solution)/shard_map/ppermute | solution.py:25
  35.0 25.2 %collective-permute-start.17 = (bf16[192,1280]{1,0:T(8,128)(2,1)}, bf16[192,1280]{1,0:T(8,128)(2,1)S(1)}, u32[]{:S(2)}, u32[]{:S(2)}) collective-permute-start(bf16[192,1280]{1,0:T(8,128)(2,1)} %collective-permute-done.16.refs_12_), channel_id=1, source_target_pairs={{0,4},{4,8},{8,12},{12,0},{1,5},{5,9},{9,13},{13,1},{2,6},{6,10},{... | collective-permute-start | bytes 1474568 | tf_op jit(solution)/shard_map/ppermute | solution.py:25
  35.1 25.1 %collective-permute-start.21 = (bf16[192,1280]{1,0:T(8,128)(2,1)}, bf16[192,1280]{1,0:T(8,128)(2,1)S(1)}, u32[]{:S(2)}, u32[]{:S(2)}) collective-permute-start(bf16[192,1280]{1,0:T(8,128)(2,1)} %collective-permute-done.20.refs_15_), channel_id=1, source_target_pairs={{0,12},{4,0},{8,4},{12,8},{1,13},{5,1},{9,5},{13,9},{2,14},{6,2},{... | collective-permute-start | bytes 1474568 | tf_op jit(solution)/shard_map/ppermute | solution.py:25
  37.7 28.9 %collective-permute-start.33 = (bf16[192,1280]{1,0:T(8,128)(2,1)}, bf16[192,1280]{1,0:T(8,128)(2,1)S(1)}, u32[]{:S(2)}, u32[]{:S(2)}) collective-permute-start(bf16[192,1280]{1,0:T(8,128)(2,1)} %collective-permute-done.16.refs_12_), channel_id=1, source_target_pairs={{0,12},{4,0},{8,4},{12,8},{1,13},{5,1},{9,5},{13,9},{2,14},{6,2},{... | collective-permute-start | bytes 1474568 | tf_op jit(solution)/shard_map/ppermute | solution.py:25
  44.5 30.8 %collective-permute-start.34 = (bf16[192,1280]{1,0:T(8,128)(2,1)}, bf16[192,1280]{1,0:T(8,128)(2,1)}, u32[]{:S(2)}, u32[]{:S(2)}) collective-permute-start(bf16[192,1280]{1,0:T(8,128)(2,1)} %collective-permute-done.20.refs_15_), channel_id=1, source_target_pairs={{0,4},{4,8},{8,12},{12,0},{1,5},{5,9},{9,13},{13,1},{2,6},{6,10},{... | collective-permute-start | bytes 1474568 | tf_op jit(solution)/shard_map/ppermute | solution.py:25
  47.1 29.9 %collective-permute-start.11 = (bf16[192,1280]{1,0:T(8,128)(2,1)S(1)}, bf16[192,1280]{1,0:T(8,128)(2,1)}, u32[]{:S(2)}, u32[]{:S(2)}) collective-permute-start(bf16[192,1280]{1,0:T(8,128)(2,1)S(1)} %collective-permute-done.10.refs_2_), channel_id=1, source_target_pairs={{0,3},{1,0},{2,1},{3,2},{4,7},{5,4},{6,5},{7,6},{8,11},{9,8},{10,9... | collective-permute-start | bytes 1474568 | tf_op jit(solution)/shard_map/ppermute | solution.py:25
  60.2 19.2 %collective-permute-start.29 = (bf16[192,1280]{1,0:T(8,128)(2,1)S(1)}, bf16[192,1280]{1,0:T(8,128)(2,1)}, u32[]{:S(2)}, u32[]{:S(2)}) collective-permute-start(bf16[192,1280]{1,0:T(8,128)(2,1)S(1)} %collective-permute-done.10.refs_2_), channel_id=1, source_target_pairs={{0,1},{1,2},{2,3},{3,0},{4,5},{5,6},{6,7},{7,4},{8,9},{9,10},{10,1... | collective-permute-start | bytes 1474568 | tf_op jit(solution)/shard_map/ppermute | solution.py:25
  60.2 21.9 %collective-permute-start.31 = (bf16[192,1280]{1,0:T(8,128)(2,1)S(1)}, bf16[192,1280]{1,0:T(8,128)(2,1)}, u32[]{:S(2)}, u32[]{:S(2)}) collective-permute-start(bf16[192,1280]{1,0:T(8,128)(2,1)S(1)} %collective-permute-done.5.refs_1_), channel_id=1, source_target_pairs={{0,3},{1,0},{2,1},{3,2},{4,7},{5,4},{6,5},{7,6},{8,11},{9,8},{10,9... | collective-permute-start | bytes 1474568 | tf_op jit(solution)/shard_map/ppermute | solution.py:25
  67.5 16.7 %collective-permute-start.6 = (bf16[192,1280]{1,0:T(8,128)(2,1)S(1)}, bf16[192,1280]{1,0:T(8,128)(2,1)}, u32[]{:S(2)}, u32[]{:S(2)}) collective-permute-start(bf16[192,1280]{1,0:T(8,128)(2,1)S(1)} %collective-permute-done.5.refs_1_), channel_id=1, source_target_pairs={{0,1},{1,2},{2,3},{3,0},{4,5},{5,6},{6,7},{7,4},{8,9},{9,10},{10,1... | collective-permute-start | bytes 1474568 | tf_op jit(solution)/shard_map/ppermute | solution.py:25
  75.3 73.1 %collective-permute-start = (f32[4,320,640]{2,1,0:T(8,128)}, f32[4,320,640]{2,1,0:T(8,128)}, u32[]{:S(2)}, u32[]{:S(2)}) collective-permute-start(f32[4,320,640]{2,1,0:T(8,128)} %get-tuple-element.32), channel_id=1, source_target_pairs={{0,16},{16,0},{1,17},{17,1},{2,18},{18,2},{3,19},{19,3},{4,20},{20... | collective-permute-start | bytes 9830408 | tf_op jit(solution)/shard_map/ppermute | solution.py:25
  90.7 15.5 %collective-permute-start.15 = (bf16[192,1280]{1,0:T(8,128)(2,1)S(1)}, bf16[192,1280]{1,0:T(8,128)(2,1)S(1)}, u32[]{:S(2)}, u32[]{:S(2)}) collective-permute-start(bf16[192,1280]{1,0:T(8,128)(2,1)S(1)} %collective-permute-done.14.refs_3_), channel_id=1, source_target_pairs={{0,4},{4,8},{8,12},{12,0},{1,5},{5,9},{9,13},{13,1},{2,6},{6,10},{... | collective-permute-start | bytes 1474568 | tf_op jit(solution)/shard_map/ppermute | solution.py:25
  92.3 15.2 %collective-permute-start.9 = (bf16[192,1280]{1,0:T(8,128)(2,1)S(1)}, bf16[192,1280]{1,0:T(8,128)(2,1)S(1)}, u32[]{:S(2)}, u32[]{:S(2)}) collective-permute-start(bf16[192,1280]{1,0:T(8,128)(2,1)S(1)} %collective-permute-done.8.refs_1_), channel_id=1, source_target_pairs={{0,1},{1,2},{2,3},{3,0},{4,5},{5,6},{6,7},{7,4},{8,9},{9,10},{10,1... | collective-permute-start | bytes 1474568 | tf_op jit(solution)/shard_map/ppermute | solution.py:25
  106.2 26.5 %collective-permute-start.18 = (bf16[192,1280]{1,0:T(8,128)(2,1)}, bf16[192,1280]{1,0:T(8,128)(2,1)S(1)}, u32[]{:S(2)}, u32[]{:S(2)}) collective-permute-start(bf16[192,1280]{1,0:T(8,128)(2,1)} %copy-done.25), channel_id=1, source_target_pairs={{0,4},{4,8},{8,12},{12,0},{1,5},{5,9},{9,13},{13,1},{2,6},{6,10},{... | collective-permute-start | bytes 1474568 | tf_op jit(solution)/shard_map/ppermute | solution.py:25
  107.5 25.2 %collective-permute-start.22 = (bf16[192,1280]{1,0:T(8,128)(2,1)}, bf16[192,1280]{1,0:T(8,128)(2,1)S(1)}, u32[]{:S(2)}, u32[]{:S(2)}) collective-permute-start(bf16[192,1280]{1,0:T(8,128)(2,1)} %copy-done.26), channel_id=1, source_target_pairs={{0,12},{4,0},{8,4},{12,8},{1,13},{5,1},{9,5},{13,9},{2,14},{6,2},{... | collective-permute-start | bytes 1474568 | tf_op jit(solution)/shard_map/ppermute | solution.py:25
  108.9 23.9 %collective-permute-start.12 = (bf16[192,1280]{1,0:T(8,128)(2,1)}, bf16[192,1280]{1,0:T(8,128)(2,1)}, u32[]{:S(2)}, u32[]{:S(2)}) collective-permute-start(bf16[192,1280]{1,0:T(8,128)(2,1)} %collective-permute-done.11.refs_8_), channel_id=1, source_target_pairs={{0,3},{1,0},{2,1},{3,2},{4,7},{5,4},{6,5},{7,6},{8,11},{9,8},{10,9... | collective-permute-start | bytes 1474568 | tf_op jit(solution)/shard_map/ppermute | solution.py:25
  109.5 23.3 %collective-permute-start.7 = (bf16[192,1280]{1,0:T(8,128)(2,1)}, bf16[192,1280]{1,0:T(8,128)(2,1)}, u32[]{:S(2)}, u32[]{:S(2)}) collective-permute-start(bf16[192,1280]{1,0:T(8,128)(2,1)} %collective-permute-done.6.refs_4_), channel_id=1, source_target_pairs={{0,1},{1,2},{2,3},{3,0},{4,5},{5,6},{6,7},{7,4},{8,9},{9,10},{10,1... | collective-permute-start | bytes 1474568 | tf_op jit(solution)/shard_map/ppermute | solution.py:25
  145.7 60.1 %collective-permute-start.35 = (f32[1280,640]{1,0:T(8,128)}, f32[1280,640]{1,0:T(8,128)}, u32[]{:S(2)}, u32[]{:S(2)}) collective-permute-start(f32[1280,640]{1,0:T(8,128)} %get-tuple-element.38), channel_id=1, source_target_pairs={{0,16},{16,0},{1,17},{17,1},{2,18},{18,2},{3,19},{19,3},{4,20},{20... | collective-permute-start | bytes 9830408 | tf_op jit(solution)/shard_map/ppermute | solution.py:25
  153.8 21.2 %collective-permute-start.1 = (f32[320,640]{1,0:T(8,128)}, f32[320,640]{1,0:T(8,128)S(1)}, u32[]{:S(2)}, u32[]{:S(2)}) collective-permute-start(f32[320,640]{1,0:T(8,128)} %get-tuple-element.34), channel_id=1, source_target_pairs={{0,32},{32,64},{64,96},{96,0},{1,33},{33,65},{65,97},{97,1},{2,34}... | collective-permute-start | bytes 2457608 | tf_op jit(solution)/shard_map/ppermute | solution.py:25
  155.1 38.5 %collective-permute-start.2 = (f32[320,640]{1,0:T(8,128)}, f32[320,640]{1,0:T(8,128)S(1)}, u32[]{:S(2)}, u32[]{:S(2)}) collective-permute-start(f32[320,640]{1,0:T(8,128)} %get-tuple-element.35), channel_id=1, source_target_pairs={{0,64},{32,96},{64,0},{96,32},{1,65},{33,97},{65,1},{97,33},{2,66}... | collective-permute-start | bytes 2457608 | tf_op jit(solution)/shard_map/ppermute | solution.py:25
  157.5 36.1 %collective-permute-start.3 = (f32[320,640]{1,0:T(8,128)}, f32[320,640]{1,0:T(8,128)S(1)}, u32[]{:S(2)}, u32[]{:S(2)}) collective-permute-start(f32[320,640]{1,0:T(8,128)} %get-tuple-element.36), channel_id=1, source_target_pairs={{0,96},{32,0},{64,32},{96,64},{1,97},{33,1},{65,33},{97,65},{2,98}... | collective-permute-start | bytes 2457608 | tf_op jit(solution)/shard_map/ppermute | solution.py:25
  195.8 18.2 %collective-permute-start.4 = (f32[320,640]{1,0:T(8,128)}, f32[320,640]{1,0:T(8,128)S(1)}, u32[]{:S(2)}, u32[]{:S(2)}) collective-permute-start(f32[320,640]{1,0:T(8,128)} %add_add_fusion), channel_id=1, source_target_pairs={{0,0},{1,32},{2,64},{3,96},{32,1},{33,33},{34,65},{35,97},{64,2},{... | collective-permute-start | bytes 2457608 | tf_op jit(solution)/shard_map/ppermute | solution.py:31
  200.8 62.5 %collective-permute-start.40 = (bf16[320,1280]{1,0:T(8,128)(2,1)}, bf16[320,1280]{1,0:T(8,128)(2,1)}, u32[]{:S(2)}, u32[]{:S(2)}) collective-permute-start(bf16[320,1280]{1,0:T(8,128)(2,1)} %get-tuple-element.68), channel_id=1, source_target_pairs={{0,1},{1,2},{2,3},{3,0},{4,5},{5,6},{6,7},{7,4},{8,9},{9,10},{10,1... | collective-permute-start | bytes 2457608 | tf_op jit(solution)/shard_map/ppermute | solution.py:25
  202.9 60.4 %collective-permute-start.41 = (bf16[320,1280]{1,0:T(8,128)(2,1)S(1)}, bf16[320,1280]{1,0:T(8,128)(2,1)}, u32[]{:S(2)}, u32[]{:S(2)}) collective-permute-start(bf16[320,1280]{1,0:T(8,128)(2,1)S(1)} %get-tuple-element.67), channel_id=1, source_target_pairs={{0,3},{1,0},{2,1},{3,2},{4,7},{5,4},{6,5},{7,6},{8,11},{9,8},{10,9... | collective-permute-start | bytes 2457608 | tf_op jit(solution)/shard_map/ppermute | solution.py:25
  210.7 44.0 %collective-permute-start.36 = (bf16[320,640]{1,0:T(8,128)(2,1)}, bf16[320,640]{1,0:T(8,128)(2,1)S(1)}, u32[]{:S(2)}, u32[]{:S(2)}) collective-permute-start(bf16[320,640]{1,0:T(8,128)(2,1)} %get-tuple-element.40), channel_id=1, source_target_pairs={{0,32},{32,64},{64,96},{96,0},{1,33},{33,65},{65,97},{97,1},{2,34}... | collective-permute-start | bytes 1228808 | tf_op jit(solution)/shard_map/ppermute | solution.py:25
  210.9 43.9 %collective-permute-start.37 = (bf16[320,640]{1,0:T(8,128)(2,1)}, bf16[320,640]{1,0:T(8,128)(2,1)}, u32[]{:S(2)}, u32[]{:S(2)}) collective-permute-start(bf16[320,640]{1,0:T(8,128)(2,1)} %get-tuple-element.41), channel_id=1, source_target_pairs={{0,64},{32,96},{64,0},{96,32},{1,65},{33,97},{65,1},{97,33},{2,66}... | collective-permute-start | bytes 1228808 | tf_op jit(solution)/shard_map/ppermute | solution.py:25
  214.0 44.6 %collective-permute-start.38 = (bf16[320,640]{1,0:T(8,128)(2,1)}, bf16[320,640]{1,0:T(8,128)(2,1)}, u32[]{:S(2)}, u32[]{:S(2)}) collective-permute-start(bf16[320,640]{1,0:T(8,128)(2,1)} %get-tuple-element.42), channel_id=1, source_target_pairs={{0,96},{32,0},{64,32},{96,64},{1,97},{33,1},{65,33},{97,65},{2,98}... | collective-permute-start | bytes 1228808 | tf_op jit(solution)/shard_map/ppermute | solution.py:25
  269.8 20.8 %collective-permute-start.52 = (bf16[320,1280]{1,0:T(8,128)(2,1)S(1)}, bf16[320,1280]{1,0:T(8,128)(2,1)S(1)}, u32[]{:S(2)}, u32[]{:S(2)}) collective-permute-start(bf16[320,1280]{1,0:T(8,128)(2,1)S(1)} %get-tuple-element.48), channel_id=1, source_target_pairs={{0,2},{1,3},{2,0},{3,1},{4,6},{5,7},{6,4},{7,5},{8,10},{9,11},{10,... | collective-permute-start | bytes 2457608 | tf_op jit(solution)/shard_map/ppermute | solution.py:25
  (63 other events, 1099.1 us)

commit v3 on v2

--- a/solution.py
+++ b/solution.py
@@ -164,15 +164,6 @@
 
     def store(total):
         out[...] = total
-
-    block_rows(n, refs, sa, sg, sems, out.shape[0], store)
-
-
-def middle_kernel(n, *refs):
-    start, out, sa, sg, sems = refs[-5:]
-
-    def store(total):
-        out[...] = start[...] + total
 
     block_rows(n, refs, sa, sg, sems, out.shape[0], store)
 
@@ -375,14 +366,12 @@
     mean = swapped((parts[0] + parts[1]) + (parts[2] + parts[3]))
 
     seen = [(m, k) for m in (0, 1, 3) for k in (0, 1, 3)]
-    middle = [(2, 0), (0, 2), (2, 2)]
-    rest = [(2, 1), (1, 2), (2, 3), (3, 2)]
+    rest = [(2, 0), (0, 2), (2, 2), (2, 1), (1, 2), (2, 3), (3, 2)]
     whole = jax.ShapeDtypeStruct((side, side), F32)
     part = jax.ShapeDtypeStruct((side, half), F32)
     smem = pl.BlockSpec(memory_space=pltpu.SMEM)
     block = pl.BlockSpec((HEIGHT, side), lambda i: (i, 0))
     near = block_call(near_kernel, seen, a_all, g_all, [], [], whole)
-    near = block_call(middle_kernel, middle, a_all, g_all, [near], [block], whole)
     rounded, mine, other = block_call(
         rest_kernel, rest, a_all, g_all, [core_ref, near], [smem, block],
         (jax.ShapeDtypeStruct((side, side), BF), part, part),

time: 343 us -> 348 us (1.015)
  waiting for transfers between devices: 124 us -> 137 us
  Pallas kernels: 75.3 us -> 66.4 us
  starting transfers between devices: 126 us -> 130 us
    ppermute x65, waiting for transfers between devices: 124 us -> 137 us  [shift(): return lax.ppermute(v, axis, [(i, (i + by) % n) for i in range(n)])]
    pallas_call x3 -> x2, Pallas kernels: 34.1 us -> 25.2 us  [block_call(): pl.pallas_call(functools.partial(kernel, n), grid=(side // HEIGHT,), out_...]
    ppermute x65, starting transfers between devices: 124 us -> 128 us  [shift(): return lax.ppermute(v, axis, [(i, (i + by) % n) for i in range(n)])]
  transfers between devices with their start and end apart: 67 -> 67, of which waited for: 32 -> 32; matrix products, arithmetic and copies ran while one was open for 3% -> 2% of each run, Pallas kernels for 17% -> 14%
where the time goes in v3:
time: 348 us; the launch traced here: 347 us
  waiting for transfers between devices  137 us (39%)
  starting transfers between devices  130 us (37%)
  Pallas kernels  66.4 us (19%)
  local copies, waits for them, and re-layouts  8.29 us (2%)
  other arithmetic  4.8 us (1%)
    ppermute x65, waiting for transfers between devices, shift(): return lax.ppermute(v, axis, [(i, (i + by) % n) for i in range(n)])  137 us
    ppermute x65, starting transfers between devices, shift(): return lax.ppermute(v, axis, [(i, (i + by) % n) for i in range(n)])  128 us
    pallas_call x2, Pallas kernels, block_call(): pl.pallas_call(functools.partial(kernel, n), grid=(side // HEIGHT,), out_...  25.2 us
    pallas_call x1, Pallas kernels, finish(): pl.pallas_call(final_kernel, out_shape=(shape, shape), grid_spec=pltpu.Pr...  12.3 us
    pallas_call x7, Pallas kernels, small_call(): pl.pallas_call(kernel, out_shape=shapes, in_specs=[pl.BlockSpec(memory_sp...  10.7 us
    pallas_call x2, Pallas kernels, fold(): pl.pallas_call(fold_kernel, out_shape=(jax.ShapeDtypeStruct((rows, width)...  10.4 us
    pallas_call x1, Pallas kernels, split_error(): pl.pallas_call(split_kernel, out_shape=(shape, shape), grid_spec=pltpu.Pr...  7.8 us
  transfers between devices with their start and end apart: 67, of which 32 were waited for; matrix products, arithmetic and copies ran while one was open for 2% of the time, Pallas kernels for 14%

profile of v3, /device:TPU:1, one launch (start us, length us, event | category | flops | bytes accessed | tf_op | source)
XLA Modules:
  0.0 347.5 jit_solution(11208916626769304041)
XLA Ops:
  0.7 2.8 dynamic-slice_bitcast_fusion
  11.2 7.0 %collective-permute-done.23.refs_12_ = bf16[192,1280]{1,0:T(8,128)(2,1)} collective-permute-done((bf16[192,1280]{1,0:T(8,128)(2,1)}, bf16[192,1280]{1,0:T(8,128)(2,1)}, u32[]{:S(2)}, u32[]{:S(2)}) %collective-permute-start.23) | collective-permute-done | bytes 491552 | tf_op jit(solution)/shard_map/ppermute | solution.py:25
  18.1 3.6 %collective-permute-start.32 = (bf16[192,1280]{1,0:T(8,128)(2,1)S(1)}, bf16[192,1280]{1,0:T(8,128)(2,1)S(1)}, u32[]{:S(2)}, u32[]{:S(2)}) collective-permute-start(bf16[192,1280]{1,0:T(8,128)(2,1)S(1)} %get-tuple-element.70.refs_9_), channel_id=1, source_target_pairs={{0,12},{4,0},{8,4},{12,8},{1,13},{5,1},{9,5},{13,9},{2,14},{6,2},{... | collective-permute-start | bytes 1474568 | tf_op jit(solution)/shard_map/ppermute | solution.py:25
  24.9 7.1 %collective-permute-done.18.refs_10_ = bf16[192,1280]{1,0:T(8,128)(2,1)S(1)} collective-permute-done((bf16[192,1280]{1,0:T(8,128)(2,1)S(1)}, bf16[192,1280]{1,0:T(8,128)(2,1)S(1)}, u32[]{:S(2)}, u32[]{:S(2)}) %collective-permute-start.18) | collective-permute-done | bytes 491552 | tf_op jit(solution)/shard_map/ppermute | solution.py:25
  38.9 5.4 %collective-permute-done.17.refs_7_ = bf16[192,1280]{1,0:T(8,128)(2,1)S(1)} collective-permute-done((bf16[192,1280]{1,0:T(8,128)(2,1)S(1)}, bf16[192,1280]{1,0:T(8,128)(2,1)S(1)}, u32[]{:S(2)}, u32[]{:S(2)}) %collective-permute-start.17) | collective-permute-done | bytes 491552 | tf_op jit(solution)/shard_map/ppermute | solution.py:25
  44.7 12.7 %collective-permute-done.24.refs_13_ = bf16[192,1280]{1,0:T(8,128)(2,1)S(1)} collective-permute-done((bf16[192,1280]{1,0:T(8,128)(2,1)}, bf16[192,1280]{1,0:T(8,128)(2,1)S(1)}, u32[]{:S(2)}, u32[]{:S(2)}) %collective-permute-start.24) | collective-permute-done | bytes 491552 | tf_op jit(solution)/shard_map/ppermute | solution.py:25
  58.8 5.5 %collective-permute-done.33.refs_14_ = bf16[192,1280]{1,0:T(8,128)(2,1)S(1)} collective-permute-done((bf16[192,1280]{1,0:T(8,128)(2,1)}, bf16[192,1280]{1,0:T(8,128)(2,1)S(1)}, u32[]{:S(2)}, u32[]{:S(2)}) %collective-permute-start.33) | collective-permute-done | bytes 491552 | tf_op jit(solution)/shard_map/ppermute | solution.py:25
  65.2 7.8 %shard_map.67 = (f32[4,320,640]{2,1,0:T(8,128)}, f32[4,320,640]{2,1,0:T(8,128)}) custom-call(s32[1]{0:T(128)} %bitcast.3.core.refs_14_, f32[12800,128]{1,0:T(8,128)} %bitcast.29), custom_call_target="tpu_custom_call" | custom-call | flops 1000000 | bytes 13107200 | tf_op jit(solution)/shard_map/pallas_call | solution.py:74
  73.0 4.5 %collective-permute-start = (f32[4,320,640]{2,1,0:T(8,128)}, f32[4,320,640]{2,1,0:T(8,128)}, u32[]{:S(2)}, u32[]{:S(2)}) collective-permute-start(f32[4,320,640]{2,1,0:T(8,128)} %get-tuple-element.32), channel_id=1, source_target_pairs={{0,16},{16,0},{1,17},{17,1},{2,18},{18,2},{3,19},{19,3},{4,20},{20... | collective-permute-start | bytes 9830408 | tf_op jit(solution)/shard_map/ppermute | solution.py:25
  80.4 9.9 %collective-permute-done.20.refs_12_ = bf16[192,1280]{1,0:T(8,128)(2,1)S(1)} collective-permute-done((bf16[192,1280]{1,0:T(8,128)(2,1)S(1)}, bf16[192,1280]{1,0:T(8,128)(2,1)S(1)}, u32[]{:S(2)}, u32[]{:S(2)}) %collective-permute-start.20) | collective-permute-done | bytes 491552 | tf_op jit(solution)/shard_map/ppermute | solution.py:25
  93.9 10.2 %collective-permute-done.22.refs_10_ = bf16[192,1280]{1,0:T(8,128)(2,1)S(1)} collective-permute-done((bf16[192,1280]{1,0:T(8,128)(2,1)S(1)}, bf16[192,1280]{1,0:T(8,128)(2,1)S(1)}, u32[]{:S(2)}, u32[]{:S(2)}) %collective-permute-start.22) | collective-permute-done | bytes 491552 | tf_op jit(solution)/shard_map/ppermute | solution.py:25
  106.9 7.0 %collective-permute-done.6.refs_0_ = bf16[192,1280]{1,0:T(8,128)(2,1)S(1)} collective-permute-done((bf16[192,1280]{1,0:T(8,128)(2,1)}, bf16[192,1280]{1,0:T(8,128)(2,1)S(1)}, u32[]{:S(2)}, u32[]{:S(2)}) %collective-permute-start.6) | collective-permute-done | bytes 491552 | tf_op jit(solution)/shard_map/ppermute | solution.py:25
  113.9 2.9 collective-permute-start.16
  117.1 11.6 %shard_map.69.refs_15_ = f32[1280,1280]{1,0:T(8,128)} custom-call(bf16[192,1280]{1,0:T(8,128)(2,1)} %copy-done.5, bf16[192,1280]{1,0:T(8,128)(2,1)} %copy-done.7, bf16[192,1280]{1,0:T(8,128)(2,1)} %copy-done.8, bf16[192,1280]{1,0:T(8,128)(2,1)} %copy-done.15, bf16[192,1280]{1,0:T(8,128)(2,1)} %collective-permute-done.11.refs_4_, ...), custom_call_target="tpu_custom_call" | custom-call | flops 5662310400 | bytes 15400960 | tf_op jit(solution)/shard_map/pallas_call | solution.py:191
  128.7 7.5 %collective-permute-done.9.refs_2_ = bf16[192,1280]{1,0:T(8,128)(2,1)} collective-permute-done((bf16[192,1280]{1,0:T(8,128)(2,1)}, bf16[192,1280]{1,0:T(8,128)(2,1)}, u32[]{:S(2)}, u32[]{:S(2)}) %collective-permute-start.9) | collective-permute-done | bytes 491552 | tf_op jit(solution)/shard_map/ppermute | solution.py:25
  136.2 13.7 %shard_map.70 = (bf16[1280,1280]{1,0:T(8,128)(2,1)}, f32[1280,640]{1,0:T(8,128)}, f32[1280,640]{1,0:T(8,128)}) custom-call(bf16[192,1280]{1,0:T(8,128)(2,1)} %copy-done.23, bf16[192,1280]{1,0:T(8,128)(2,1)} %copy-done.12, bf16[192,1280]{1,0:T(8,128)(2,1)} %collective-permute-done.9.refs_2_, bf16[192,1280]{1,0:T(8,128)(2,1)} %collective-permute-done.12.refs_3_, ...), custom_call_target="tpu_custom_call" | custom-call | flops 4404019200 | bytes 13434880 | tf_op jit(solution)/shard_map/pallas_call | solution.py:191
  149.8 3.0 collective-permute-start.35
  152.9 5.4 %shard_map.68 = (f32[320,640]{1,0:T(8,128)}, f32[320,640]{1,0:T(8,128)}, f32[320,640]{1,0:T(8,128)}, f32[320,640]{1,0:T(8,128)}) custom-call(s32[1]{0:T(128)} %bitcast.2.x, f32[1280,640]{1,0:T(8,128)} %bitcast.31, f32[1280,640]{1,0:T(8,128)} %bitcast.6.theirs), custom_call_target="tpu_custom_call" | custom-call | flops 1000000 | bytes 8192000 | tf_op jit(solution)/shard_map/pallas_call | solution.py:108
  163.1 16.4 %collective-permute-done.1 = f32[320,640]{1,0:T(8,128)S(1)} collective-permute-done((f32[320,640]{1,0:T(8,128)}, f32[320,640]{1,0:T(8,128)S(1)}, u32[]{:S(2)}, u32[]{:S(2)}) %collective-permute-start.1) | collective-permute-done | bytes 819232 | tf_op jit(solution)/shard_map/ppermute | solution.py:25
  179.4 18.5 %collective-permute-done.2 = f32[320,640]{1,0:T(8,128)S(1)} collective-permute-done((f32[320,640]{1,0:T(8,128)}, f32[320,640]{1,0:T(8,128)S(1)}, u32[]{:S(2)}, u32[]{:S(2)}) %collective-permute-start.2) | collective-permute-done | bytes 819232 | tf_op jit(solution)/shard_map/ppermute | solution.py:25
  202.0 3.2 constant_dynamic-slice_fusion
  207.4 2.8 collective-permute-start.41
  210.2 5.0 %shard_map.71 = (f32[320,640]{1,0:T(8,128)}, bf16[320,640]{1,0:T(8,128)(2,1)}, bf16[320,640]{1,0:T(8,128)(2,1)}, bf16[320,640]{1,0:T(8,128)(2,1)}) custom-call(s32[1]{0:T(128)} %bitcast.2.x, f32[1280,640]{1,0:T(8,128)} %get-tuple-element.37.mine, f32[1280,640]{1,0:T(8,128)} %collective-permute-done.35.theirs), custom_call_target="tpu_custom_call" | custom-call | flops 1000000 | bytes 8192000 | tf_op jit(solution)/shard_map/pallas_call | solution.py:108
  215.2 4.9 %collective-permute-start.37 = (bf16[320,640]{1,0:T(8,128)(2,1)}, bf16[320,640]{1,0:T(8,128)(2,1)}, u32[]{:S(2)}, u32[]{:S(2)}) collective-permute-start(bf16[320,640]{1,0:T(8,128)(2,1)} %get-tuple-element.41), channel_id=1, source_target_pairs={{0,64},{32,96},{64,0},{96,32},{1,65},{33,97},{65,1},{97,33},{2,66}... | collective-permute-start | bytes 1228808 | tf_op jit(solution)/shard_map/ppermute | solution.py:25
  220.0 33.6 %collective-permute-start.38 = (bf16[320,640]{1,0:T(8,128)(2,1)}, bf16[320,640]{1,0:T(8,128)(2,1)}, u32[]{:S(2)}, u32[]{:S(2)}) collective-permute-start(bf16[320,640]{1,0:T(8,128)(2,1)} %get-tuple-element.42), channel_id=1, source_target_pairs={{0,96},{32,0},{64,32},{96,64},{1,97},{33,1},{65,33},{97,65},{2,98}... | collective-permute-start | bytes 1228808 | tf_op jit(solution)/shard_map/ppermute | solution.py:25
  253.7 7.0 %collective-permute-done.36 = bf16[320,640]{1,0:T(8,128)(2,1)S(1)} collective-permute-done((bf16[320,640]{1,0:T(8,128)(2,1)}, bf16[320,640]{1,0:T(8,128)(2,1)S(1)}, u32[]{:S(2)}, u32[]{:S(2)}) %collective-permute-start.36) | collective-permute-done | bytes 409632 | tf_op jit(solution)/shard_map/ppermute | solution.py:25
  267.2 3.4 collective-permute-start.43
  280.7 3.3 collective-permute-done.46
  291.4 4.0 %collective-permute-start.51 = (f32[32,320]{1,0:T(8,128)S(1)}, f32[32,320]{1,0:T(8,128)S(1)}, u32[]{:S(2)}, u32[]{:S(2)}) collective-permute-start(f32[32,320]{1,0:T(8,128)S(1)} %get-tuple-element.47), channel_id=1, source_target_pairs={{0,16},{16,0},{1,17},{17,1},{2,18},{18,2},{3,19},{19,3},{4,20},{20... | collective-permute-start | bytes 122888 | tf_op jit(solution)/shard_map/ppermute | solution.py:25
  319.0 3.3 collective-permute-start.64
  326.4 4.5 %collective-permute-start.66 = (f32[128,640]{1,0:T(8,128)S(1)}, f32[128,640]{1,0:T(8,128)S(1)}, u32[]{:S(2)}, u32[]{:S(2)}) collective-permute-start(f32[128,640]{1,0:T(8,128)S(1)} %pad_maximum_fusion.mine), channel_id=1, source_target_pairs={{0,16},{16,0},{1,17},{17,1},{2,18},{18,2},{3,19},{19,3},{4,20},{20... | collective-permute-start | bytes 983048 | tf_op jit(solution)/shard_map/ppermute | solution.py:25
  335.2 12.3 %shard_map.79 = (f32[12800,128]{1,0:T(8,128)}, f32[12800,128]{1,0:T(8,128)}) custom-call(s32[1]{0:T(128)} %bitcast.me, bf16[320,96]{1,0:T(8,128)(2,1)} %pad_maximum_fusion.1.basis, bf16[96,5120]{1,0:T(8,128)(2,1)} %copy-done.1, f32[12800,128]{1,0:T(8,128)} %bitcast.30, bf16[320,1280]{1,0:T(8,128)(2,1)} %get-tuple-element.65.g0, ...), custom_call_target="tpu_custom_call" | custom-call | flops 314572800 | bytes 22937600 | tf_op jit(solution)/shard_map/pallas_call | solution.py:309
  (189 shorter events, 96.7 us)
Async XLA Ops:
  5.6 16.2 %collective-permute-start.26 = (bf16[192,1280]{1,0:T(8,128)(2,1)}, bf16[192,1280]{1,0:T(8,128)(2,1)}, u32[]{:S(2)}, u32[]{:S(2)}) collective-permute-start(bf16[192,1280]{1,0:T(8,128)(2,1)} %get-tuple-element.69), channel_id=1, source_target_pairs={{0,3},{1,0},{2,1},{3,2},{4,7},{5,4},{6,5},{7,6},{8,11},{9,8},{10,9... | collective-permute-start | bytes 1474568 | tf_op jit(solution)/shard_map/ppermute | solution.py:25
  7.2 16.0 %collective-permute-start.10 = (bf16[192,1280]{1,0:T(8,128)(2,1)S(1)}, bf16[192,1280]{1,0:T(8,128)(2,1)S(1)}, u32[]{:S(2)}, u32[]{:S(2)}) collective-permute-start(bf16[192,1280]{1,0:T(8,128)(2,1)S(1)} %get-tuple-element.76), channel_id=1, source_target_pairs={{0,4},{4,8},{8,12},{12,0},{1,5},{5,9},{9,13},{13,1},{2,6},{6,10},{... | collective-permute-start | bytes 1474568 | tf_op jit(solution)/shard_map/ppermute | solution.py:25
  11.1 20.9 %collective-permute-start.18 = (bf16[192,1280]{1,0:T(8,128)(2,1)S(1)}, bf16[192,1280]{1,0:T(8,128)(2,1)S(1)}, u32[]{:S(2)}, u32[]{:S(2)}) collective-permute-start(bf16[192,1280]{1,0:T(8,128)(2,1)S(1)} %get-tuple-element.70.refs_9_), channel_id=1, source_target_pairs={{0,4},{4,8},{8,12},{12,0},{1,5},{5,9},{9,13},{13,1},{2,6},{6,10},{... | collective-permute-start | bytes 1474568 | tf_op jit(solution)/shard_map/ppermute | solution.py:25
  18.1 14.9 %collective-permute-start.32 = (bf16[192,1280]{1,0:T(8,128)(2,1)S(1)}, bf16[192,1280]{1,0:T(8,128)(2,1)S(1)}, u32[]{:S(2)}, u32[]{:S(2)}) collective-permute-start(bf16[192,1280]{1,0:T(8,128)(2,1)S(1)} %get-tuple-element.70.refs_9_), channel_id=1, source_target_pairs={{0,12},{4,0},{8,4},{12,8},{1,13},{5,1},{9,5},{13,9},{2,14},{6,2},{... | collective-permute-start | bytes 1474568 | tf_op jit(solution)/shard_map/ppermute | solution.py:25
  23.3 21.0 %collective-permute-start.17 = (bf16[192,1280]{1,0:T(8,128)(2,1)S(1)}, bf16[192,1280]{1,0:T(8,128)(2,1)S(1)}, u32[]{:S(2)}, u32[]{:S(2)}) collective-permute-start(bf16[192,1280]{1,0:T(8,128)(2,1)S(1)} %copy-done.6), channel_id=1, source_target_pairs={{0,2},{1,3},{2,0},{3,1},{4,6},{5,7},{6,4},{7,5},{8,10},{9,11},{10,... | collective-permute-start | bytes 1474568 | tf_op jit(solution)/shard_map/ppermute | solution.py:25
  33.1 24.3 %collective-permute-start.24 = (bf16[192,1280]{1,0:T(8,128)(2,1)}, bf16[192,1280]{1,0:T(8,128)(2,1)S(1)}, u32[]{:S(2)}, u32[]{:S(2)}) collective-permute-start(bf16[192,1280]{1,0:T(8,128)(2,1)} %collective-permute-done.23.refs_12_), channel_id=1, source_target_pairs={{0,4},{4,8},{8,12},{12,0},{1,5},{5,9},{9,13},{13,1},{2,6},{6,10},{... | collective-permute-start | bytes 1474568 | tf_op jit(solution)/shard_map/ppermute | solution.py:25
  33.9 24.7 %collective-permute-start.27 = (bf16[192,1280]{1,0:T(8,128)(2,1)}, bf16[192,1280]{1,0:T(8,128)(2,1)S(1)}, u32[]{:S(2)}, u32[]{:S(2)}) collective-permute-start(bf16[192,1280]{1,0:T(8,128)(2,1)} %collective-permute-done.26.refs_15_), channel_id=1, source_target_pairs={{0,12},{4,0},{8,4},{12,8},{1,13},{5,1},{9,5},{13,9},{2,14},{6,2},{... | collective-permute-start | bytes 1474568 | tf_op jit(solution)/shard_map/ppermute | solution.py:25
  36.5 27.9 %collective-permute-start.33 = (bf16[192,1280]{1,0:T(8,128)(2,1)}, bf16[192,1280]{1,0:T(8,128)(2,1)S(1)}, u32[]{:S(2)}, u32[]{:S(2)}) collective-permute-start(bf16[192,1280]{1,0:T(8,128)(2,1)} %collective-permute-done.23.refs_12_), channel_id=1, source_target_pairs={{0,12},{4,0},{8,4},{12,8},{1,13},{5,1},{9,5},{13,9},{2,14},{6,2},{... | collective-permute-start | bytes 1474568 | tf_op jit(solution)/shard_map/ppermute | solution.py:25
  44.3 28.7 %collective-permute-start.34 = (bf16[192,1280]{1,0:T(8,128)(2,1)}, bf16[192,1280]{1,0:T(8,128)(2,1)}, u32[]{:S(2)}, u32[]{:S(2)}) collective-permute-start(bf16[192,1280]{1,0:T(8,128)(2,1)} %collective-permute-done.26.refs_15_), channel_id=1, source_target_pairs={{0,4},{4,8},{8,12},{12,0},{1,5},{5,9},{9,13},{13,1},{2,6},{6,10},{... | collective-permute-start | bytes 1474568 | tf_op jit(solution)/shard_map/ppermute | solution.py:25
  44.7 32.8 %collective-permute-start.11 = (bf16[192,1280]{1,0:T(8,128)(2,1)S(1)}, bf16[192,1280]{1,0:T(8,128)(2,1)}, u32[]{:S(2)}, u32[]{:S(2)}) collective-permute-start(bf16[192,1280]{1,0:T(8,128)(2,1)S(1)} %collective-permute-done.10.refs_1_), channel_id=1, source_target_pairs={{0,1},{1,2},{2,3},{3,0},{4,5},{5,6},{6,7},{7,4},{8,9},{9,10},{10,1... | collective-permute-start | bytes 1474568 | tf_op jit(solution)/shard_map/ppermute | solution.py:25
  57.3 22.5 %collective-permute-start.15 = (bf16[192,1280]{1,0:T(8,128)(2,1)S(1)}, bf16[192,1280]{1,0:T(8,128)(2,1)}, u32[]{:S(2)}, u32[]{:S(2)}) collective-permute-start(bf16[192,1280]{1,0:T(8,128)(2,1)S(1)} %collective-permute-done.14.refs_2_), channel_id=1, source_target_pairs={{0,3},{1,0},{2,1},{3,2},{4,7},{5,4},{6,5},{7,6},{8,11},{9,8},{10,9... | collective-permute-start | bytes 1474568 | tf_op jit(solution)/shard_map/ppermute | solution.py:25
  58.6 21.7 %collective-permute-start.29 = (bf16[192,1280]{1,0:T(8,128)(2,1)S(1)}, bf16[192,1280]{1,0:T(8,128)(2,1)}, u32[]{:S(2)}, u32[]{:S(2)}) collective-permute-start(bf16[192,1280]{1,0:T(8,128)(2,1)S(1)} %collective-permute-done.14.refs_2_), channel_id=1, source_target_pairs={{0,1},{1,2},{2,3},{3,0},{4,5},{5,6},{6,7},{7,4},{8,9},{9,10},{10,1... | collective-permute-start | bytes 1474568 | tf_op jit(solution)/shard_map/ppermute | solution.py:25
  65.2 15.1 %collective-permute-start.31 = (bf16[192,1280]{1,0:T(8,128)(2,1)S(1)}, bf16[192,1280]{1,0:T(8,128)(2,1)}, u32[]{:S(2)}, u32[]{:S(2)}) collective-permute-start(bf16[192,1280]{1,0:T(8,128)(2,1)S(1)} %collective-permute-done.10.refs_1_), channel_id=1, source_target_pairs={{0,3},{1,0},{2,1},{3,2},{4,7},{5,4},{6,5},{7,6},{8,11},{9,8},{10,9... | collective-permute-start | bytes 1474568 | tf_op jit(solution)/shard_map/ppermute | solution.py:25
  73.0 79.8 %collective-permute-start = (f32[4,320,640]{2,1,0:T(8,128)}, f32[4,320,640]{2,1,0:T(8,128)}, u32[]{:S(2)}, u32[]{:S(2)}) collective-permute-start(f32[4,320,640]{2,1,0:T(8,128)} %get-tuple-element.32), channel_id=1, source_target_pairs={{0,16},{16,0},{1,17},{17,1},{2,18},{18,2},{3,19},{19,3},{4,20},{20... | collective-permute-start | bytes 9830408 | tf_op jit(solution)/shard_map/ppermute | solution.py:25
  80.3 23.8 %collective-permute-start.22 = (bf16[192,1280]{1,0:T(8,128)(2,1)S(1)}, bf16[192,1280]{1,0:T(8,128)(2,1)S(1)}, u32[]{:S(2)}, u32[]{:S(2)}) collective-permute-start(bf16[192,1280]{1,0:T(8,128)(2,1)S(1)} %collective-permute-done.17.refs_7_), channel_id=1, source_target_pairs={{0,4},{4,8},{8,12},{12,0},{1,5},{5,9},{9,13},{13,1},{2,6},{6,10},{... | collective-permute-start | bytes 1474568 | tf_op jit(solution)/shard_map/ppermute | solution.py:25
  92.4 21.5 %collective-permute-start.6 = (bf16[192,1280]{1,0:T(8,128)(2,1)}, bf16[192,1280]{1,0:T(8,128)(2,1)S(1)}, u32[]{:S(2)}, u32[]{:S(2)}) collective-permute-start(bf16[192,1280]{1,0:T(8,128)(2,1)} %copy-done.15), channel_id=1, source_target_pairs={{0,1},{1,2},{2,3},{3,0},{4,5},{5,6},{6,7},{7,4},{8,9},{9,10},{10,1... | collective-permute-start | bytes 1474568 | tf_op jit(solution)/shard_map/ppermute | solution.py:25
  93.7 20.3 %collective-permute-start.21 = (bf16[192,1280]{1,0:T(8,128)(2,1)S(1)}, bf16[192,1280]{1,0:T(8,128)(2,1)S(1)}, u32[]{:S(2)}, u32[]{:S(2)}) collective-permute-start(bf16[192,1280]{1,0:T(8,128)(2,1)S(1)} %collective-permute-done.20.refs_12_), channel_id=1, source_target_pairs={{0,12},{4,0},{8,4},{12,8},{1,13},{5,1},{9,5},{13,9},{2,14},{6,2},{... | collective-permute-start | bytes 1474568 | tf_op jit(solution)/shard_map/ppermute | solution.py:25
  104.2 24.5 %collective-permute-start.28 = (bf16[192,1280]{1,0:T(8,128)(2,1)}, bf16[192,1280]{1,0:T(8,128)(2,1)S(1)}, u32[]{:S(2)}, u32[]{:S(2)}) collective-permute-start(bf16[192,1280]{1,0:T(8,128)(2,1)} %copy-done.17), channel_id=1, source_target_pairs={{0,12},{4,0},{8,4},{12,8},{1,13},{5,1},{9,5},{13,9},{2,14},{6,2},{... | collective-permute-start | bytes 1474568 | tf_op jit(solution)/shard_map/ppermute | solution.py:25
  113.9 14.8 %collective-permute-start.12 = (bf16[192,1280]{1,0:T(8,128)(2,1)}, bf16[192,1280]{1,0:T(8,128)(2,1)}, u32[]{:S(2)}, u32[]{:S(2)}) collective-permute-start(bf16[192,1280]{1,0:T(8,128)(2,1)} %collective-permute-done.11.refs_4_), channel_id=1, source_target_pairs={{0,1},{1,2},{2,3},{3,0},{4,5},{5,6},{6,7},{7,4},{8,9},{9,10},{10,1... | collective-permute-start | bytes 1474568 | tf_op jit(solution)/shard_map/ppermute | solution.py:25
  113.9 14.8 %collective-permute-start.16 = (bf16[192,1280]{1,0:T(8,128)(2,1)}, bf16[192,1280]{1,0:T(8,128)(2,1)}, u32[]{:S(2)}, u32[]{:S(2)}) collective-permute-start(bf16[192,1280]{1,0:T(8,128)(2,1)} %collective-permute-done.15.refs_8_), channel_id=1, source_target_pairs={{0,3},{1,0},{2,1},{3,2},{4,7},{5,4},{6,5},{7,6},{8,11},{9,8},{10,9... | collective-permute-start | bytes 1474568 | tf_op jit(solution)/shard_map/ppermute | solution.py:25
  116.9 19.3 %collective-permute-start.9 = (bf16[192,1280]{1,0:T(8,128)(2,1)}, bf16[192,1280]{1,0:T(8,128)(2,1)}, u32[]{:S(2)}, u32[]{:S(2)}) collective-permute-start(bf16[192,1280]{1,0:T(8,128)(2,1)} %collective-permute-done.8.refs_6_), channel_id=1, source_target_pairs={{0,3},{1,0},{2,1},{3,2},{4,7},{5,4},{6,5},{7,6},{8,11},{9,8},{10,9... | collective-permute-start | bytes 1474568 | tf_op jit(solution)/shard_map/ppermute | solution.py:25
  149.8 60.3 %collective-permute-start.35 = (f32[1280,640]{1,0:T(8,128)}, f32[1280,640]{1,0:T(8,128)}, u32[]{:S(2)}, u32[]{:S(2)}) collective-permute-start(f32[1280,640]{1,0:T(8,128)} %get-tuple-element.38), channel_id=1, source_target_pairs={{0,16},{16,0},{1,17},{17,1},{2,18},{18,2},{3,19},{19,3},{4,20},{20... | collective-permute-start | bytes 9830408 | tf_op jit(solution)/shard_map/ppermute | solution.py:25
  158.3 21.2 %collective-permute-start.1 = (f32[320,640]{1,0:T(8,128)}, f32[320,640]{1,0:T(8,128)S(1)}, u32[]{:S(2)}, u32[]{:S(2)}) collective-permute-start(f32[320,640]{1,0:T(8,128)} %get-tuple-element.34), channel_id=1, source_target_pairs={{0,32},{32,64},{64,96},{96,0},{1,33},{33,65},{65,97},{97,1},{2,34}... | collective-permute-start | bytes 2457608 | tf_op jit(solution)/shard_map/ppermute | solution.py:25
  159.5 38.5 %collective-permute-start.2 = (f32[320,640]{1,0:T(8,128)}, f32[320,640]{1,0:T(8,128)S(1)}, u32[]{:S(2)}, u32[]{:S(2)}) collective-permute-start(f32[320,640]{1,0:T(8,128)} %get-tuple-element.35), channel_id=1, source_target_pairs={{0,64},{32,96},{64,0},{96,32},{1,65},{33,97},{65,1},{97,33},{2,66}... | collective-permute-start | bytes 2457608 | tf_op jit(solution)/shard_map/ppermute | solution.py:25
  161.9 36.1 %collective-permute-start.3 = (f32[320,640]{1,0:T(8,128)}, f32[320,640]{1,0:T(8,128)S(1)}, u32[]{:S(2)}, u32[]{:S(2)}) collective-permute-start(f32[320,640]{1,0:T(8,128)} %get-tuple-element.36), channel_id=1, source_target_pairs={{0,96},{32,0},{64,32},{96,64},{1,97},{33,1},{65,33},{97,65},{2,98}... | collective-permute-start | bytes 2457608 | tf_op jit(solution)/shard_map/ppermute | solution.py:25
  200.2 19.8 %collective-permute-start.4 = (f32[320,640]{1,0:T(8,128)}, f32[320,640]{1,0:T(8,128)S(1)}, u32[]{:S(2)}, u32[]{:S(2)}) collective-permute-start(f32[320,640]{1,0:T(8,128)} %add_add_fusion), channel_id=1, source_target_pairs={{0,0},{1,32},{2,64},{3,96},{32,1},{33,33},{34,65},{35,97},{64,2},{... | collective-permute-start | bytes 2457608 | tf_op jit(solution)/shard_map/ppermute | solution.py:31
  205.2 61.8 %collective-permute-start.40 = (bf16[320,1280]{1,0:T(8,128)(2,1)}, bf16[320,1280]{1,0:T(8,128)(2,1)}, u32[]{:S(2)}, u32[]{:S(2)}) collective-permute-start(bf16[320,1280]{1,0:T(8,128)(2,1)} %get-tuple-element.68), channel_id=1, source_target_pairs={{0,1},{1,2},{2,3},{3,0},{4,5},{5,6},{6,7},{7,4},{8,9},{9,10},{10,1... | collective-permute-start | bytes 2457608 | tf_op jit(solution)/shard_map/ppermute | solution.py:25
  207.4 59.7 %collective-permute-start.41 = (bf16[320,1280]{1,0:T(8,128)(2,1)S(1)}, bf16[320,1280]{1,0:T(8,128)(2,1)}, u32[]{:S(2)}, u32[]{:S(2)}) collective-permute-start(bf16[320,1280]{1,0:T(8,128)(2,1)S(1)} %get-tuple-element.67), channel_id=1, source_target_pairs={{0,3},{1,0},{2,1},{3,2},{4,7},{5,4},{6,5},{7,6},{8,11},{9,8},{10,9... | collective-permute-start | bytes 2457608 | tf_op jit(solution)/shard_map/ppermute | solution.py:25
  215.2 45.5 %collective-permute-start.36 = (bf16[320,640]{1,0:T(8,128)(2,1)}, bf16[320,640]{1,0:T(8,128)(2,1)S(1)}, u32[]{:S(2)}, u32[]{:S(2)}) collective-permute-start(bf16[320,640]{1,0:T(8,128)(2,1)} %get-tuple-element.40), channel_id=1, source_target_pairs={{0,32},{32,64},{64,96},{96,0},{1,33},{33,65},{65,97},{97,1},{2,34}... | collective-permute-start | bytes 1228808 | tf_op jit(solution)/shard_map/ppermute | solution.py:25
  215.2 45.5 %collective-permute-start.37 = (bf16[320,640]{1,0:T(8,128)(2,1)}, bf16[320,640]{1,0:T(8,128)(2,1)}, u32[]{:S(2)}, u32[]{:S(2)}) collective-permute-start(bf16[320,640]{1,0:T(8,128)(2,1)} %get-tuple-element.41), channel_id=1, source_target_pairs={{0,64},{32,96},{64,0},{96,32},{1,65},{33,97},{65,1},{97,33},{2,66}... | collective-permute-start | bytes 1228808 | tf_op jit(solution)/shard_map/ppermute | solution.py:25
  220.0 42.3 %collective-permute-start.38 = (bf16[320,640]{1,0:T(8,128)(2,1)}, bf16[320,640]{1,0:T(8,128)(2,1)}, u32[]{:S(2)}, u32[]{:S(2)}) collective-permute-start(bf16[320,640]{1,0:T(8,128)(2,1)} %get-tuple-element.42), channel_id=1, source_target_pairs={{0,96},{32,0},{64,32},{96,64},{1,97},{33,1},{65,33},{97,65},{2,98}... | collective-permute-start | bytes 1228808 | tf_op jit(solution)/shard_map/ppermute | solution.py:25
  274.4 21.9 %collective-permute-start.52 = (bf16[320,1280]{1,0:T(8,128)(2,1)S(1)}, bf16[320,1280]{1,0:T(8,128)(2,1)S(1)}, u32[]{:S(2)}, u32[]{:S(2)}) collective-permute-start(bf16[320,1280]{1,0:T(8,128)(2,1)S(1)} %get-tuple-element.48), channel_id=1, source_target_pairs={{0,2},{1,3},{2,0},{3,1},{4,6},{5,7},{6,4},{7,5},{8,10},{9,11},{10,... | collective-permute-start | bytes 2457608 | tf_op jit(solution)/shard_map/ppermute | solution.py:25
  (62 other events, 1135.6 us)

commit v4 on v3

--- a/solution.py
+++ b/solution.py
@@ -161,15 +161,24 @@
 
 def near_kernel(n, *refs):
     out, sa, sg, sems = refs[-4:]
-
-    def store(total):
-        out[...] = total
-
-    block_rows(n, refs, sa, sg, sems, out.shape[0], store)
+    height = out.shape[0]
+
+    @pl.when(pl.program_id(0) == 0)
+    def _():
+        copies = pair_copies(n, refs, sa, sg, sems)
+        for left, right in copies:
+            left.start()
+            right.start()
+        for left, right in copies:
+            left.wait()
+            right.wait()
+
+    lanes = pl.ds(pl.multiple_of(pl.program_id(0) * height, height), height)
+    out[...] = product(sa, sg, slice(0, sa.shape[0]), lanes)
 
 
 def rest_kernel(n, *refs):
-    core, start, rounded, mine, other, sa, sg, sems = refs[-8:]
+    core, start, right, rounded, mine, other, left, sa, sg, sems = refs[-10:]
     half = mine.shape[1]
 
     def store(total):
@@ -181,6 +190,16 @@
         other[...] = jnp.where(first, high, low)
 
     block_rows(n, refs, sa, sg, sems, start.shape[0], store)
+    first = core[0] == 0
+    low, high = right[:, :half], right[:, half:]
+    total = dot(jnp.where(first, low, high), mine[...], ((1,), (1,)))
+    left[...] = total + dot(jnp.where(first, high, low), other[...], ((1,), (1,)))
+
+
+def block_spec(v):
+    if v.shape[0] < HEIGHT:
+        return pl.BlockSpec((v.shape[0], HEIGHT), lambda i: (0, i))
+    return pl.BlockSpec((HEIGHT, v.shape[1]), lambda i: (i, 0))
 
 
 def block_call(kernel, pairs, a_all, g_all, extra, extra_specs, shapes):
@@ -193,7 +212,7 @@
         grid=(side // HEIGHT,),
         out_shape=shapes,
         in_specs=[pl.BlockSpec(memory_space=pl.ANY)] * (2 * n) + extra_specs,
-        out_specs=jax.tree.map(lambda v: pl.BlockSpec((HEIGHT, v.shape[1]), lambda i: (i, 0)), shapes),
+        out_specs=jax.tree.map(block_spec, shapes),
         scratch_shapes=[
             pltpu.VMEM((n * toks, side), BF),
             pltpu.VMEM((n * toks, side), BF),
@@ -267,10 +286,6 @@
 
 def ring(v, axis):
     return v, shift(v, axis, 2), shift(v, axis, 1), shift(v, axis, -1)
-
-
-def after(v, token):
-    return lax.optimization_barrier((v, token))[0]
 
 
 def final_kernel(me, basis, factor, err, g0, g1, g2, g3, update, error_next):
@@ -320,7 +335,7 @@
             ],
             out_specs=(tall, tall),
         ),
-        compiler_params=pltpu.CompilerParams(vmem_limit_bytes=FULL),
+        compiler_params=pltpu.CompilerParams(vmem_limit_bytes=40 * 2**20),
         cost_estimate=pl.CostEstimate(flops=2 * 96 * own_rows * width, bytes_accessed=14 * own_rows * width, transcendentals=0),
     )(me, left3, right3, err, *pieces)
 
@@ -372,31 +387,35 @@
     smem = pl.BlockSpec(memory_space=pltpu.SMEM)
     block = pl.BlockSpec((HEIGHT, side), lambda i: (i, 0))
     near = block_call(near_kernel, seen, a_all, g_all, [], [], whole)
-    rounded, mine, other = block_call(
-        rest_kernel, rest, a_all, g_all, [core_ref, near], [smem, block],
-        (jax.ShapeDtypeStruct((side, side), BF), part, part),
+    right = lax.dynamic_slice_in_dim(q_start[0], y * side, side, 1)
+    start_spec = pl.BlockSpec(right.shape, lambda i: (0, 0))
+    rounded, mine, other, partial = block_call(
+        rest_kernel, rest, a_all, g_all, [core_ref, near, right], [smem, block, start_spec],
+        (jax.ShapeDtypeStruct((side, side), BF), part, part, jax.ShapeDtypeStruct(right.shape, F32)),
     )
-    parts = fold(x, mine, shift(other, "c", 1), BF)
+    theirs = shift(other, "c", 1)
+    terms = spread(partial, "x", 1, own_rows)
+    right = lax.dynamic_slice_in_dim(right, core * half, half, 1)
+    partial = small_call(left_kernel, jax.ShapeDtypeStruct((rank, own_rows), F32), (right, mean))
+    partial = (partial + (terms[0] + terms[2])) + (terms[1] + terms[3])
+    partial = (partial + shift(partial, "c", 1)) / groups
+    first = (partial, shift(partial, "y", 2), shift(partial, "y", 1), shift(partial, "y", -1))
+    parts = fold(x, mine, theirs, BF)
     pieces = [lax.dynamic_slice_in_dim(rounded, lax.rem(y + k, 4) * own_rows, own_rows, 0) for k in range(4)]
-    pieces[1], pieces[3] = shift(pieces[1], "y", 1), shift(pieces[3], "y", 3)
+    pieces = pieces[:1] + [shift(pieces[k], "y", k) for k in (1, 2, 3)]
     mean = ((mean + parts[0]) + (parts[1].astype(F32) + parts[2].astype(F32)) + parts[3].astype(F32)) / groups
 
-    right = lax.dynamic_slice_in_dim(q_start[0], y * side + core * half, half, 1)
     left_shape = jax.ShapeDtypeStruct((rank, own_rows), F32)
     right_shape = jax.ShapeDtypeStruct((rank, half + LANES), F32)
     gram_shape = jax.ShapeDtypeStruct((rank, LANES), F32)
-    partial = small_call(left_kernel, left_shape, (right, mean))
     for step in range(ITERS):
-        partial = partial + shift(partial, "c", 1)
         if step == 0:
-            partial, pieces[1], pieces[3] = lax.optimization_barrier((partial, pieces[1], pieces[3]))
-            terms = (*ring(partial, "y"), mean)
+            terms = (*first, mean)
         else:
-            partial, pieces[2] = lax.optimization_barrier((partial, pieces[2]))
+            partial = partial + shift(partial, "c", 1)
+            partial, pieces = lax.optimization_barrier((partial, pieces))
             terms = (inverse_factor(gram), *ring(partial, "y"), mean)
         left, both = small_call(functools.partial(right_kernel, step > 0), (left_shape, right_shape), terms)
-        if step == 0:
-            pieces[2] = shift(after(pieces[2], both), "y", 2)
         own, far, below, above = ring(both, "z")
         both = (own + far) + (below + above)
         if step + 1 < ITERS:

time: 348 us -> 380 us (1.092)
  waiting for transfers between devices: 137 us -> 186 us
  starting transfers between devices: 130 us -> 111 us
    ppermute x65 -> x68, waiting for transfers between devices: 137 us -> 186 us  [shift(): return lax.ppermute(v, axis, [(i, (i + by) % n) for i in range(n)])]
    ppermute x65 -> x68, starting transfers between devices: 128 us -> 110 us  [shift(): return lax.ppermute(v, axis, [(i, (i + by) % n) for i in range(n)])]
    pallas_call x1, Pallas kernels: 12.3 us -> 6.76 us  [finish(): pl.pallas_call(final_kernel, out_shape=(shape, shape), grid_spec=pltpu.Pr...]
    pallas_call x2, Pallas kernels: 25.2 us -> 29.8 us  [block_call(): pl.pallas_call(functools.partial(kernel, n), grid=(side // HEIGHT,), out_...]
  transfers between devices with their start and end apart: 67 -> 70, of which waited for: 32 -> 32; matrix products, arithmetic and copies ran while one was open for 2% -> 2% of each run, Pallas kernels for 14% -> 15%
where the time goes in v4:
time: 380 us
  waiting for transfers between devices  186 us (49%)
  starting transfers between devices  111 us (29%)
  Pallas kernels  65.4 us (17%)
  local copies, waits for them, and re-layouts  12 us (3%)
    ppermute x68, waiting for transfers between devices, shift(): return lax.ppermute(v, axis, [(i, (i + by) % n) for i in range(n)])  186 us
    ppermute x68, starting transfers between devices, shift(): return lax.ppermute(v, axis, [(i, (i + by) % n) for i in range(n)])  110 us
    pallas_call x2, Pallas kernels, block_call(): pl.pallas_call(functools.partial(kernel, n), grid=(side // HEIGHT,), out_...  29.8 us
    pallas_call x7, Pallas kernels, small_call(): pl.pallas_call(kernel, out_shape=shapes, in_specs=[pl.BlockSpec(memory_sp...  10.7 us
    pallas_call x2, Pallas kernels, fold(): pl.pallas_call(fold_kernel, out_shape=(jax.ShapeDtypeStruct((rows, width)...  10.4 us
    pallas_call x1, Pallas kernels, split_error(): pl.pallas_call(split_kernel, out_shape=(shape, shape), grid_spec=pltpu.Pr...  7.74 us
  transfers between devices with their start and end apart: 70, of which 32 were waited for; matrix products, arithmetic and copies ran while one was open for 2% of the time, Pallas kernels for 15%

profile of v4, /device:TPU:1, one launch (start us, length us, event | category | flops | bytes accessed | tf_op | source)
XLA Modules:
  0.0 379.8 jit_solution(10812487696803899137)
XLA Ops:
  0.7 2.8 dynamic-slice_bitcast_fusion
  11.2 7.0 %collective-permute-done.23.refs_12_ = bf16[192,1280]{1,0:T(8,128)(2,1)} collective-permute-done((bf16[192,1280]{1,0:T(8,128)(2,1)}, bf16[192,1280]{1,0:T(8,128)(2,1)}, u32[]{:S(2)}, u32[]{:S(2)}) %collective-permute-start.23) | collective-permute-done | bytes 491552 | tf_op jit(solution)/shard_map/ppermute | solution.py:25
  18.1 3.6 collective-permute-start.32
  24.9 7.2 %collective-permute-done.18.refs_10_ = bf16[192,1280]{1,0:T(8,128)(2,1)S(1)} collective-permute-done((bf16[192,1280]{1,0:T(8,128)(2,1)S(1)}, bf16[192,1280]{1,0:T(8,128)(2,1)S(1)}, u32[]{:S(2)}, u32[]{:S(2)}) %collective-permute-start.18) | collective-permute-done | bytes 491552 | tf_op jit(solution)/shard_map/ppermute | solution.py:25
  39.0 5.4 %collective-permute-done.17.refs_7_ = bf16[192,1280]{1,0:T(8,128)(2,1)S(1)} collective-permute-done((bf16[192,1280]{1,0:T(8,128)(2,1)S(1)}, bf16[192,1280]{1,0:T(8,128)(2,1)S(1)}, u32[]{:S(2)}, u32[]{:S(2)}) %collective-permute-start.17) | collective-permute-done | bytes 491552 | tf_op jit(solution)/shard_map/ppermute | solution.py:25
  45.0 12.5 %collective-permute-done.24.refs_13_ = bf16[192,1280]{1,0:T(8,128)(2,1)} collective-permute-done((bf16[192,1280]{1,0:T(8,128)(2,1)}, bf16[192,1280]{1,0:T(8,128)(2,1)}, u32[]{:S(2)}, u32[]{:S(2)}) %collective-permute-start.24) | collective-permute-done | bytes 491552 | tf_op jit(solution)/shard_map/ppermute | solution.py:25
  58.9 5.6 %collective-permute-done.33.refs_14_ = bf16[192,1280]{1,0:T(8,128)(2,1)S(1)} collective-permute-done((bf16[192,1280]{1,0:T(8,128)(2,1)}, bf16[192,1280]{1,0:T(8,128)(2,1)S(1)}, u32[]{:S(2)}, u32[]{:S(2)}) %collective-permute-start.33) | collective-permute-done | bytes 491552 | tf_op jit(solution)/shard_map/ppermute | solution.py:25
  65.4 7.7 %shard_map.67 = (f32[4,320,640]{2,1,0:T(8,128)}, f32[4,320,640]{2,1,0:T(8,128)}) custom-call(s32[1]{0:T(128)} %bitcast.3.core.refs_14_, f32[12800,128]{1,0:T(8,128)} %bitcast.31), custom_call_target="tpu_custom_call" | custom-call | flops 1000000 | bytes 13107200 | tf_op jit(solution)/shard_map/pallas_call | solution.py:74
  73.2 4.4 %collective-permute-start = (f32[4,320,640]{2,1,0:T(8,128)}, f32[4,320,640]{2,1,0:T(8,128)}, u32[]{:S(2)}, u32[]{:S(2)}) collective-permute-start(f32[4,320,640]{2,1,0:T(8,128)} %get-tuple-element.32), channel_id=1, source_target_pairs={{0,16},{16,0},{1,17},{17,1},{2,18},{18,2},{3,19},{19,3},{4,20},{20... | collective-permute-start | bytes 9830408 | tf_op jit(solution)/shard_map/ppermute | solution.py:25
  80.5 9.9 %collective-permute-done.20.refs_12_ = bf16[192,1280]{1,0:T(8,128)(2,1)S(1)} collective-permute-done((bf16[192,1280]{1,0:T(8,128)(2,1)S(1)}, bf16[192,1280]{1,0:T(8,128)(2,1)S(1)}, u32[]{:S(2)}, u32[]{:S(2)}) %collective-permute-start.20) | collective-permute-done | bytes 491552 | tf_op jit(solution)/shard_map/ppermute | solution.py:25
  94.0 10.3 %collective-permute-done.22.refs_10_ = bf16[192,1280]{1,0:T(8,128)(2,1)S(1)} collective-permute-done((bf16[192,1280]{1,0:T(8,128)(2,1)S(1)}, bf16[192,1280]{1,0:T(8,128)(2,1)S(1)}, u32[]{:S(2)}, u32[]{:S(2)}) %collective-permute-start.22) | collective-permute-done | bytes 491552 | tf_op jit(solution)/shard_map/ppermute | solution.py:25
  107.7 6.6 %collective-permute-done.6.refs_0_ = bf16[192,1280]{1,0:T(8,128)(2,1)} collective-permute-done((bf16[192,1280]{1,0:T(8,128)(2,1)}, bf16[192,1280]{1,0:T(8,128)(2,1)}, u32[]{:S(2)}, u32[]{:S(2)}) %collective-permute-start.6) | collective-permute-done | bytes 491552 | tf_op jit(solution)/shard_map/ppermute | solution.py:25
  117.1 12.1 %shard_map.70.refs_15_ = f32[1280,1280]{1,0:T(8,128)} custom-call(bf16[192,1280]{1,0:T(8,128)(2,1)} %copy-done.9, bf16[192,1280]{1,0:T(8,128)(2,1)} %copy-done.12, bf16[192,1280]{1,0:T(8,128)(2,1)} %copy-done.13, bf16[192,1280]{1,0:T(8,128)(2,1)} %collective-permute-done.5.refs_3_, bf16[192,1280]{1,0:T(8,128)(2,1)} %collective-permute-done.11.refs_4_, ...), custom_call_target="tpu_custom_call" | custom-call | flops 5662310400 | bytes 15400960 | tf_op jit(solution)/shard_map/pallas_call | solution.py:210
  129.3 7.0 %collective-permute-done.9.refs_2_ = bf16[192,1280]{1,0:T(8,128)(2,1)} collective-permute-done((bf16[192,1280]{1,0:T(8,128)(2,1)}, bf16[192,1280]{1,0:T(8,128)(2,1)}, u32[]{:S(2)}, u32[]{:S(2)}) %collective-permute-start.9) | collective-permute-done | bytes 491552 | tf_op jit(solution)/shard_map/ppermute | solution.py:25
  136.3 17.7 %shard_map.71 = (bf16[1280,1280]{1,0:T(8,128)(2,1)}, f32[1280,640]{1,0:T(8,128)}, f32[1280,640]{1,0:T(8,128)}, f32[32,1280]{1,0:T(8,128)}) custom-call(bf16[192,1280]{1,0:T(8,128)(2,1)} %collective-permute-done.6.refs_0_, bf16[192,1280]{1,0:T(8,128)(2,1)} %collective-permute-done.7.refs_1_, bf16[192,1280]{1,0:T(8,128)(2,1)} %collective-permute-done.9.refs_2_, ...), custom_call_target="tpu_custom_call" | custom-call | flops 4404019200 | bytes 13434880 | tf_op jit(solution)/shard_map/pallas_call | solution.py:210
  154.1 3.0 collective-permute-start.42
  157.0 5.4 %shard_map.68 = (f32[320,640]{1,0:T(8,128)}, f32[320,640]{1,0:T(8,128)}, f32[320,640]{1,0:T(8,128)}, f32[320,640]{1,0:T(8,128)}) custom-call(s32[1]{0:T(128)} %bitcast.2.x, f32[1280,640]{1,0:T(8,128)} %bitcast.33, f32[1280,640]{1,0:T(8,128)} %bitcast.6.theirs), custom_call_target="tpu_custom_call" | custom-call | flops 1000000 | bytes 8192000 | tf_op jit(solution)/shard_map/pallas_call | solution.py:108
  167.3 16.4 %collective-permute-done.1 = f32[320,640]{1,0:T(8,128)S(1)} collective-permute-done((f32[320,640]{1,0:T(8,128)}, f32[320,640]{1,0:T(8,128)S(1)}, u32[]{:S(2)}, u32[]{:S(2)}) %collective-permute-start.1) | collective-permute-done | bytes 819232 | tf_op jit(solution)/shard_map/ppermute | solution.py:25
  183.6 18.5 %collective-permute-done.2 = f32[320,640]{1,0:T(8,128)S(1)} collective-permute-done((f32[320,640]{1,0:T(8,128)}, f32[320,640]{1,0:T(8,128)S(1)}, u32[]{:S(2)}, u32[]{:S(2)}) %collective-permute-start.2) | collective-permute-done | bytes 819232 | tf_op jit(solution)/shard_map/ppermute | solution.py:25
  204.4 5.9 %collective-permute-start.35 = (f32[32,320]{1,0:T(8,128)S(1)}, f32[32,320]{1,0:T(8,128)S(1)}, u32[]{:S(2)}, u32[]{:S(2)}) collective-permute-start(f32[32,320]{1,0:T(8,128)S(1)} %get-tuple-element.79), channel_id=1, source_target_pairs={{0,64},{32,96},{64,0},{96,32},{1,65},{33,97},{65,1},{97,33},{2,66}... | collective-permute-start | bytes 122888 | tf_op jit(solution)/shard_map/ppermute | solution.py:25
  213.9 23.0 %collective-permute-done.35 = f32[32,320]{1,0:T(8,128)S(1)} collective-permute-done((f32[32,320]{1,0:T(8,128)S(1)}, f32[32,320]{1,0:T(8,128)S(1)}, u32[]{:S(2)}, u32[]{:S(2)}) %collective-permute-start.35) | collective-permute-done | bytes 40992 | tf_op jit(solution)/shard_map/ppermute | solution.py:25
  236.8 11.4 %collective-permute-done.36 = f32[32,320]{1,0:T(8,128)S(1)} collective-permute-done((f32[32,320]{1,0:T(8,128)S(1)}, f32[32,320]{1,0:T(8,128)S(1)}, u32[]{:S(2)}, u32[]{:S(2)}) %collective-permute-start.36) | collective-permute-done | bytes 40992 | tf_op jit(solution)/shard_map/ppermute | solution.py:25
  249.0 5.0 %shard_map.72 = (f32[320,640]{1,0:T(8,128)}, bf16[320,640]{1,0:T(8,128)(2,1)}, bf16[320,640]{1,0:T(8,128)(2,1)}, bf16[320,640]{1,0:T(8,128)(2,1)}) custom-call(s32[1]{0:T(128)} %bitcast.2.x, f32[1280,640]{1,0:T(8,128)} %get-tuple-element.38.mine, f32[1280,640]{1,0:T(8,128)} %collective-permute-done.42.theirs), custom_call_target="tpu_custom_call" | custom-call | flops 1000000 | bytes 8192000 | tf_op jit(solution)/shard_map/pallas_call | solution.py:108
  254.0 2.8 collective-permute-start.44
  266.4 11.1 %collective-permute-start.55 = (bf16[320,1280]{1,0:T(8,128)(2,1)S(1)}, bf16[320,1280]{1,0:T(8,128)(2,1)S(1)}, u32[]{:S(2)}, u32[]{:S(2)}) collective-permute-start(bf16[320,1280]{1,0:T(8,128)(2,1)S(1)} %get-tuple-element.65), channel_id=1, source_target_pairs={{0,3},{1,0},{2,1},{3,2},{4,7},{5,4},{6,5},{7,6},{8,11},{9,8},{10,9... | collective-permute-start | bytes 2457608 | tf_op jit(solution)/shard_map/ppermute | solution.py:25
  280.5 19.6 %collective-permute-done.40.refs_2_ = f32[32,320]{1,0:T(8,128)S(1)} collective-permute-done((f32[32,320]{1,0:T(8,128)S(1)}, f32[32,320]{1,0:T(8,128)S(1)}, u32[]{:S(2)}, u32[]{:S(2)}) %collective-permute-start.40) | collective-permute-done | bytes 40992 | tf_op jit(solution)/shard_map/ppermute | solution.py:25
  307.0 3.4 collective-permute-start.48
  313.8 3.3 collective-permute-done.49.far
  321.4 6.6 %collective-permute-start.52 = (f32[32,320]{1,0:T(8,128)S(1)}, f32[32,320]{1,0:T(8,128)S(1)}, u32[]{:S(2)}, u32[]{:S(2)}) collective-permute-start(f32[32,320]{1,0:T(8,128)S(1)} %get-tuple-element.46), channel_id=1, source_target_pairs={{0,16},{16,0},{1,17},{17,1},{2,18},{18,2},{3,19},{19,3},{4,20},{20... | collective-permute-start | bytes 122888 | tf_op jit(solution)/shard_map/ppermute | solution.py:25
  362.1 3.5 collective-permute-start.69
  369.0 2.9 copy-done.1
  373.0 6.8 %shard_map.79 = (f32[12800,128]{1,0:T(8,128)}, f32[12800,128]{1,0:T(8,128)}) custom-call(s32[1]{0:T(128)} %bitcast.me, bf16[320,96]{1,0:T(8,128)(2,1)S(1)} %pad_maximum_fusion.1.basis, bf16[96,5120]{1,0:T(8,128)(2,1)S(1)} %get-tuple-element.51.factor, f32[12800,128]{1,0:T(8,128)S(1)} %bitcast.32, bf16[320,1280]{1,0:T(8,128)(2,1)S(1)} %get-tuple-element.52.g0, ...), custom_call_target="tpu_custom_call" | custom-call | flops 314572800 | bytes 22937600 | tf_op jit(solution)/shard_map/pallas_call | solution.py:324
  (198 shorter events, 110.2 us)
Async XLA Ops:
  5.6 16.2 %collective-permute-start.26 = (bf16[192,1280]{1,0:T(8,128)(2,1)}, bf16[192,1280]{1,0:T(8,128)(2,1)}, u32[]{:S(2)}, u32[]{:S(2)}) collective-permute-start(bf16[192,1280]{1,0:T(8,128)(2,1)} %get-tuple-element.69), channel_id=1, source_target_pairs={{0,3},{1,0},{2,1},{3,2},{4,7},{5,4},{6,5},{7,6},{8,11},{9,8},{10,9... | collective-permute-start | bytes 1474568 | tf_op jit(solution)/shard_map/ppermute | solution.py:25
  7.2 16.0 %collective-permute-start.10 = (bf16[192,1280]{1,0:T(8,128)(2,1)S(1)}, bf16[192,1280]{1,0:T(8,128)(2,1)S(1)}, u32[]{:S(2)}, u32[]{:S(2)}) collective-permute-start(bf16[192,1280]{1,0:T(8,128)(2,1)S(1)} %get-tuple-element.76), channel_id=1, source_target_pairs={{0,4},{4,8},{8,12},{12,0},{1,5},{5,9},{9,13},{13,1},{2,6},{6,10},{... | collective-permute-start | bytes 1474568 | tf_op jit(solution)/shard_map/ppermute | solution.py:25
  11.1 21.0 %collective-permute-start.18 = (bf16[192,1280]{1,0:T(8,128)(2,1)S(1)}, bf16[192,1280]{1,0:T(8,128)(2,1)S(1)}, u32[]{:S(2)}, u32[]{:S(2)}) collective-permute-start(bf16[192,1280]{1,0:T(8,128)(2,1)S(1)} %get-tuple-element.70.refs_9_), channel_id=1, source_target_pairs={{0,4},{4,8},{8,12},{12,0},{1,5},{5,9},{9,13},{13,1},{2,6},{6,10},{... | collective-permute-start | bytes 1474568 | tf_op jit(solution)/shard_map/ppermute | solution.py:25
  23.3 21.2 %collective-permute-start.17 = (bf16[192,1280]{1,0:T(8,128)(2,1)S(1)}, bf16[192,1280]{1,0:T(8,128)(2,1)S(1)}, u32[]{:S(2)}, u32[]{:S(2)}) collective-permute-start(bf16[192,1280]{1,0:T(8,128)(2,1)S(1)} %copy-done.10), channel_id=1, source_target_pairs={{0,2},{1,3},{2,0},{3,1},{4,6},{5,7},{6,4},{7,5},{8,10},{9,11},{10,... | collective-permute-start | bytes 1474568 | tf_op jit(solution)/shard_map/ppermute | solution.py:25
  33.2 24.3 %collective-permute-start.24 = (bf16[192,1280]{1,0:T(8,128)(2,1)}, bf16[192,1280]{1,0:T(8,128)(2,1)}, u32[]{:S(2)}, u32[]{:S(2)}) collective-permute-start(bf16[192,1280]{1,0:T(8,128)(2,1)} %collective-permute-done.23.refs_12_), channel_id=1, source_target_pairs={{0,4},{4,8},{8,12},{12,0},{1,5},{5,9},{9,13},{13,1},{2,6},{6,10},{... | collective-permute-start | bytes 1474568 | tf_op jit(solution)/shard_map/ppermute | solution.py:25
  34.0 24.7 %collective-permute-start.27 = (bf16[192,1280]{1,0:T(8,128)(2,1)}, bf16[192,1280]{1,0:T(8,128)(2,1)S(1)}, u32[]{:S(2)}, u32[]{:S(2)}) collective-permute-start(bf16[192,1280]{1,0:T(8,128)(2,1)} %collective-permute-done.26.refs_15_), channel_id=1, source_target_pairs={{0,12},{4,0},{8,4},{12,8},{1,13},{5,1},{9,5},{13,9},{2,14},{6,2},{... | collective-permute-start | bytes 1474568 | tf_op jit(solution)/shard_map/ppermute | solution.py:25
  36.6 28.0 %collective-permute-start.33 = (bf16[192,1280]{1,0:T(8,128)(2,1)}, bf16[192,1280]{1,0:T(8,128)(2,1)S(1)}, u32[]{:S(2)}, u32[]{:S(2)}) collective-permute-start(bf16[192,1280]{1,0:T(8,128)(2,1)} %collective-permute-done.23.refs_12_), channel_id=1, source_target_pairs={{0,12},{4,0},{8,4},{12,8},{1,13},{5,1},{9,5},{13,9},{2,14},{6,2},{... | collective-permute-start | bytes 1474568 | tf_op jit(solution)/shard_map/ppermute | solution.py:25
  44.4 28.7 %collective-permute-start.34 = (bf16[192,1280]{1,0:T(8,128)(2,1)}, bf16[192,1280]{1,0:T(8,128)(2,1)}, u32[]{:S(2)}, u32[]{:S(2)}) collective-permute-start(bf16[192,1280]{1,0:T(8,128)(2,1)} %collective-permute-done.26.refs_15_), channel_id=1, source_target_pairs={{0,4},{4,8},{8,12},{12,0},{1,5},{5,9},{9,13},{13,1},{2,6},{6,10},{... | collective-permute-start | bytes 1474568 | tf_op jit(solution)/shard_map/ppermute | solution.py:25
  45.0 32.6 %collective-permute-start.11 = (bf16[192,1280]{1,0:T(8,128)(2,1)S(1)}, bf16[192,1280]{1,0:T(8,128)(2,1)}, u32[]{:S(2)}, u32[]{:S(2)}) collective-permute-start(bf16[192,1280]{1,0:T(8,128)(2,1)S(1)} %collective-permute-done.10.refs_1_), channel_id=1, source_target_pairs={{0,1},{1,2},{2,3},{3,0},{4,5},{5,6},{6,7},{7,4},{8,9},{9,10},{10,1... | collective-permute-start | bytes 1474568 | tf_op jit(solution)/shard_map/ppermute | solution.py:25
  57.4 22.4 %collective-permute-start.15 = (bf16[192,1280]{1,0:T(8,128)(2,1)S(1)}, bf16[192,1280]{1,0:T(8,128)(2,1)}, u32[]{:S(2)}, u32[]{:S(2)}) collective-permute-start(bf16[192,1280]{1,0:T(8,128)(2,1)S(1)} %collective-permute-done.14.refs_2_), channel_id=1, source_target_pairs={{0,3},{1,0},{2,1},{3,2},{4,7},{5,4},{6,5},{7,6},{8,11},{9,8},{10,9... | collective-permute-start | bytes 1474568 | tf_op jit(solution)/shard_map/ppermute | solution.py:25
  58.7 21.6 %collective-permute-start.29 = (bf16[192,1280]{1,0:T(8,128)(2,1)S(1)}, bf16[192,1280]{1,0:T(8,128)(2,1)}, u32[]{:S(2)}, u32[]{:S(2)}) collective-permute-start(bf16[192,1280]{1,0:T(8,128)(2,1)S(1)} %collective-permute-done.14.refs_2_), channel_id=1, source_target_pairs={{0,1},{1,2},{2,3},{3,0},{4,5},{5,6},{6,7},{7,4},{8,9},{9,10},{10,1... | collective-permute-start | bytes 1474568 | tf_op jit(solution)/shard_map/ppermute | solution.py:25
  73.2 83.9 %collective-permute-start = (f32[4,320,640]{2,1,0:T(8,128)}, f32[4,320,640]{2,1,0:T(8,128)}, u32[]{:S(2)}, u32[]{:S(2)}) collective-permute-start(f32[4,320,640]{2,1,0:T(8,128)} %get-tuple-element.32), channel_id=1, source_target_pairs={{0,16},{16,0},{1,17},{17,1},{2,18},{18,2},{3,19},{19,3},{4,20},{20... | collective-permute-start | bytes 9830408 | tf_op jit(solution)/shard_map/ppermute | solution.py:25
  80.4 24.0 %collective-permute-start.22 = (bf16[192,1280]{1,0:T(8,128)(2,1)S(1)}, bf16[192,1280]{1,0:T(8,128)(2,1)S(1)}, u32[]{:S(2)}, u32[]{:S(2)}) collective-permute-start(bf16[192,1280]{1,0:T(8,128)(2,1)S(1)} %collective-permute-done.17.refs_7_), channel_id=1, source_target_pairs={{0,4},{4,8},{8,12},{12,0},{1,5},{5,9},{9,13},{13,1},{2,6},{6,10},{... | collective-permute-start | bytes 1474568 | tf_op jit(solution)/shard_map/ppermute | solution.py:25
  92.5 21.8 %collective-permute-start.6 = (bf16[192,1280]{1,0:T(8,128)(2,1)}, bf16[192,1280]{1,0:T(8,128)(2,1)}, u32[]{:S(2)}, u32[]{:S(2)}) collective-permute-start(bf16[192,1280]{1,0:T(8,128)(2,1)} %collective-permute-done.5.refs_3_), channel_id=1, source_target_pairs={{0,1},{1,2},{2,3},{3,0},{4,5},{5,6},{6,7},{7,4},{8,9},{9,10},{10,1... | collective-permute-start | bytes 1474568 | tf_op jit(solution)/shard_map/ppermute | solution.py:25
  93.7 20.6 %collective-permute-start.21 = (bf16[192,1280]{1,0:T(8,128)(2,1)S(1)}, bf16[192,1280]{1,0:T(8,128)(2,1)S(1)}, u32[]{:S(2)}, u32[]{:S(2)}) collective-permute-start(bf16[192,1280]{1,0:T(8,128)(2,1)S(1)} %collective-permute-done.20.refs_12_), channel_id=1, source_target_pairs={{0,12},{4,0},{8,4},{12,8},{1,13},{5,1},{9,5},{13,9},{2,14},{6,2},{... | collective-permute-start | bytes 1474568 | tf_op jit(solution)/shard_map/ppermute | solution.py:25
  105.1 24.2 %collective-permute-start.28 = (bf16[192,1280]{1,0:T(8,128)(2,1)}, bf16[192,1280]{1,0:T(8,128)(2,1)S(1)}, u32[]{:S(2)}, u32[]{:S(2)}) collective-permute-start(bf16[192,1280]{1,0:T(8,128)(2,1)} %copy-done.18), channel_id=1, source_target_pairs={{0,12},{4,0},{8,4},{12,8},{1,13},{5,1},{9,5},{13,9},{2,14},{6,2},{... | collective-permute-start | bytes 1474568 | tf_op jit(solution)/shard_map/ppermute | solution.py:25
  114.3 15.1 %collective-permute-start.12 = (bf16[192,1280]{1,0:T(8,128)(2,1)}, bf16[192,1280]{1,0:T(8,128)(2,1)}, u32[]{:S(2)}, u32[]{:S(2)}) collective-permute-start(bf16[192,1280]{1,0:T(8,128)(2,1)} %collective-permute-done.11.refs_4_), channel_id=1, source_target_pairs={{0,1},{1,2},{2,3},{3,0},{4,5},{5,6},{6,7},{7,4},{8,9},{9,10},{10,1... | collective-permute-start | bytes 1474568 | tf_op jit(solution)/shard_map/ppermute | solution.py:25
  117.1 19.2 %collective-permute-start.9 = (bf16[192,1280]{1,0:T(8,128)(2,1)}, bf16[192,1280]{1,0:T(8,128)(2,1)}, u32[]{:S(2)}, u32[]{:S(2)}) collective-permute-start(bf16[192,1280]{1,0:T(8,128)(2,1)} %copy-done.21), channel_id=1, source_target_pairs={{0,3},{1,0},{2,1},{3,2},{4,7},{5,4},{6,5},{7,6},{8,11},{9,8},{10,9... | collective-permute-start | bytes 1474568 | tf_op jit(solution)/shard_map/ppermute | solution.py:25
  154.1 95.0 %collective-permute-start.42 = (f32[1280,640]{1,0:T(8,128)}, f32[1280,640]{1,0:T(8,128)}, u32[]{:S(2)}, u32[]{:S(2)}) collective-permute-start(f32[1280,640]{1,0:T(8,128)} %get-tuple-element.39), channel_id=1, source_target_pairs={{0,16},{16,0},{1,17},{17,1},{2,18},{18,2},{3,19},{19,3},{4,20},{20... | collective-permute-start | bytes 9830408 | tf_op jit(solution)/shard_map/ppermute | solution.py:25
  162.5 21.2 %collective-permute-start.1 = (f32[320,640]{1,0:T(8,128)}, f32[320,640]{1,0:T(8,128)S(1)}, u32[]{:S(2)}, u32[]{:S(2)}) collective-permute-start(f32[320,640]{1,0:T(8,128)} %get-tuple-element.34), channel_id=1, source_target_pairs={{0,32},{32,64},{64,96},{96,0},{1,33},{33,65},{65,97},{97,1},{2,34}... | collective-permute-start | bytes 2457608 | tf_op jit(solution)/shard_map/ppermute | solution.py:25
  163.7 38.5 %collective-permute-start.2 = (f32[320,640]{1,0:T(8,128)}, f32[320,640]{1,0:T(8,128)S(1)}, u32[]{:S(2)}, u32[]{:S(2)}) collective-permute-start(f32[320,640]{1,0:T(8,128)} %get-tuple-element.35), channel_id=1, source_target_pairs={{0,64},{32,96},{64,0},{96,32},{1,65},{33,97},{65,1},{97,33},{2,66}... | collective-permute-start | bytes 2457608 | tf_op jit(solution)/shard_map/ppermute | solution.py:25
  166.1 36.1 %collective-permute-start.3 = (f32[320,640]{1,0:T(8,128)}, f32[320,640]{1,0:T(8,128)S(1)}, u32[]{:S(2)}, u32[]{:S(2)}) collective-permute-start(f32[320,640]{1,0:T(8,128)} %get-tuple-element.36), channel_id=1, source_target_pairs={{0,96},{32,0},{64,32},{96,64},{1,97},{33,1},{65,33},{97,65},{2,98}... | collective-permute-start | bytes 2457608 | tf_op jit(solution)/shard_map/ppermute | solution.py:25
  204.4 32.5 %collective-permute-start.35 = (f32[32,320]{1,0:T(8,128)S(1)}, f32[32,320]{1,0:T(8,128)S(1)}, u32[]{:S(2)}, u32[]{:S(2)}) collective-permute-start(f32[32,320]{1,0:T(8,128)S(1)} %get-tuple-element.79), channel_id=1, source_target_pairs={{0,64},{32,96},{64,0},{96,32},{1,65},{33,97},{65,1},{97,33},{2,66}... | collective-permute-start | bytes 122888 | tf_op jit(solution)/shard_map/ppermute | solution.py:25
  210.3 38.0 %collective-permute-start.36 = (f32[32,320]{1,0:T(8,128)S(1)}, f32[32,320]{1,0:T(8,128)S(1)}, u32[]{:S(2)}, u32[]{:S(2)}) collective-permute-start(f32[32,320]{1,0:T(8,128)S(1)} %get-tuple-element.81), channel_id=1, source_target_pairs={{0,32},{32,64},{64,96},{96,0},{1,33},{33,65},{65,97},{97,1},{2,34}... | collective-permute-start | bytes 122888 | tf_op jit(solution)/shard_map/ppermute | solution.py:25
  212.0 36.2 %collective-permute-start.37 = (f32[32,320]{1,0:T(8,128)S(1)}, f32[32,320]{1,0:T(8,128)S(1)}, u32[]{:S(2)}, u32[]{:S(2)}) collective-permute-start(f32[32,320]{1,0:T(8,128)S(1)} %get-tuple-element.80), channel_id=1, source_target_pairs={{0,96},{32,0},{64,32},{96,64},{1,97},{33,1},{65,33},{97,65},{2,98}... | collective-permute-start | bytes 122888 | tf_op jit(solution)/shard_map/ppermute | solution.py:25
  254.0 23.5 %collective-permute-start.44 = (bf16[320,640]{1,0:T(8,128)(2,1)}, bf16[320,640]{1,0:T(8,128)(2,1)S(1)}, u32[]{:S(2)}, u32[]{:S(2)}) collective-permute-start(bf16[320,640]{1,0:T(8,128)(2,1)} %get-tuple-element.42), channel_id=1, source_target_pairs={{0,64},{32,96},{64,0},{96,32},{1,65},{33,97},{65,1},{97,33},{2,66}... | collective-permute-start | bytes 1228808 | tf_op jit(solution)/shard_map/ppermute | solution.py:25
  256.8 20.7 %collective-permute-start.45 = (bf16[320,640]{1,0:T(8,128)(2,1)}, bf16[320,640]{1,0:T(8,128)(2,1)S(1)}, u32[]{:S(2)}, u32[]{:S(2)}) collective-permute-start(bf16[320,640]{1,0:T(8,128)(2,1)} %get-tuple-element.43), channel_id=1, source_target_pairs={{0,96},{32,0},{64,32},{96,64},{1,97},{33,1},{65,33},{97,65},{2,98}... | collective-permute-start | bytes 1228808 | tf_op jit(solution)/shard_map/ppermute | solution.py:25
  261.5 67.3 %collective-permute-start.53 = (bf16[320,1280]{1,0:T(8,128)(2,1)S(1)}, bf16[320,1280]{1,0:T(8,128)(2,1)S(1)}, u32[]{:S(2)}, u32[]{:S(2)}) collective-permute-start(bf16[320,1280]{1,0:T(8,128)(2,1)S(1)} %get-tuple-element.67), channel_id=1, source_target_pairs={{0,1},{1,2},{2,3},{3,0},{4,5},{5,6},{6,7},{7,4},{8,9},{9,10},{10,1... | collective-permute-start | bytes 2457608 | tf_op jit(solution)/shard_map/ppermute | solution.py:25
  262.0 66.9 %collective-permute-start.54 = (bf16[320,1280]{1,0:T(8,128)(2,1)S(1)}, bf16[320,1280]{1,0:T(8,128)(2,1)S(1)}, u32[]{:S(2)}, u32[]{:S(2)}) collective-permute-start(bf16[320,1280]{1,0:T(8,128)(2,1)S(1)} %get-tuple-element.66), channel_id=1, source_target_pairs={{0,2},{1,3},{2,0},{3,1},{4,6},{5,7},{6,4},{7,5},{8,10},{9,11},{10,... | collective-permute-start | bytes 2457608 | tf_op jit(solution)/shard_map/ppermute | solution.py:25
  266.4 62.5 %collective-permute-start.55 = (bf16[320,1280]{1,0:T(8,128)(2,1)S(1)}, bf16[320,1280]{1,0:T(8,128)(2,1)S(1)}, u32[]{:S(2)}, u32[]{:S(2)}) collective-permute-start(bf16[320,1280]{1,0:T(8,128)(2,1)S(1)} %get-tuple-element.65), channel_id=1, source_target_pairs={{0,3},{1,0},{2,1},{3,2},{4,7},{5,4},{6,5},{7,6},{8,11},{9,8},{10,9... | collective-permute-start | bytes 2457608 | tf_op jit(solution)/shard_map/ppermute | solution.py:25
  277.5 22.5 %collective-permute-start.40 = (f32[32,320]{1,0:T(8,128)S(1)}, f32[32,320]{1,0:T(8,128)S(1)}, u32[]{:S(2)}, u32[]{:S(2)}) collective-permute-start(f32[32,320]{1,0:T(8,128)S(1)} %add_multiply_fusion.1.refs_0_), channel_id=1, source_target_pairs={{0,1},{1,2},{2,3},{3,0},{4,5},{5,6},{6,7},{7,4},{8,9},{9,10},{10,1... | collective-permute-start | bytes 122888 | tf_op jit(solution)/shard_map/ppermute | solution.py:25
  277.5 23.6 %collective-permute-start.41 = (f32[32,320]{1,0:T(8,128)S(1)}, f32[32,320]{1,0:T(8,128)S(1)}, u32[]{:S(2)}, u32[]{:S(2)}) collective-permute-start(f32[32,320]{1,0:T(8,128)S(1)} %add_multiply_fusion.1.refs_0_), channel_id=1, source_target_pairs={{0,3},{1,0},{2,1},{3,2},{4,7},{5,4},{6,5},{7,6},{8,11},{9,8},{10,9... | collective-permute-start | bytes 122888 | tf_op jit(solution)/shard_map/ppermute | solution.py:25
  (65 other events, 1062.4 us)

commit v5 on v4

--- a/solution.py
+++ b/solution.py
@@ -190,10 +190,10 @@
         other[...] = jnp.where(first, high, low)
 
     block_rows(n, refs, sa, sg, sems, start.shape[0], store)
-    first = core[0] == 0
-    low, high = right[:, :half], right[:, half:]
-    total = dot(jnp.where(first, low, high), mine[...], ((1,), (1,)))
-    left[...] = total + dot(jnp.where(first, high, low), other[...], ((1,), (1,)))
+    dims = (((1,), (1,)), ((), ()))
+    both = lax.dot_general(right[...], rounded[...], dims, preferred_element_type=F32)
+    rank = left.shape[0]
+    left[...] = both[:rank] + both[rank:]
 
 
 def block_spec(v):
@@ -286,6 +286,10 @@
 
 def ring(v, axis):
     return v, shift(v, axis, 2), shift(v, axis, 1), shift(v, axis, -1)
+
+
+def after(v, token):
+    return lax.optimization_barrier((v, token))[0]
 
 
 def final_kernel(me, basis, factor, err, g0, g1, g2, g3, update, error_next):
@@ -388,19 +392,22 @@
     block = pl.BlockSpec((HEIGHT, side), lambda i: (i, 0))
     near = block_call(near_kernel, seen, a_all, g_all, [], [], whole)
     right = lax.dynamic_slice_in_dim(q_start[0], y * side, side, 1)
-    start_spec = pl.BlockSpec(right.shape, lambda i: (0, 0))
+    right_hi = lax.reduce_precision(right, 8, 7)
+    two = jnp.concatenate([right_hi, right - right_hi], axis=0).astype(BF)
+    start_spec = pl.BlockSpec(two.shape, lambda i: (0, 0))
     rounded, mine, other, partial = block_call(
-        rest_kernel, rest, a_all, g_all, [core_ref, near, right], [smem, block, start_spec],
+        rest_kernel, rest, a_all, g_all, [core_ref, near, two], [smem, block, start_spec],
         (jax.ShapeDtypeStruct((side, side), BF), part, part, jax.ShapeDtypeStruct(right.shape, F32)),
     )
     theirs = shift(other, "c", 1)
     terms = spread(partial, "x", 1, own_rows)
+    parts = fold(x, mine, theirs, BF)
+    terms, right = after((terms, right), parts[0])
     right = lax.dynamic_slice_in_dim(right, core * half, half, 1)
     partial = small_call(left_kernel, jax.ShapeDtypeStruct((rank, own_rows), F32), (right, mean))
     partial = (partial + (terms[0] + terms[2])) + (terms[1] + terms[3])
     partial = (partial + shift(partial, "c", 1)) / groups
     first = (partial, shift(partial, "y", 2), shift(partial, "y", 1), shift(partial, "y", -1))
-    parts = fold(x, mine, theirs, BF)
     pieces = [lax.dynamic_slice_in_dim(rounded, lax.rem(y + k, 4) * own_rows, own_rows, 0) for k in range(4)]
     pieces = pieces[:1] + [shift(pieces[k], "y", k) for k in (1, 2, 3)]
     mean = ((mean + parts[0]) + (parts[1].astype(F32) + parts[2].astype(F32)) + parts[3].astype(F32)) / groups
@@ -413,7 +420,6 @@
             terms = (*first, mean)
         else:
             partial = partial + shift(partial, "c", 1)
-            partial, pieces = lax.optimization_barrier((partial, pieces))
             terms = (inverse_factor(gram), *ring(partial, "y"), mean)
         left, both = small_call(functools.partial(right_kernel, step > 0), (left_shape, right_shape), terms)
         own, far, below, above = ring(both, "z")

time: 380 us -> 368 us (0.968)
  starting transfers between devices: 111 us -> 91.5 us
  local copies, waits for them, and re-layouts: 12 us -> 17.5 us
  Pallas kernels: 65.4 us -> 61.2 us
    ppermute x68, starting transfers between devices: 110 us -> 90.2 us  [shift(): return lax.ppermute(v, axis, [(i, (i + by) % n) for i in range(n)])]
    pallas_call x2, Pallas kernels: 29.8 us -> 25.5 us  [block_call(): pl.pallas_call(functools.partial(kernel, n), grid=(side // HEIGHT,), out_...]
    unnamed x54 -> x52, local copies, waits for them, and re-layouts: 4.95 us -> 9 us
  transfers between devices with their start and end apart: 70 -> 70, of which waited for: 32 -> 31; matrix products, arithmetic and copies ran while one was open for 2% -> 4% of each run, Pallas kernels for 15% -> 14%
where the time goes in v5:
time: 368 us; the launch traced here: 367 us
  waiting for transfers between devices  189 us (51%)
  starting transfers between devices  91.5 us (25%)
  Pallas kernels  61.2 us (17%)
  local copies, waits for them, and re-layouts  17.5 us (5%)
  other arithmetic  6.63 us (2%)
    ppermute x68, waiting for transfers between devices, shift(): return lax.ppermute(v, axis, [(i, (i + by) % n) for i in range(n)])  189 us
    ppermute x68, starting transfers between devices, shift(): return lax.ppermute(v, axis, [(i, (i + by) % n) for i in range(n)])  90.2 us
    pallas_call x2, Pallas kernels, block_call(): pl.pallas_call(functools.partial(kernel, n), grid=(side // HEIGHT,), out_...  25.5 us
    pallas_call x7, Pallas kernels, small_call(): pl.pallas_call(kernel, out_shape=shapes, in_specs=[pl.BlockSpec(memory_sp...  10.7 us
    pallas_call x2, Pallas kernels, fold(): pl.pallas_call(fold_kernel, out_shape=(jax.ShapeDtypeStruct((rows, width)...  10.4 us
    unnamed x52, local copies, waits for them, and re-layouts  9 us
    pallas_call x1, Pallas kernels, split_error(): pl.pallas_call(split_kernel, out_shape=(shape, shape), grid_spec=pltpu.Pr...  7.79 us
  transfers between devices with their start and end apart: 70, of which 31 were waited for; matrix products, arithmetic and copies ran while one was open for 4% of the time, Pallas kernels for 14%

profile of v5, /device:TPU:1, one launch (start us, length us, event | category | flops | bytes accessed | tf_op | source)
XLA Modules:
  0.0 367.4 jit_solution(8678835038645066818)
XLA Ops:
  7.0 3.8 %collective-permute-start.9 = (bf16[192,1280]{1,0:T(8,128)(2,1)S(1)}, bf16[192,1280]{1,0:T(8,128)(2,1)S(1)}, u32[]{:S(2)}, u32[]{:S(2)}) collective-permute-start(bf16[192,1280]{1,0:T(8,128)(2,1)S(1)} %get-tuple-element.75), channel_id=1, source_target_pairs={{0,12},{4,0},{8,4},{12,8},{1,13},{5,1},{9,5},{13,9},{2,14},{6,2},{... | collective-permute-start | bytes 1474568 | tf_op jit(solution)/shard_map/ppermute | solution.py:25
  10.8 7.1 %collective-permute-done.18.refs_12_ = bf16[192,1280]{1,0:T(8,128)(2,1)} collective-permute-done((bf16[192,1280]{1,0:T(8,128)(2,1)}, bf16[192,1280]{1,0:T(8,128)(2,1)}, u32[]{:S(2)}, u32[]{:S(2)}) %collective-permute-start.18) | collective-permute-done | bytes 491552 | tf_op jit(solution)/shard_map/ppermute | solution.py:25
  17.9 3.6 collective-permute-start.27
  24.9 9.1 %collective-permute-done.13.refs_10_ = bf16[192,1280]{1,0:T(8,128)(2,1)} collective-permute-done((bf16[192,1280]{1,0:T(8,128)(2,1)S(1)}, bf16[192,1280]{1,0:T(8,128)(2,1)}, u32[]{:S(2)}, u32[]{:S(2)}) %collective-permute-start.13) | collective-permute-done | bytes 491552 | tf_op jit(solution)/shard_map/ppermute | solution.py:25
  37.4 6.9 %collective-permute-done.12.refs_7_ = bf16[192,1280]{1,0:T(8,128)(2,1)} collective-permute-done((bf16[192,1280]{1,0:T(8,128)(2,1)S(1)}, bf16[192,1280]{1,0:T(8,128)(2,1)}, u32[]{:S(2)}, u32[]{:S(2)}) %collective-permute-start.12) | collective-permute-done | bytes 491552 | tf_op jit(solution)/shard_map/ppermute | solution.py:25
  47.5 11.7 %collective-permute-done.19.refs_13_ = bf16[192,1280]{1,0:T(8,128)(2,1)S(1)} collective-permute-done((bf16[192,1280]{1,0:T(8,128)(2,1)}, bf16[192,1280]{1,0:T(8,128)(2,1)S(1)}, u32[]{:S(2)}, u32[]{:S(2)}) %collective-permute-start.19) | collective-permute-done | bytes 491552 | tf_op jit(solution)/shard_map/ppermute | solution.py:25
  61.8 3.7 %collective-permute-done.28.refs_14_ = bf16[192,1280]{1,0:T(8,128)(2,1)S(1)} collective-permute-done((bf16[192,1280]{1,0:T(8,128)(2,1)}, bf16[192,1280]{1,0:T(8,128)(2,1)S(1)}, u32[]{:S(2)}, u32[]{:S(2)}) %collective-permute-start.28) | collective-permute-done | bytes 491552 | tf_op jit(solution)/shard_map/ppermute | solution.py:25
  65.5 4.1 %collective-permute-done.29.refs_16_ = bf16[192,1280]{1,0:T(8,128)(2,1)S(1)} collective-permute-done((bf16[192,1280]{1,0:T(8,128)(2,1)}, bf16[192,1280]{1,0:T(8,128)(2,1)S(1)}, u32[]{:S(2)}, u32[]{:S(2)}) %collective-permute-start.29) | collective-permute-done | bytes 491552 | tf_op jit(solution)/shard_map/ppermute | solution.py:25
  74.2 7.8 %shard_map.70 = (f32[4,320,640]{2,1,0:T(8,128)}, f32[4,320,640]{2,1,0:T(8,128)}) custom-call(s32[1]{0:T(128)} %bitcast.9.refs_14_.core, f32[12800,128]{1,0:T(8,128)} %bitcast.30), custom_call_target="tpu_custom_call" | custom-call | flops 1000000 | bytes 13107200 | tf_op jit(solution)/shard_map/pallas_call | solution.py:74
  86.4 3.0 collective-permute-start.16
  89.4 5.5 %collective-permute-done.17.refs_10_ = bf16[192,1280]{1,0:T(8,128)(2,1)} collective-permute-done((bf16[192,1280]{1,0:T(8,128)(2,1)}, bf16[192,1280]{1,0:T(8,128)(2,1)}, u32[]{:S(2)}, u32[]{:S(2)}) %collective-permute-start.17) | collective-permute-done | bytes 491552 | tf_op jit(solution)/shard_map/ppermute | solution.py:25
  95.6 15.4 %collective-permute-done.1.refs_0_ = bf16[192,1280]{1,0:T(8,128)(2,1)S(1)} collective-permute-done((bf16[192,1280]{1,0:T(8,128)(2,1)}, bf16[192,1280]{1,0:T(8,128)(2,1)S(1)}, u32[]{:S(2)}, u32[]{:S(2)}) %collective-permute-start.1) | collective-permute-done | bytes 491552 | tf_op jit(solution)/shard_map/ppermute | solution.py:25
  117.0 11.9 %shard_map.67.refs_15_ = f32[1280,1280]{1,0:T(8,128)} custom-call(bf16[192,1280]{1,0:T(8,128)(2,1)} %copy-done.4, bf16[192,1280]{1,0:T(8,128)(2,1)} %copy-done.8, bf16[192,1280]{1,0:T(8,128)(2,1)} %copy-done.7, bf16[192,1280]{1,0:T(8,128)(2,1)} %copy-done.10, bf16[192,1280]{1,0:T(8,128)(2,1)} %copy-done.19, bf16[192,1280]{1,0:T(8,128)(2,1)} %copy-done.18, ...), custom_call_target="tpu_custom_call" | custom-call | flops 5662310400 | bytes 15400960 | tf_op jit(solution)/shard_map/pallas_call | solution.py:210
  128.9 7.5 %collective-permute-done.4.refs_2_ = bf16[192,1280]{1,0:T(8,128)(2,1)} collective-permute-done((bf16[192,1280]{1,0:T(8,128)(2,1)}, bf16[192,1280]{1,0:T(8,128)(2,1)}, u32[]{:S(2)}, u32[]{:S(2)}) %collective-permute-start.4) | collective-permute-done | bytes 491552 | tf_op jit(solution)/shard_map/ppermute | solution.py:25
  137.2 13.6 %shard_map.68 = (bf16[1280,1280]{1,0:T(8,128)(2,1)}, f32[1280,640]{1,0:T(8,128)}, f32[1280,640]{1,0:T(8,128)}, f32[32,1280]{1,0:T(8,128)}) custom-call(bf16[192,1280]{1,0:T(8,128)(2,1)} %copy-done.22, bf16[192,1280]{1,0:T(8,128)(2,1)} %collective-permute-done.2.refs_1_, bf16[192,1280]{1,0:T(8,128)(2,1)} %collective-permute-done.4.refs_2_, ...), custom_call_target="tpu_custom_call" | custom-call | flops 4404019200 | bytes 13434880 | tf_op jit(solution)/shard_map/pallas_call | solution.py:210
  154.7 5.4 %shard_map.71 = (f32[320,640]{1,0:T(8,128)}, f32[320,640]{1,0:T(8,128)}, f32[320,640]{1,0:T(8,128)}, f32[320,640]{1,0:T(8,128)}) custom-call(s32[1]{0:T(128)} %bitcast.11.x, f32[1280,640]{1,0:T(8,128)} %bitcast.32, f32[1280,640]{1,0:T(8,128)} %bitcast.33), custom_call_target="tpu_custom_call" | custom-call | flops 1000000 | bytes 8192000 | tf_op jit(solution)/shard_map/pallas_call | solution.py:108
  164.9 16.4 %collective-permute-done.35 = f32[320,640]{1,0:T(8,128)S(1)} collective-permute-done((f32[320,640]{1,0:T(8,128)}, f32[320,640]{1,0:T(8,128)S(1)}, u32[]{:S(2)}, u32[]{:S(2)}) %collective-permute-start.35) | collective-permute-done | bytes 819232 | tf_op jit(solution)/shard_map/ppermute | solution.py:25
  181.3 18.5 %collective-permute-done.36 = f32[320,640]{1,0:T(8,128)S(1)} collective-permute-done((f32[320,640]{1,0:T(8,128)}, f32[320,640]{1,0:T(8,128)S(1)}, u32[]{:S(2)}, u32[]{:S(2)}) %collective-permute-start.36) | collective-permute-done | bytes 819232 | tf_op jit(solution)/shard_map/ppermute | solution.py:25
  204.1 4.3 %collective-permute-start.31 = (f32[32,320]{1,0:T(8,128)S(1)}, f32[32,320]{1,0:T(8,128)S(1)}, u32[]{:S(2)}, u32[]{:S(2)}) collective-permute-start(f32[32,320]{1,0:T(8,128)S(1)} %get-tuple-element.82), channel_id=1, source_target_pairs={{0,64},{32,96},{64,0},{96,32},{1,65},{33,97},{65,1},{97,33},{2,66}... | collective-permute-start | bytes 122888 | tf_op jit(solution)/shard_map/ppermute | solution.py:25
  208.4 5.0 %shard_map.69 = (f32[320,640]{1,0:T(8,128)}, bf16[320,640]{1,0:T(8,128)(2,1)}, bf16[320,640]{1,0:T(8,128)(2,1)}, bf16[320,640]{1,0:T(8,128)(2,1)}) custom-call(s32[1]{0:T(128)} %bitcast.11.x, f32[1280,640]{1,0:T(8,128)} %get-tuple-element.32.mine, f32[1280,640]{1,0:T(8,128)} %collective-permute-done.33.theirs), custom_call_target="tpu_custom_call" | custom-call | flops 1000000 | bytes 8192000 | tf_op jit(solution)/shard_map/pallas_call | solution.py:108
  214.8 29.2 %collective-permute-done.30 = f32[32,320]{1,0:T(8,128)S(1)} collective-permute-done((f32[32,320]{1,0:T(8,128)S(1)}, f32[32,320]{1,0:T(8,128)S(1)}, u32[]{:S(2)}, u32[]{:S(2)}) %collective-permute-start.30) | collective-permute-done | bytes 40992 | tf_op jit(solution)/shard_map/ppermute | solution.py:25
  246.6 3.6 collective-permute-start.40
  250.2 3.4 collective-permute-start.41
  253.6 8.0 %collective-permute-done.43 = bf16[320,640]{1,0:T(8,128)(2,1)S(1)} collective-permute-done((bf16[320,640]{1,0:T(8,128)(2,1)}, bf16[320,640]{1,0:T(8,128)(2,1)S(1)}, u32[]{:S(2)}, u32[]{:S(2)}) %collective-permute-start.43) | collective-permute-done | bytes 409632 | tf_op jit(solution)/shard_map/ppermute | solution.py:25
  271.3 4.7 %collective-permute-start.50 = (f32[32,768]{1,0:T(8,128)S(1)}, f32[32,768]{1,0:T(8,128)S(1)}, u32[]{:S(2)}, u32[]{:S(2)}) collective-permute-start(f32[32,768]{1,0:T(8,128)S(1)} %add_add_fusion.3.own), channel_id=1, source_target_pairs={{0,32},{32,64},{64,96},{96,0},{1,33},{33,65},{65,97},{97,1},{2,34}... | collective-permute-start | bytes 294920 | tf_op jit(solution)/shard_map/ppermute | solution.py:25
  277.7 3.0 collective-permute-done.51.above
  302.0 3.4 constant_dynamic-slice_fusion
  309.6 3.3 collective-permute-start.63
  315.7 3.6 collective-permute-start.64
  319.2 23.1 %collective-permute-done.63 = f32[32,640]{1,0:T(8,128)S(1)} collective-permute-done((f32[32,640]{1,0:T(8,128)}, f32[32,640]{1,0:T(8,128)S(1)}, u32[]{:S(2)}, u32[]{:S(2)}) %collective-permute-start.63) | collective-permute-done | bytes 81952 | tf_op jit(solution)/shard_map/ppermute | solution.py:25
  348.6 5.7 %collective-permute-start.66 = (f32[128,640]{1,0:T(8,128)S(1)}, f32[128,640]{1,0:T(8,128)S(1)}, u32[]{:S(2)}, u32[]{:S(2)}) collective-permute-start(f32[128,640]{1,0:T(8,128)S(1)} %pad_maximum_fusion.mine), channel_id=1, source_target_pairs={{0,16},{16,0},{1,17},{17,1},{2,18},{18,2},{3,19},{19,3},{4,20},{20... | collective-permute-start | bytes 983048 | tf_op jit(solution)/shard_map/ppermute | solution.py:25
  360.6 6.8 %shard_map.79 = (f32[12800,128]{1,0:T(8,128)}, f32[12800,128]{1,0:T(8,128)}) custom-call(s32[1]{0:T(128)} %bitcast.me, bf16[320,96]{1,0:T(8,128)(2,1)S(1)} %pad_maximum_fusion.2.basis, bf16[96,5120]{1,0:T(8,128)(2,1)S(1)} %get-tuple-element.54.factor, f32[12800,128]{1,0:T(8,128)S(1)} %bitcast.31, bf16[320,1280]{1,0:T(8,128)(2,1)S(1)} %get-tuple-element.70.g0, ...), custom_call_target="tpu_custom_call" | custom-call | flops 314572800 | bytes 22937600 | tf_op jit(solution)/shard_map/pallas_call | solution.py:328
  (198 shorter events, 104.1 us)
Async XLA Ops:
  10.8 23.2 %collective-permute-start.13 = (bf16[192,1280]{1,0:T(8,128)(2,1)S(1)}, bf16[192,1280]{1,0:T(8,128)(2,1)}, u32[]{:S(2)}, u32[]{:S(2)}) collective-permute-start(bf16[192,1280]{1,0:T(8,128)(2,1)S(1)} %get-tuple-element.72.refs_9_), channel_id=1, source_target_pairs={{0,4},{4,8},{8,12},{12,0},{1,5},{5,9},{9,13},{13,1},{2,6},{6,10},{... | collective-permute-start | bytes 1474568 | tf_op jit(solution)/shard_map/ppermute | solution.py:25
  24.2 20.1 %collective-permute-start.12 = (bf16[192,1280]{1,0:T(8,128)(2,1)S(1)}, bf16[192,1280]{1,0:T(8,128)(2,1)}, u32[]{:S(2)}, u32[]{:S(2)}) collective-permute-start(bf16[192,1280]{1,0:T(8,128)(2,1)S(1)} %get-tuple-element.73), channel_id=1, source_target_pairs={{0,2},{1,3},{2,0},{3,1},{4,6},{5,7},{6,4},{7,5},{8,10},{9,11},{10,... | collective-permute-start | bytes 1474568 | tf_op jit(solution)/shard_map/ppermute | solution.py:25
  34.0 25.2 %collective-permute-start.19 = (bf16[192,1280]{1,0:T(8,128)(2,1)}, bf16[192,1280]{1,0:T(8,128)(2,1)S(1)}, u32[]{:S(2)}, u32[]{:S(2)}) collective-permute-start(bf16[192,1280]{1,0:T(8,128)(2,1)} %collective-permute-done.18.refs_12_), channel_id=1, source_target_pairs={{0,4},{4,8},{8,12},{12,0},{1,5},{5,9},{9,13},{13,1},{2,6},{6,10},{... | collective-permute-start | bytes 1474568 | tf_op jit(solution)/shard_map/ppermute | solution.py:25
  34.1 25.1 %collective-permute-start.22 = (bf16[192,1280]{1,0:T(8,128)(2,1)}, bf16[192,1280]{1,0:T(8,128)(2,1)S(1)}, u32[]{:S(2)}, u32[]{:S(2)}) collective-permute-start(bf16[192,1280]{1,0:T(8,128)(2,1)} %collective-permute-done.21.refs_15_), channel_id=1, source_target_pairs={{0,12},{4,0},{8,4},{12,8},{1,13},{5,1},{9,5},{13,9},{2,14},{6,2},{... | collective-permute-start | bytes 1474568 | tf_op jit(solution)/shard_map/ppermute | solution.py:25
  36.7 28.8 %collective-permute-start.28 = (bf16[192,1280]{1,0:T(8,128)(2,1)}, bf16[192,1280]{1,0:T(8,128)(2,1)S(1)}, u32[]{:S(2)}, u32[]{:S(2)}) collective-permute-start(bf16[192,1280]{1,0:T(8,128)(2,1)} %collective-permute-done.18.refs_12_), channel_id=1, source_target_pairs={{0,12},{4,0},{8,4},{12,8},{1,13},{5,1},{9,5},{13,9},{2,14},{6,2},{... | collective-permute-start | bytes 1474568 | tf_op jit(solution)/shard_map/ppermute | solution.py:25
  44.3 25.4 %collective-permute-start.29 = (bf16[192,1280]{1,0:T(8,128)(2,1)}, bf16[192,1280]{1,0:T(8,128)(2,1)S(1)}, u32[]{:S(2)}, u32[]{:S(2)}) collective-permute-start(bf16[192,1280]{1,0:T(8,128)(2,1)} %collective-permute-done.21.refs_15_), channel_id=1, source_target_pairs={{0,4},{4,8},{8,12},{12,0},{1,5},{5,9},{9,13},{13,1},{2,6},{6,10},{... | collective-permute-start | bytes 1474568 | tf_op jit(solution)/shard_map/ppermute | solution.py:25
  46.1 23.6 %collective-permute-start.10 = (bf16[192,1280]{1,0:T(8,128)(2,1)S(1)}, bf16[192,1280]{1,0:T(8,128)(2,1)S(1)}, u32[]{:S(2)}, u32[]{:S(2)}) collective-permute-start(bf16[192,1280]{1,0:T(8,128)(2,1)S(1)} %collective-permute-done.9.refs_2_), channel_id=1, source_target_pairs={{0,3},{1,0},{2,1},{3,2},{4,7},{5,4},{6,5},{7,6},{8,11},{9,8},{10,9... | collective-permute-start | bytes 1474568 | tf_op jit(solution)/shard_map/ppermute | solution.py:25
  65.5 17.7 %collective-permute-start.6 = (bf16[192,1280]{1,0:T(8,128)(2,1)S(1)}, bf16[192,1280]{1,0:T(8,128)(2,1)S(1)}, u32[]{:S(2)}, u32[]{:S(2)}) collective-permute-start(bf16[192,1280]{1,0:T(8,128)(2,1)S(1)} %collective-permute-done.5.refs_1_), channel_id=1, source_target_pairs={{0,1},{1,2},{2,3},{3,0},{4,5},{5,6},{6,7},{7,4},{8,9},{9,10},{10,1... | collective-permute-start | bytes 1474568 | tf_op jit(solution)/shard_map/ppermute | solution.py:25
  74.2 20.7 %collective-permute-start.17 = (bf16[192,1280]{1,0:T(8,128)(2,1)}, bf16[192,1280]{1,0:T(8,128)(2,1)}, u32[]{:S(2)}, u32[]{:S(2)}) collective-permute-start(bf16[192,1280]{1,0:T(8,128)(2,1)} %collective-permute-done.12.refs_7_), channel_id=1, source_target_pairs={{0,4},{4,8},{8,12},{12,0},{1,5},{5,9},{9,13},{13,1},{2,6},{6,10},{... | collective-permute-start | bytes 1474568 | tf_op jit(solution)/shard_map/ppermute | solution.py:25
  84.0 69.0 %collective-permute-start.34 = (f32[4,320,640]{2,1,0:T(8,128)}, f32[4,320,640]{2,1,0:T(8,128)S(1)}, u32[]{:S(2)}, u32[]{:S(2)}) collective-permute-start(f32[4,320,640]{2,1,0:T(8,128)} %get-tuple-element.37), channel_id=1, source_target_pairs={{0,16},{16,0},{1,17},{17,1},{2,18},{18,2},{3,19},{19,3},{4,20},{20... | collective-permute-start | bytes 9830408 | tf_op jit(solution)/shard_map/ppermute | solution.py:25
  86.2 27.7 %collective-permute-start.8 = (bf16[192,1280]{1,0:T(8,128)(2,1)}, bf16[192,1280]{1,0:T(8,128)(2,1)S(1)}, u32[]{:S(2)}, u32[]{:S(2)}) collective-permute-start(bf16[192,1280]{1,0:T(8,128)(2,1)} %collective-permute-done.2.refs_1_), channel_id=1, source_target_pairs={{0,1},{1,2},{2,3},{3,0},{4,5},{5,6},{6,7},{7,4},{8,9},{9,10},{10,1... | collective-permute-start | bytes 1474568 | tf_op jit(solution)/shard_map/ppermute | solution.py:25
  86.3 24.7 %collective-permute-start.1 = (bf16[192,1280]{1,0:T(8,128)(2,1)}, bf16[192,1280]{1,0:T(8,128)(2,1)S(1)}, u32[]{:S(2)}, u32[]{:S(2)}) collective-permute-start(bf16[192,1280]{1,0:T(8,128)(2,1)} %copy-done.10), channel_id=1, source_target_pairs={{0,1},{1,2},{2,3},{3,0},{4,5},{5,6},{6,7},{7,4},{8,9},{9,10},{10,1... | collective-permute-start | bytes 1474568 | tf_op jit(solution)/shard_map/ppermute | solution.py:25
  86.4 27.8 %collective-permute-start.16 = (bf16[192,1280]{1,0:T(8,128)(2,1)}, bf16[192,1280]{1,0:T(8,128)(2,1)S(1)}, u32[]{:S(2)}, u32[]{:S(2)}) collective-permute-start(bf16[192,1280]{1,0:T(8,128)(2,1)} %collective-permute-done.15.refs_12_), channel_id=1, source_target_pairs={{0,12},{4,0},{8,4},{12,8},{1,13},{5,1},{9,5},{13,9},{2,14},{6,2},{... | collective-permute-start | bytes 1474568 | tf_op jit(solution)/shard_map/ppermute | solution.py:25
  94.9 19.6 %collective-permute-start.20 = (bf16[192,1280]{1,0:T(8,128)(2,1)S(1)}, bf16[192,1280]{1,0:T(8,128)(2,1)S(1)}, u32[]{:S(2)}, u32[]{:S(2)}) collective-permute-start(bf16[192,1280]{1,0:T(8,128)(2,1)S(1)} %copy-done.13), channel_id=1, source_target_pairs={{0,4},{4,8},{8,12},{12,0},{1,5},{5,9},{9,13},{13,1},{2,6},{6,10},{... | collective-permute-start | bytes 1474568 | tf_op jit(solution)/shard_map/ppermute | solution.py:25
  111.0 17.9 %collective-permute-start.23 = (bf16[192,1280]{1,0:T(8,128)(2,1)}, bf16[192,1280]{1,0:T(8,128)(2,1)}, u32[]{:S(2)}, u32[]{:S(2)}) collective-permute-start(bf16[192,1280]{1,0:T(8,128)(2,1)} %copy-done.14), channel_id=1, source_target_pairs={{0,12},{4,0},{8,4},{12,8},{1,13},{5,1},{9,5},{13,9},{2,14},{6,2},{... | collective-permute-start | bytes 1474568 | tf_op jit(solution)/shard_map/ppermute | solution.py:25
  114.3 22.2 %collective-permute-start.4 = (bf16[192,1280]{1,0:T(8,128)(2,1)}, bf16[192,1280]{1,0:T(8,128)(2,1)}, u32[]{:S(2)}, u32[]{:S(2)}) collective-permute-start(bf16[192,1280]{1,0:T(8,128)(2,1)} %collective-permute-done.3.refs_6_), channel_id=1, source_target_pairs={{0,3},{1,0},{2,1},{3,2},{4,7},{5,4},{6,5},{7,6},{8,11},{9,8},{10,9... | collective-permute-start | bytes 1474568 | tf_op jit(solution)/shard_map/ppermute | solution.py:25
  115.8 20.6 %collective-permute-start.7 = (bf16[192,1280]{1,0:T(8,128)(2,1)}, bf16[192,1280]{1,0:T(8,128)(2,1)S(1)}, u32[]{:S(2)}, u32[]{:S(2)}) collective-permute-start(bf16[192,1280]{1,0:T(8,128)(2,1)} %copy-done.19), channel_id=1, source_target_pairs={{0,1},{1,2},{2,3},{3,0},{4,5},{5,6},{6,7},{7,4},{8,9},{9,10},{10,1... | collective-permute-start | bytes 1474568 | tf_op jit(solution)/shard_map/ppermute | solution.py:25
  150.9 57.5 %collective-permute-start.33 = (f32[1280,640]{1,0:T(8,128)}, f32[1280,640]{1,0:T(8,128)}, u32[]{:S(2)}, u32[]{:S(2)}) collective-permute-start(f32[1280,640]{1,0:T(8,128)} %get-tuple-element.33), channel_id=1, source_target_pairs={{0,16},{16,0},{1,17},{17,1},{2,18},{18,2},{3,19},{19,3},{4,20},{20... | collective-permute-start | bytes 9830408 | tf_op jit(solution)/shard_map/ppermute | solution.py:25
  160.1 21.2 %collective-permute-start.35 = (f32[320,640]{1,0:T(8,128)}, f32[320,640]{1,0:T(8,128)S(1)}, u32[]{:S(2)}, u32[]{:S(2)}) collective-permute-start(f32[320,640]{1,0:T(8,128)} %get-tuple-element.39), channel_id=1, source_target_pairs={{0,32},{32,64},{64,96},{96,0},{1,33},{33,65},{65,97},{97,1},{2,34}... | collective-permute-start | bytes 2457608 | tf_op jit(solution)/shard_map/ppermute | solution.py:25
  161.3 38.5 %collective-permute-start.36 = (f32[320,640]{1,0:T(8,128)}, f32[320,640]{1,0:T(8,128)S(1)}, u32[]{:S(2)}, u32[]{:S(2)}) collective-permute-start(f32[320,640]{1,0:T(8,128)} %get-tuple-element.40), channel_id=1, source_target_pairs={{0,64},{32,96},{64,0},{96,32},{1,65},{33,97},{65,1},{97,33},{2,66}... | collective-permute-start | bytes 2457608 | tf_op jit(solution)/shard_map/ppermute | solution.py:25
  163.7 36.1 %collective-permute-start.37 = (f32[320,640]{1,0:T(8,128)}, f32[320,640]{1,0:T(8,128)S(1)}, u32[]{:S(2)}, u32[]{:S(2)}) collective-permute-start(f32[320,640]{1,0:T(8,128)} %get-tuple-element.41), channel_id=1, source_target_pairs={{0,96},{32,0},{64,32},{96,64},{1,97},{33,1},{65,33},{97,65},{2,98}... | collective-permute-start | bytes 2457608 | tf_op jit(solution)/shard_map/ppermute | solution.py:25
  201.1 43.0 %collective-permute-start.38 = (f32[320,640]{1,0:T(8,128)S(1)}, f32[320,640]{1,0:T(8,128)S(1)}, u32[]{:S(2)}, u32[]{:S(2)}) collective-permute-start(f32[320,640]{1,0:T(8,128)S(1)} %add_add_fusion), channel_id=1, source_target_pairs={{0,0},{1,32},{2,64},{3,96},{32,1},{33,33},{34,65},{35,97},{64,2},{... | collective-permute-start | bytes 2457608 | tf_op jit(solution)/shard_map/ppermute | solution.py:31
  202.0 42.0 %collective-permute-start.30 = (f32[32,320]{1,0:T(8,128)S(1)}, f32[32,320]{1,0:T(8,128)S(1)}, u32[]{:S(2)}, u32[]{:S(2)}) collective-permute-start(f32[32,320]{1,0:T(8,128)S(1)} %get-tuple-element.83), channel_id=1, source_target_pairs={{0,32},{32,64},{64,96},{96,0},{1,33},{33,65},{65,97},{97,1},{2,34}... | collective-permute-start | bytes 122888 | tf_op jit(solution)/shard_map/ppermute | solution.py:25
  204.1 40.0 %collective-permute-start.31 = (f32[32,320]{1,0:T(8,128)S(1)}, f32[32,320]{1,0:T(8,128)S(1)}, u32[]{:S(2)}, u32[]{:S(2)}) collective-permute-start(f32[32,320]{1,0:T(8,128)S(1)} %get-tuple-element.82), channel_id=1, source_target_pairs={{0,64},{32,96},{64,0},{96,32},{1,65},{33,97},{65,1},{97,33},{2,66}... | collective-permute-start | bytes 122888 | tf_op jit(solution)/shard_map/ppermute | solution.py:25
  208.4 35.7 %collective-permute-start.32 = (f32[32,320]{1,0:T(8,128)S(1)}, f32[32,320]{1,0:T(8,128)S(1)}, u32[]{:S(2)}, u32[]{:S(2)}) collective-permute-start(f32[32,320]{1,0:T(8,128)S(1)} %get-tuple-element.81), channel_id=1, source_target_pairs={{0,96},{32,0},{64,32},{96,64},{1,97},{33,1},{65,33},{97,65},{2,98}... | collective-permute-start | bytes 122888 | tf_op jit(solution)/shard_map/ppermute | solution.py:25
  213.3 48.3 %collective-permute-start.43 = (bf16[320,640]{1,0:T(8,128)(2,1)}, bf16[320,640]{1,0:T(8,128)(2,1)S(1)}, u32[]{:S(2)}, u32[]{:S(2)}) collective-permute-start(bf16[320,640]{1,0:T(8,128)(2,1)} %get-tuple-element.46), channel_id=1, source_target_pairs={{0,32},{32,64},{64,96},{96,0},{1,33},{33,65},{65,97},{97,1},{2,34}... | collective-permute-start | bytes 1228808 | tf_op jit(solution)/shard_map/ppermute | solution.py:25
  244.0 17.8 %collective-permute-start.45 = (bf16[320,640]{1,0:T(8,128)(2,1)}, bf16[320,640]{1,0:T(8,128)(2,1)S(1)}, u32[]{:S(2)}, u32[]{:S(2)}) collective-permute-start(bf16[320,640]{1,0:T(8,128)(2,1)} %get-tuple-element.48), channel_id=1, source_target_pairs={{0,96},{32,0},{64,32},{96,64},{1,97},{33,1},{65,33},{97,65},{2,98}... | collective-permute-start | bytes 1228808 | tf_op jit(solution)/shard_map/ppermute | solution.py:25
  305.3 52.4 %collective-permute-start.67 = (bf16[320,1280]{1,0:T(8,128)(2,1)}, bf16[320,1280]{1,0:T(8,128)(2,1)S(1)}, u32[]{:S(2)}, u32[]{:S(2)}) collective-permute-start(bf16[320,1280]{1,0:T(8,128)(2,1)} %get-tuple-element.69), channel_id=1, source_target_pairs={{0,1},{1,2},{2,3},{3,0},{4,5},{5,6},{6,7},{7,4},{8,9},{9,10},{10,1... | collective-permute-start | bytes 2457608 | tf_op jit(solution)/shard_map/ppermute | solution.py:25
  305.3 52.4 %collective-permute-start.68 = (bf16[320,1280]{1,0:T(8,128)(2,1)}, bf16[320,1280]{1,0:T(8,128)(2,1)S(1)}, u32[]{:S(2)}, u32[]{:S(2)}) collective-permute-start(bf16[320,1280]{1,0:T(8,128)(2,1)} %get-tuple-element.68), channel_id=1, source_target_pairs={{0,2},{1,3},{2,0},{3,1},{4,6},{5,7},{6,4},{7,5},{8,10},{9,11},{10,... | collective-permute-start | bytes 2457608 | tf_op jit(solution)/shard_map/ppermute | solution.py:25
  307.2 50.6 %collective-permute-start.69 = (bf16[320,1280]{1,0:T(8,128)(2,1)}, bf16[320,1280]{1,0:T(8,128)(2,1)S(1)}, u32[]{:S(2)}, u32[]{:S(2)}) collective-permute-start(bf16[320,1280]{1,0:T(8,128)(2,1)} %get-tuple-element.67), channel_id=1, source_target_pairs={{0,3},{1,0},{2,1},{3,2},{4,7},{5,4},{6,5},{7,6},{8,11},{9,8},{10,9... | collective-permute-start | bytes 2457608 | tf_op jit(solution)/shard_map/ppermute | solution.py:25
  309.6 32.7 %collective-permute-start.63 = (f32[32,640]{1,0:T(8,128)}, f32[32,640]{1,0:T(8,128)S(1)}, u32[]{:S(2)}, u32[]{:S(2)}) collective-permute-start(f32[32,640]{1,0:T(8,128)} %slice.9), channel_id=1, source_target_pairs={{0,1},{1,2},{2,3},{3,0},{4,5},{5,6},{6,7},{7,4},{8,9},{9,10},{10,1... | collective-permute-start | bytes 245768 | tf_op jit(solution)/shard_map/ppermute | solution.py:25
  315.7 29.1 %collective-permute-start.64 = (f32[32,640]{1,0:T(8,128)}, f32[32,640]{1,0:T(8,128)}, u32[]{:S(2)}, u32[]{:S(2)}) collective-permute-start(f32[32,640]{1,0:T(8,128)} %slice.9), channel_id=1, source_target_pairs={{0,2},{1,3},{2,0},{3,1},{4,6},{5,7},{6,4},{7,5},{8,10},{9,11},{10,... | collective-permute-start | bytes 245768 | tf_op jit(solution)/shard_map/ppermute | solution.py:25
  (64 other events, 843.9 us)
